TPU v7x, 512 devices: a whole 4x4x16 slice. The times are simulated.
512 devices in a mesh: row: 16 (over x_hi, y, core), col: 32 (over z, x_lo).
Axes of the slice: x: 4 (x_hi: 2, x_lo: 2; x = x_hi * 2 + x_lo), y: 4, z: 16, core: 2. Of those that a mesh axis runs over, the one named last changes fastest.
Arguments:
- phase: float32 [512, 32, 512], P('col', 'row'), may hold values from -6 to 6
- velocity: float32 [3, 512, 32, 512], P(None, 'col', 'row'), may hold values from -12 to 12
Outputs:
- phase_next: float32 [512, 32, 512], P('col', 'row')
- velocity_next: float32 [3, 512, 32, 512], P(None, 'col', 'row')
All inputs are finite; a program needn't handle non-finite values.
Results may differ from a plain program's by a relative error of at most 0.013.
Values may be sent and summed in bfloat16 or wider, within the bound.
No kernel may reach another device: no remote copies, remote signals or barrier semaphores. Data moves between devices by JAX's collectives and lax.ppermute only.
A program may use at most 64 MiB of HBM per device.

v0:
```python
import numpy as np

import jax
import jax.numpy as jnp
from jax import lax
from jax.experimental import pallas as pl
from jax.experimental.pallas import tpu as pltpu
from jax.sharding import PartitionSpec as P

NX = 512
NY = 512
NZ = 32
KC = 192
KZ = 24
COLS = 32
ROWS = 16
AS = KC // COLS
LO = 32 // ROWS
YL = NY // COLS
QS = 12
QP = 16
BATCH = AS * LO
MODES = KZ * BATCH
LINES = COLS * AS * 2

time_step = 0.001
epsilon = 0.01
mobility = 1.0
reynolds = 100.0
stabilizer = 2.0


def roots(numerator, period):
    angle = (numerator % period) * (2.0 * np.pi / period)
    return np.cos(angle), np.sin(angle)


def as_bf16(values):
    return jnp.asarray(np.asarray(values, np.float32)).astype(jnp.bfloat16)


def x_forward_table():
    c, s = roots(np.arange(KC)[:, None] * np.arange(NX)[None, :], NX)
    return np.stack([c, -s], axis=1).reshape(LINES, NX)


def x_inverse_table():
    c, s = roots(np.arange(KC)[:, None] * np.arange(NX)[None, :], NX)
    w = np.where(np.arange(KC) == 0, 1.0, 2.0)[:, None]
    return np.stack([w * c, -w * s], axis=1).reshape(LINES, NX)


def complex_rotation(c, s):
    return np.array([[c, -s], [s, c]])


def left_y_table(zr, direction):
    k32 = np.arange(32)
    c, s = roots(k32[:, None] * np.arange(COLS)[None, :], 32)
    same = np.einsum("ab,zy->abzy", np.eye(AS), np.eye(zr))
    rot = complex_rotation(c, direction * s).reshape(2, 2, ROWS, LO, COLS)
    n = 2 * 32 * AS * zr
    if direction < 0:
        return np.einsum("pqrlc,abzy->pralzcbqy", rot, same).reshape(n, n)
    return np.einsum("pqrlc,abzy->capzqrbly", rot, same).reshape(n, n)


def twiddles(zr):
    k32 = np.arange(32).reshape(ROWS, 1, LO, 1, 1)
    yl = lane_yl(zr).reshape(1, 1, 1, 1, 128)
    c, s = roots(np.broadcast_to(k32 * yl, (ROWS, AS, LO, zr, 128)), 512)
    return c.reshape(-1, 128), s.reshape(-1, 128)


def lane_yl(zr):
    if zr == 1:
        return np.broadcast_to(np.arange(YL)[None, :, None], (4, YL, 2)).reshape(-1)
    return np.broadcast_to(np.arange(YL)[None, :], (8, YL)).reshape(-1)


def right_y_table(zr, direction):
    q = np.arange(QS) - QS // 2
    c, s = np.zeros((2, QP, YL))
    c[:QS], s[:QS] = roots(q[:, None] * np.arange(YL)[None, :], 16)
    rot = complex_rotation(c, direction * s)
    eye = np.eye
    if zr == 1:
        if direction < 0:
            out = np.einsum("pkqy,fg,zw->kfyzpwgq", rot, eye(4), eye(2))
        else:
            out = np.einsum("pkqy,fg,zw->kzfqpgyw", rot, eye(4), eye(2))
    elif direction < 0:
        out = np.einsum("pkqy,fg->kfypgq", rot, eye(8))
    else:
        out = np.einsum("pkqy,fg->kfqpgy", rot, eye(8))
    return out.reshape(256, 256)


def left_z_table(direction, z_major):
    q = np.arange(KZ) - KZ // 2
    c, s = roots(q[:, None] * np.arange(NZ)[None, :], NZ)
    rot = complex_rotation(c, direction * s).reshape(2, 2, KZ, ROWS, 2)
    same = np.eye(BATCH)
    if direction < 0:
        form = "pkmsz,ab->pmazsbk" if z_major else "pkmsz,ab->pmasbzk"
        out = np.einsum(form, rot, same).reshape(2 * MODES, -1)
        return out / (NX * NY * NZ)
    form = "pkmsz,ab->zsapkmb" if z_major else "pkmsz,ab->sazpkmb"
    return np.einsum(form, rot, same).reshape(-1, 2 * MODES)


def spread_table():
    low = [0, 0, 0, 0]
    high = [3, 1, 2, None]
    plain = [0, 1, 2, 3]
    other = [2, 3, 1, None]
    out = np.zeros((2, 4, QP, 2, 16, QP))
    for slot, f in enumerate(low + high + plain + other):
        if f is not None:
            for z in range(2):
                out[z, f, :, z, slot, :] = np.eye(QP)
    return out.reshape(128, 512)


def wave_table():
    a = np.arange(AS).reshape(1, AS, 1, 1, 1)
    lo = np.arange(LO).reshape(1, 1, LO, 1, 1)
    m = np.arange(KZ).reshape(KZ, 1, 1, 1, 1)
    q = np.arange(QP).reshape(1, 1, 1, 1, QP)
    full = (KZ, AS, LO, 8, QP)
    return np.stack(
        [
            np.broadcast_to(a, full),
            np.broadcast_to(32 * (q - QS // 2) + lo, full),
            np.broadcast_to((m - KZ // 2) * (NX // NZ), full),
        ]
    ).reshape(3 * MODES, 128)


def dot(lhs, rhs):
    return lax.dot_general(
        lhs, rhs, (((1,), (0,)), ((), ())), preferred_element_type=jnp.float32
    )


def dot_nt(lhs, rhs):
    return lax.dot_general(
        lhs, rhs, (((1,), (1,)), ((), ())), preferred_element_type=jnp.float32
    )


def to_bf16(values):
    return values.astype(jnp.bfloat16)


def flat_rows(ref, *lead):
    return ref[lead].reshape(2 * YL, NX) if lead else ref[...].reshape(2 * YL, NX)


def x_forward_kernel(phase_ref, vel_ref, table_ref, out_ref):
    x = jnp.concatenate(
        [flat_rows(phase_ref)] + [flat_rows(vel_ref, j) for j in range(3)], axis=0
    )
    out_ref[...] = to_bf16(dot_nt(table_ref[...], to_bf16(x)))


def y_forward_kernel(in_ref, left_ref, cos_ref, sin_ref, right_ref, out_ref, wide):
    half = in_ref.shape[0] // 2
    sums = dot(left_ref[...], in_ref[...])
    re, im = sums[:half], sums[half:]
    c, s = cos_ref[...], sin_ref[...]
    lines = jnp.concatenate([to_bf16(re * c + im * s), to_bf16(im * c - re * s)], axis=1)
    modes = dot(lines, right_ref[...])
    for p in range(2):
        wide[pl.ds(p, half, stride=2), :] = modes[:, 128 * p : 128 * (p + 1)]
    out_ref[...] = to_bf16(wide[...])


def y_inverse_kernel(in_ref, left_ref, cos_ref, sin_ref, right_ref, out_ref, wide):
    half = in_ref.shape[0] // 2
    wide[...] = in_ref[...].astype(jnp.float32)
    modes = jnp.concatenate(
        [to_bf16(wide[pl.ds(p, half, stride=2), :]) for p in range(2)], axis=1
    )
    lines = dot(modes, right_ref[...])
    re, im = lines[:, :128], lines[:, 128:]
    c, s = cos_ref[...], sin_ref[...]
    spun = jnp.concatenate([to_bf16(re * c - im * s), to_bf16(re * s + im * c)], axis=0)
    out_ref[...] = to_bf16(dot(left_ref[...], spun))


def wave_numbers(where_ref, wave_ref):
    kx = wave_ref[0:MODES] + where_ref[0].astype(jnp.float32)
    ky = wave_ref[MODES : 2 * MODES] + where_ref[1].astype(jnp.float32)
    kz = wave_ref[2 * MODES : 3 * MODES]
    slot = lax.broadcasted_iota(jnp.int32, (MODES, 128), 1) // QP
    return kx, ky, kz, kx * kx + ky * ky + kz * kz, slot


def derive_kernel(
    where_ref, in_ref, spread_ref, left_ref, wave_ref, back_ref, out_ref, spectra_ref
):
    spread = to_bf16(dot(in_ref[...], spread_ref[...]))
    modes = dot(left_ref[...], jnp.concatenate([spread[:, :256], spread[:, 256:]], axis=0))
    spectra_ref[...] = modes[:, 128:]
    kx, ky, kz, k2, slot = wave_numbers(where_ref, wave_ref)
    one = jnp.where(
        (slot == 0) | (slot == 6),
        kx,
        jnp.where(
            (slot == 1) | (slot == 4),
            ky,
            jnp.where((slot == 2) | (slot == 5), kz, jnp.where(slot == 3, -k2, 0.0)),
        ),
    )
    two = jnp.where(
        slot == 4, kz, jnp.where(slot == 5, kx, jnp.where(slot == 6, ky, 0.0))
    )
    re = modes[:MODES, :128] * one - modes[:MODES, 128:] * two
    im = modes[MODES:, :128] * one - modes[MODES:, 128:] * two
    plain = slot == 3
    coeff = jnp.concatenate(
        [to_bf16(jnp.where(plain, re, -im)), to_bf16(jnp.where(plain, im, re))], axis=0
    )
    out_ref[...] = to_bf16(dot(back_ref[...], coeff))


def solve_kernel(where_ref, in_ref, spectra_ref, left_ref, wave_ref, back_ref, out_ref):
    modes = dot(left_ref[...], in_ref[...])
    kx, ky, kz, k2, slot = wave_numbers(where_ref, wave_ref)
    scalar = slot == 0
    stable = 1.0 / time_step + mobility * stabilizer * k2
    below = jnp.where(
        scalar,
        stable + mobility * epsilon * epsilon * k2 * k2,
        1.0 / time_step + k2 / reynolds,
    )
    used = slot < 4
    inv = jnp.where(used, 1.0 / below, 0.0)
    keep = jnp.where(scalar, stable, 1.0 / time_step)
    mean = scalar & (k2 == 0.0)
    sign = jnp.where(mean, 0.0, jnp.where(scalar, -1.0, 1.0))
    bulk = jnp.where(scalar, mobility * k2, 0.0)
    wave = jnp.where(
        slot == 1, kx, jnp.where(slot == 2, ky, jnp.where(slot == 3, kz, 0.0))
    )
    shared = wave / jnp.maximum(k2, 1.0)
    parts = []
    for p in range(2):
        now = modes[p * MODES : (p + 1) * MODES]
        old = spectra_ref[p * MODES : (p + 1) * MODES]
        fresh = (keep * old + sign * now - bulk * pltpu.roll(now, 64, 1)) * inv
        normal = wave * fresh
        for step in (16, 32, 64):
            normal = normal + pltpu.roll(normal, step, 1)
        parts.append(to_bf16(fresh - shared * normal))
    both = dot(back_ref[...], jnp.concatenate(parts, axis=0))
    half = both.shape[0] // 2
    out_ref[...] = to_bf16(both[:half] + pltpu.roll(both[half:], 64, 1))


def nonlinear_kernel(in_ref, phase_ref, vel_ref, back_ref, table_ref, out_ref, wide):
    wide[...] = in_ref[...].astype(jnp.float32)
    for z in range(2):
        lines = to_bf16(wide[pl.ds(z, LINES, stride=2), :].T)
        values = dot(lines, back_ref[...])
        d = [values[YL * f : YL * (f + 1)] for f in range(7)]
        phase = phase_ref[:, z, :]
        v = [vel_ref[j, :, z, :] for j in range(3)]
        g, lap, w = d[0:3], d[3], d[4:7]
        advect = v[0] * g[0] + v[1] * g[1] + v[2] * g[2]
        bulk = phase * phase * phase - phase
        potential = bulk - epsilon * epsilon * lap
        terms = [
            advect,
            v[1] * w[2] - v[2] * w[1] + potential * g[0],
            v[2] * w[0] - v[0] * w[2] + potential * g[1],
            v[0] * w[1] - v[1] * w[0] + potential * g[2],
            bulk,
            jnp.zeros((3 * YL, NX), jnp.float32),
        ]
        x = jnp.concatenate([to_bf16(t) for t in terms], axis=0)
        wide[pl.ds(z, LINES, stride=2), :] = dot_nt(table_ref[...], x)
    out_ref[...] = to_bf16(wide[...])


def x_inverse_kernel(in_ref, back_ref, phase_ref, vel_ref):
    lines = to_bf16(in_ref[...].astype(jnp.float32).T)
    values = dot(lines, back_ref[...])
    phase_ref[...] = values[0:32].reshape(YL, 2, NX)
    for j in range(3):
        vel_ref[j] = values[32 * (j + 1) : 32 * (j + 2)].reshape(YL, 2, NX)


def call(kernel, outs, scratch, *args, scalars=0):
    vmem = pl.BlockSpec(memory_space=pltpu.VMEM)
    specs = [pl.BlockSpec(memory_space=pltpu.SMEM)] * scalars + [vmem] * (
        len(args) - scalars
    )
    return pl.pallas_call(
        kernel,
        in_specs=specs,
        out_specs=[vmem] * len(outs),
        out_shape=outs,
        scratch_shapes=scratch,
        compiler_params=pltpu.CompilerParams(vmem_limit_bytes=16 * 1024 * 1024),
    )(*args)


def buffer(rows, dtype=jnp.bfloat16):
    return jax.ShapeDtypeStruct((rows, 128), dtype)


def exchange(values, axis):
    rows = values.shape[0]
    swapped = lax.all_to_all(
        values.reshape(rows // 2, 2, 128), axis, split_axis=0, concat_axis=0, tiled=True
    )
    return swapped.reshape(rows, 128)


def on_device(phase, velocity):
    f32 = jnp.float32
    x_table = as_bf16(x_forward_table())
    x_back = as_bf16(x_inverse_table())
    waves = jnp.asarray(wave_table(), f32)
    where = jnp.stack(
        [lax.axis_index("col") * AS, lax.axis_index("row") * LO]
    ).astype(jnp.int32)

    def y_tables(zr, direction):
        cos_t, sin_t = twiddles(zr)
        return (
            as_bf16(left_y_table(zr, direction)),
            jnp.asarray(cos_t, f32),
            jnp.asarray(sin_t, f32),
            as_bf16(right_y_table(zr, direction)),
        )

    def y_step(kernel, lines, zr, direction):
        rows = LINES * zr
        return call(
            kernel, [buffer(rows)], [pltpu.VMEM((rows, 128), f32)],
            lines, *y_tables(zr, direction),
        )[0]

    lines = call(x_forward_kernel, [buffer(LINES)], [], phase, velocity, x_table)[0]
    planes = y_step(y_forward_kernel, exchange(lines, "col"), 1, -1)
    planes, spectra = call(
        derive_kernel, [buffer(2 * LINES), buffer(2 * MODES, f32)], [],
        where, exchange(planes, "row"), as_bf16(spread_table()),
        as_bf16(left_z_table(-1, True)), waves, as_bf16(left_z_table(1, False)), scalars=1,
    )
    lines = y_step(y_inverse_kernel, exchange(planes, "row"), 2, 1)
    lines = call(
        nonlinear_kernel, [buffer(2 * LINES)], [pltpu.VMEM((2 * LINES, 128), f32)],
        exchange(lines, "col"), phase, velocity, x_back, x_table,
    )[0]
    planes = y_step(y_forward_kernel, exchange(lines, "col"), 2, -1)
    planes = call(
        solve_kernel, [buffer(LINES)], [],
        where, exchange(planes, "row"), spectra, as_bf16(left_z_table(-1, False)), waves,
        as_bf16(left_z_table(1, True)), scalars=1,
    )[0]
    lines = y_step(y_inverse_kernel, exchange(planes, "row"), 1, 1)
    return tuple(
        call(
            x_inverse_kernel,
            [
                jax.ShapeDtypeStruct(phase.shape, f32),
                jax.ShapeDtypeStruct(velocity.shape, f32),
            ],
            [], exchange(lines, "col"), x_back,
        )
    )


def solution(mesh):
    in_specs = (P("col", "row", None), P(None, "col", "row", None))
    out_specs = (P("col", "row", None), P(None, "col", "row", None))
    return jax.shard_map(
        on_device, mesh=mesh, in_specs=in_specs, out_specs=out_specs, check_vma=False
    )
```

profile of v0, /device:TPU:2, one launch (start us, length us, event | category | flops | bytes accessed | tf_op | source)
XLA Modules:
  0.0 161.0 jit_solution(13414950165330985671)
XLA Ops:
  0.6 0.0 copy-start
  0.6 0.0 copy-start.1
  0.7 1.0 copy-done.1
  1.7 0.0 copy-start.12
  1.7 0.9 copy-done.12
  2.6 0.0 copy-start.20
  2.6 0.8 copy-done.20
  3.5 0.0 copy-start.7
  3.5 0.9 shard_map.257
  4.4 16.7 %all-to-all-start = ((bf16[192,2,128]{2,1,0:T(2,128)(2,1)}), bf16[192,2,128]{2,1,0:T(2,128)(2,1)S(1)}, u32[]{:S(2)}, u32[]{:S(2)}) async-start(bf16[192,2,128]{2,1,0:T(2,128)(2,1)} %bitcast.2), calls=%async_computation | async-start | bytes 196608 | tf_op jit(solution)/shard_map/all_to_all | solution.py:316
  21.1 14.6 %all-to-all-done = bf16[192,2,128]{2,1,0:T(2,128)(2,1)S(1)} async-done(((bf16[192,2,128]{2,1,0:T(2,128)(2,1)}), bf16[192,2,128]{2,1,0:T(2,128)(2,1)S(1)}, u32[]{:S(2)}, u32[]{:S(2)}) %all-to-all-start) | async-done | bytes 98336 | tf_op jit(solution)/shard_map/all_to_all | solution.py:316
  35.7 0.0 copy-start.14
  35.7 0.9 copy-done.14
  36.6 0.0 copy-start.16
  36.6 0.9 copy-done.16
  37.5 0.0 copy-start.19
  37.5 1.0 copy-done.19
  38.4 0.0 copy-start.26
  38.4 0.9 copy-done.26
  39.3 1.0 shard_map.258
  40.4 6.1 %all-to-all-start.1 = ((bf16[192,2,128]{2,1,0:T(2,128)(2,1)}), bf16[192,2,128]{2,1,0:T(2,128)(2,1)S(1)}, u32[]{:S(2)}, u32[]{:S(2)}) async-start(bf16[192,2,128]{2,1,0:T(2,128)(2,1)} %bitcast.4), calls=%async_computation.1 | async-start | bytes 196608 | tf_op jit(solution)/shard_map/all_to_all | solution.py:316
  46.5 0.1 pad_add_fusion.where_ref
  46.6 7.7 %all-to-all-done.1 = bf16[192,2,128]{2,1,0:T(2,128)(2,1)S(1)} async-done(((bf16[192,2,128]{2,1,0:T(2,128)(2,1)}), bf16[192,2,128]{2,1,0:T(2,128)(2,1)S(1)}, u32[]{:S(2)}, u32[]{:S(2)}) %all-to-all-start.1) | async-done | bytes 98336 | tf_op jit(solution)/shard_map/all_to_all | solution.py:316
  54.3 0.0 copy-done
  54.3 0.0 copy-done.7
  54.3 1.2 copy-done.9
  55.5 0.9 copy-done.25
  56.4 1.9 %shard_map.259 = (bf16[768,128]{1,0:T(8,128)(2,1)S(1)}, f32[576,128]{1,0:T(8,128)S(1)}) custom-call(s32[2]{0:T(128)S(1)} %pad_add_fusion.where_ref, bf16[384,128]{1,0:T(8,128)(2,1)S(1)} %bitcast.25, bf16[128,512]{1,0:T(8,128)(2,1)S(1)} %copy-done.25, bf16[576,768]{1,0:T(8,128)(2,1)S(1)} %copy-done.9, f32[864,128]{1,0:T(8,128)S(1)} %copy-done, ...), custom_call_target="tpu_custom_call" | custom-call | tf_op jit(solution)/shard_map/pallas_call | solution.py:300
  58.3 11.4 %all_to_all.40 = bf16[384,2,128]{2,1,0:T(2,128)(2,1)S(1)} all-to-all(bf16[384,2,128]{2,1,0:T(2,128)(2,1)S(1)} %bitcast.31), channel_id=1, replica_groups=mesh['row'=16,'col'=32] {'row'}, dimensions={0} | all-to-all | bytes 393216 | tf_op jit(solution)/shard_map/all_to_all | solution.py:316
  69.8 0.0 copy-done.5
  69.8 0.0 copy-done.10
  69.8 0.0 copy-done.11
  69.8 0.0 copy-done.24
  69.8 0.0 copy-start.2
  69.8 0.0 copy-start.3
  69.8 0.0 copy-start.13
  69.8 0.0 copy-start.21
  69.9 0.7 shard_map.260
  70.6 0.0 copy-start.4
  70.6 0.0 copy-start.23
  70.6 23.0 %all_to_all.41 = bf16[384,2,128]{2,1,0:T(2,128)(2,1)S(1)} all-to-all(bf16[384,2,128]{2,1,0:T(2,128)(2,1)S(1)} %bitcast.22), channel_id=1, replica_groups=mesh['row'=16,'col'=32] {'col'}, dimensions={0} | all-to-all | bytes 393216 | tf_op jit(solution)/shard_map/all_to_all | solution.py:316
  93.6 0.0 copy-done.2
  93.6 0.0 copy-done.3
  93.6 0.0 copy-done.13
  93.7 0.0 copy-done.21
  93.7 0.7 shard_map.261
  94.4 21.6 %all_to_all.42 = bf16[384,2,128]{2,1,0:T(2,128)(2,1)S(1)} all-to-all(bf16[384,2,128]{2,1,0:T(2,128)(2,1)S(1)} %bitcast.24), channel_id=1, replica_groups=mesh['row'=16,'col'=32] {'col'}, dimensions={0} | all-to-all | bytes 393216 | tf_op jit(solution)/shard_map/all_to_all | solution.py:316
  116.0 0.0 copy-done.4
  116.0 0.0 copy-done.23
  116.0 0.7 shard_map.262
  116.7 12.0 %all_to_all.43 = bf16[384,2,128]{2,1,0:T(2,128)(2,1)S(1)} all-to-all(bf16[384,2,128]{2,1,0:T(2,128)(2,1)S(1)} %bitcast.20), channel_id=1, replica_groups=mesh['row'=16,'col'=32] {'row'}, dimensions={0} | all-to-all | bytes 393216 | tf_op jit(solution)/shard_map/all_to_all | solution.py:316
  128.7 0.0 copy-done.6
  128.7 0.0 copy-done.8
  128.7 0.0 copy-start.18
  128.8 0.0 copy-start.22
  128.8 2.1 %shard_map.263 = bf16[384,128]{1,0:T(8,128)(2,1)S(1)} custom-call(s32[2]{0:T(128)S(1)} %pad_add_fusion.where_ref, bf16[768,128]{1,0:T(8,128)(2,1)S(1)} %bitcast.18, f32[576,128]{1,0:T(8,128)S(1)} %get-tuple-element.5.spectra_ref, bf16[576,768]{1,0:T(8,128)(2,1)S(1)} %copy-done.8, f32[864,128]{1,0:T(8,128)S(1)} %copy-done, bf16[768,576]{1,0:T(8,128)(2,1)S(1)} %copy-done.6), custom_call_target="tpu_custom_call" | custom-call | tf_op jit(solution)/shard_map/pallas_call | solution.py:300
  130.9 10.4 %all_to_all.44 = bf16[192,2,128]{2,1,0:T(2,128)(2,1)S(1)} all-to-all(bf16[192,2,128]{2,1,0:T(2,128)(2,1)S(1)} %bitcast.26), channel_id=1, replica_groups=mesh['row'=16,'col'=32] {'row'}, dimensions={0} | all-to-all | bytes 196608 | tf_op jit(solution)/shard_map/all_to_all | solution.py:316
  141.3 0.0 copy-done.15
  141.3 0.0 copy-done.17
  141.3 0.0 copy-done.18
  141.3 0.0 copy-done.22
  141.3 0.4 shard_map.264
  141.8 18.2 %all_to_all.45 = bf16[192,2,128]{2,1,0:T(2,128)(2,1)S(1)} all-to-all(bf16[192,2,128]{2,1,0:T(2,128)(2,1)S(1)} %bitcast.29), channel_id=1, replica_groups=mesh['row'=16,'col'=32] {'col'}, dimensions={0} | all-to-all | bytes 196608 | tf_op jit(solution)/shard_map/all_to_all | solution.py:316
  160.0 1.0 shard_map.265
  (10 shorter events, 0.0 us)
Async XLA Ops:
  0.6 53.7 %copy-start = (f32[864,128]{1,0:T(8,128)S(1)}, f32[864,128]{1,0:T(8,128)}, u32[]{:S(2)}) copy-start(f32[864,128]{1,0:T(8,128)} %constant.55.clone.wave_ref) | copy-start | bytes 1327108
  0.6 1.1 copy-start.1
  1.7 0.9 copy-start.12
  2.6 0.8 copy-start.20
  3.5 50.9 %copy-start.7 = (bf16[768,576]{1,0:T(8,128)(2,1)S(1)}, bf16[768,576]{1,0:T(8,128)(2,1)}, u32[]{:S(2)}) copy-start(bf16[768,576]{1,0:T(8,128)(2,1)} %constant.80.back_ref) | copy-start | bytes 2654212
  4.4 31.3 %all-to-all-start = ((bf16[192,2,128]{2,1,0:T(2,128)(2,1)}), bf16[192,2,128]{2,1,0:T(2,128)(2,1)S(1)}, u32[]{:S(2)}, u32[]{:S(2)}) async-start(bf16[192,2,128]{2,1,0:T(2,128)(2,1)} %bitcast.2), calls=%async_computation | async-start | bytes 196608 | tf_op jit(solution)/shard_map/all_to_all | solution.py:316
  35.7 0.9 copy-start.14
  36.6 0.9 copy-start.16
  37.5 1.0 copy-start.19
  38.4 0.9 copy-start.26
  40.4 14.0 %all-to-all-start.1 = ((bf16[192,2,128]{2,1,0:T(2,128)(2,1)}), bf16[192,2,128]{2,1,0:T(2,128)(2,1)S(1)}, u32[]{:S(2)}, u32[]{:S(2)}) async-start(bf16[192,2,128]{2,1,0:T(2,128)(2,1)} %bitcast.4), calls=%async_computation.1 | async-start | bytes 196608 | tf_op jit(solution)/shard_map/all_to_all | solution.py:316
  54.3 1.2 copy-start.9
  55.5 0.9 copy-start.25
  56.4 13.4 %copy-start.5 = (bf16[768,768]{1,0:T(8,128)(2,1)S(1)}, bf16[768,768]{1,0:T(8,128)(2,1)}, u32[]{:S(2)}) copy-start(bf16[768,768]{1,0:T(8,128)(2,1)} %constant.81.left_ref) | copy-start | bytes 3538948
  56.4 13.4 %copy-start.10 = (f32[384,128]{1,0:T(8,128)S(1)}, f32[384,128]{1,0:T(8,128)}, u32[]{:S(2)}) copy-start(f32[384,128]{1,0:T(8,128)} %constant.65.clone.sin_ref) | copy-start | bytes 589828
  56.4 13.4 %copy-start.11 = (f32[384,128]{1,0:T(8,128)S(1)}, f32[384,128]{1,0:T(8,128)}, u32[]{:S(2)}) copy-start(f32[384,128]{1,0:T(8,128)} %constant.64.clone.cos_ref) | copy-start | bytes 589828
  56.4 13.4 %copy-start.24 = (bf16[256,256]{1,0:T(8,128)(2,1)S(1)}, bf16[256,256]{1,0:T(8,128)(2,1)}, u32[]{:S(2)}) copy-start(bf16[256,256]{1,0:T(8,128)(2,1)} %constant.82.right_ref) | copy-start | bytes 393220
  69.8 23.8 %copy-start.2 = (bf16[384,512]{1,0:T(8,128)(2,1)S(1)}, bf16[384,512]{1,0:T(8,128)(2,1)}, u32[]{:S(2)}) copy-start(bf16[384,512]{1,0:T(8,128)(2,1)} %constant.75.table_ref) | copy-start | bytes 1179652
  69.8 23.8 %copy-start.3 = (bf16[384,512]{1,0:T(8,128)(2,1)S(1)}, bf16[384,512]{1,0:T(8,128)(2,1)}, u32[]{:S(2)}) copy-start(bf16[384,512]{1,0:T(8,128)(2,1)} %constant.83.back_ref) | copy-start | bytes 1179652
  69.8 23.8 %copy-start.13 = (f32[3,16,2,512]{3,2,1,0:T(2,128)S(1)}, f32[3,16,2,512]{3,2,1,0:T(2,128)}, u32[]{:S(2)}) copy-start(f32[3,16,2,512]{3,2,1,0:T(2,128)} %vel_ref.3) | copy-start | bytes 589828
  69.8 23.8 %copy-start.21 = (f32[16,2,512]{2,1,0:T(2,128)S(1)}, f32[16,2,512]{2,1,0:T(2,128)}, u32[]{:S(2)}) copy-start(f32[16,2,512]{2,1,0:T(2,128)} %phase_ref.3) | copy-start | bytes 196612
  70.6 45.4 %copy-start.4 = (bf16[768,768]{1,0:T(8,128)(2,1)S(1)}, bf16[768,768]{1,0:T(8,128)(2,1)}, u32[]{:S(2)}) copy-start(bf16[768,768]{1,0:T(8,128)(2,1)} %constant.84.left_ref) | copy-start | bytes 3538948
  70.6 45.4 %copy-start.23 = (bf16[256,256]{1,0:T(8,128)(2,1)S(1)}, bf16[256,256]{1,0:T(8,128)(2,1)}, u32[]{:S(2)}) copy-start(bf16[256,256]{1,0:T(8,128)(2,1)} %constant.85.right_ref) | copy-start | bytes 393220
  116.0 12.7 %copy-start.6 = (bf16[768,576]{1,0:T(8,128)(2,1)S(1)}, bf16[768,576]{1,0:T(8,128)(2,1)}, u32[]{:S(2)}) copy-start(bf16[768,576]{1,0:T(8,128)(2,1)} %constant.87.back_ref) | copy-start | bytes 2654212
  116.0 12.7 %copy-start.8 = (bf16[576,768]{1,0:T(8,128)(2,1)S(1)}, bf16[576,768]{1,0:T(8,128)(2,1)}, u32[]{:S(2)}) copy-start(bf16[576,768]{1,0:T(8,128)(2,1)} %constant.86.left_ref) | copy-start | bytes 2654212
  128.7 12.6 %copy-start.15 = (f32[192,128]{1,0:T(8,128)S(1)}, f32[192,128]{1,0:T(8,128)}, u32[]{:S(2)}) copy-start(f32[192,128]{1,0:T(8,128)} %constant.58.clone.sin_ref) | copy-start | bytes 294916
  128.7 12.6 %copy-start.17 = (f32[192,128]{1,0:T(8,128)S(1)}, f32[192,128]{1,0:T(8,128)}, u32[]{:S(2)}) copy-start(f32[192,128]{1,0:T(8,128)} %constant.57.clone.cos_ref) | copy-start | bytes 294916
  128.7 12.6 %copy-start.18 = (bf16[384,384]{1,0:T(8,128)(2,1)S(1)}, bf16[384,384]{1,0:T(8,128)(2,1)}, u32[]{:S(2)}) copy-start(bf16[384,384]{1,0:T(8,128)(2,1)} %constant.88.left_ref) | copy-start | bytes 884740
  128.8 12.5 %copy-start.22 = (bf16[256,256]{1,0:T(8,128)(2,1)S(1)}, bf16[256,256]{1,0:T(8,128)(2,1)}, u32[]{:S(2)}) copy-start(bf16[256,256]{1,0:T(8,128)(2,1)} %constant.89.right_ref) | copy-start | bytes 393220
where the time goes:
time: 162 us; the launch traced here: 161 us
  blocking collectives  96.7 us (60%)
  starting transfers between devices  22.9 us (14%)
  waiting for transfers between devices  22.3 us (14%)
  Pallas kernels  9.56 us (6%)
  local copies, waits for them, and re-layouts  8.62 us (5%)
    all_to_all x6, blocking collectives, exchange(): lax.all_to_all(values.reshape(rows // 2, 2, 128), axis, split_axis=0, con...  96.7 us
    all_to_all x2, starting transfers between devices, exchange(): lax.all_to_all(values.reshape(rows // 2, 2, 128), axis, split_axis=0, con...  22.9 us
    all_to_all x2, waiting for transfers between devices, exchange(): lax.all_to_all(values.reshape(rows // 2, 2, 128), axis, split_axis=0, con...  22.3 us
    pallas_call x9, Pallas kernels, call(): pl.pallas_call(kernel, in_specs=specs, out_specs=[vmem] * len(outs), out_...  9.56 us
    unnamed x54, local copies, waits for them, and re-layouts  8.62 us
  transfers between devices with their start and end apart: 2, of which 2 were waited for; matrix products, arithmetic and copies ran while one was open for 0% of the time, Pallas kernels for 0%

commit v1 on v0

--- a/solution.py
+++ b/solution.py
@@ -22,6 +22,7 @@
 BATCH = AS * LO
 MODES = KZ * BATCH
 LINES = COLS * AS * 2
+COST = 10_000_000_000
 
 time_step = 0.001
 epsilon = 0.01
@@ -157,7 +158,19 @@
     return ref[lead].reshape(2 * YL, NX) if lead else ref[...].reshape(2 * YL, NX)
 
 
-def x_forward_kernel(phase_ref, vel_ref, table_ref, out_ref):
+def x_forward_kernel(
+    phase_hbm, vel_hbm, table_hbm, out_ref, phase_ref, vel_ref, table_ref, sems
+):
+    copies = [
+        pltpu.make_async_copy(src, dst, sems.at[i])
+        for i, (src, dst) in enumerate(
+            [(phase_hbm, phase_ref), (vel_hbm, vel_ref), (table_hbm, table_ref)]
+        )
+    ]
+    for c in copies:
+        c.start()
+    for c in copies:
+        c.wait()
     x = jnp.concatenate(
         [flat_rows(phase_ref)] + [flat_rows(vel_ref, j) for j in range(3)], axis=0
     )
@@ -189,21 +202,21 @@
     out_ref[...] = to_bf16(dot(left_ref[...], spun))
 
 
-def wave_numbers(where_ref, wave_ref):
-    kx = wave_ref[0:MODES] + where_ref[0].astype(jnp.float32)
-    ky = wave_ref[MODES : 2 * MODES] + where_ref[1].astype(jnp.float32)
+def wave_numbers(wave_ref):
+    kx = wave_ref[0:MODES] + (lax.axis_index("col") * AS).astype(jnp.float32)
+    ky = wave_ref[MODES : 2 * MODES] + (lax.axis_index("row") * LO).astype(jnp.float32)
     kz = wave_ref[2 * MODES : 3 * MODES]
     slot = lax.broadcasted_iota(jnp.int32, (MODES, 128), 1) // QP
     return kx, ky, kz, kx * kx + ky * ky + kz * kz, slot
 
 
 def derive_kernel(
-    where_ref, in_ref, spread_ref, left_ref, wave_ref, back_ref, out_ref, spectra_ref
+    in_ref, spread_ref, left_ref, wave_ref, back_ref, out_ref, spectra_ref
 ):
     spread = to_bf16(dot(in_ref[...], spread_ref[...]))
     modes = dot(left_ref[...], jnp.concatenate([spread[:, :256], spread[:, 256:]], axis=0))
     spectra_ref[...] = modes[:, 128:]
-    kx, ky, kz, k2, slot = wave_numbers(where_ref, wave_ref)
+    kx, ky, kz, k2, slot = wave_numbers(wave_ref)
     one = jnp.where(
         (slot == 0) | (slot == 6),
         kx,
@@ -225,9 +238,9 @@
     out_ref[...] = to_bf16(dot(back_ref[...], coeff))
 
 
-def solve_kernel(where_ref, in_ref, spectra_ref, left_ref, wave_ref, back_ref, out_ref):
+def solve_kernel(in_ref, spectra_ref, left_ref, wave_ref, back_ref, out_ref):
     modes = dot(left_ref[...], in_ref[...])
-    kx, ky, kz, k2, slot = wave_numbers(where_ref, wave_ref)
+    kx, ky, kz, k2, slot = wave_numbers(wave_ref)
     scalar = slot == 0
     stable = 1.0 / time_step + mobility * stabilizer * k2
     below = jnp.where(
@@ -292,11 +305,9 @@
         vel_ref[j] = values[32 * (j + 1) : 32 * (j + 2)].reshape(YL, 2, NX)
 
 
-def call(kernel, outs, scratch, *args, scalars=0):
+def call(kernel, outs, scratch, *args, space=pltpu.VMEM, traffic=COST // 400):
     vmem = pl.BlockSpec(memory_space=pltpu.VMEM)
-    specs = [pl.BlockSpec(memory_space=pltpu.SMEM)] * scalars + [vmem] * (
-        len(args) - scalars
-    )
+    specs = [pl.BlockSpec(memory_space=space)] * len(args)
     return pl.pallas_call(
         kernel,
         in_specs=specs,
@@ -304,6 +315,9 @@
         out_shape=outs,
         scratch_shapes=scratch,
         compiler_params=pltpu.CompilerParams(vmem_limit_bytes=16 * 1024 * 1024),
+        cost_estimate=pl.CostEstimate(
+            flops=COST, bytes_accessed=traffic, transcendentals=0
+        ),
     )(*args)
 
 
@@ -324,9 +338,6 @@
     x_table = as_bf16(x_forward_table())
     x_back = as_bf16(x_inverse_table())
     waves = jnp.asarray(wave_table(), f32)
-    where = jnp.stack(
-        [lax.axis_index("col") * AS, lax.axis_index("row") * LO]
-    ).astype(jnp.int32)
 
     def y_tables(zr, direction):
         cos_t, sin_t = twiddles(zr)
@@ -344,12 +355,25 @@
             lines, *y_tables(zr, direction),
         )[0]
 
-    lines = call(x_forward_kernel, [buffer(LINES)], [], phase, velocity, x_table)[0]
+    lines = call(
+        x_forward_kernel, [buffer(LINES)],
+        [
+            pltpu.VMEM(phase.shape, f32),
+            pltpu.VMEM(velocity.shape, f32),
+            pltpu.VMEM(x_table.shape, x_table.dtype),
+            pltpu.SemaphoreType.DMA((3,)),
+        ],
+        *(
+            pltpu.with_memory_space_constraint(v, pltpu.HBM)
+            for v in (phase, velocity, x_table)
+        ),
+        space=pltpu.HBM,
+    )[0]
     planes = y_step(y_forward_kernel, exchange(lines, "col"), 1, -1)
     planes, spectra = call(
         derive_kernel, [buffer(2 * LINES), buffer(2 * MODES, f32)], [],
-        where, exchange(planes, "row"), as_bf16(spread_table()),
-        as_bf16(left_z_table(-1, True)), waves, as_bf16(left_z_table(1, False)), scalars=1,
+        exchange(planes, "row"), as_bf16(spread_table()),
+        as_bf16(left_z_table(-1, True)), waves, as_bf16(left_z_table(1, False)),
     )
     lines = y_step(y_inverse_kernel, exchange(planes, "row"), 2, 1)
     lines = call(
@@ -359,8 +383,8 @@
     planes = y_step(y_forward_kernel, exchange(lines, "col"), 2, -1)
     planes = call(
         solve_kernel, [buffer(LINES)], [],
-        where, exchange(planes, "row"), spectra, as_bf16(left_z_table(-1, False)), waves,
-        as_bf16(left_z_table(1, True)), scalars=1,
+        exchange(planes, "row"), spectra, as_bf16(left_z_table(-1, False)), waves,
+        as_bf16(left_z_table(1, True)),
     )[0]
     lines = y_step(y_inverse_kernel, exchange(planes, "row"), 1, 1)
     return tuple(

time: 162 us -> 151 us (0.932)
  blocking collectives: 96.7 us -> 142 us
  starting transfers between devices: 22.9 us -> 0 us
  waiting for transfers between devices: 22.3 us -> 0 us
  local copies, waits for them, and re-layouts: 8.62 us -> 0.14 us
    all_to_all x6 -> x8, blocking collectives: 96.7 us -> 142 us  [exchange(): lax.all_to_all(values.reshape(rows // 2, 2, 128), axis, split_axis=0, con...]
    all_to_all x2 -> x0, starting transfers between devices: 22.9 us -> none  [exchange(): lax.all_to_all(values.reshape(rows // 2, 2, 128), axis, split_axis=0, con...]
    all_to_all x2 -> x0, waiting for transfers between devices: 22.3 us -> none  [exchange(): lax.all_to_all(values.reshape(rows // 2, 2, 128), axis, split_axis=0, con...]
    unnamed x54 -> x44, local copies, waits for them, and re-layouts: 8.62 us -> 0.14 us
  transfers between devices with their start and end apart: 2 -> 0, of which waited for: 2 -> 0; matrix products, arithmetic and copies ran while one was open for 0% -> 0% of each run, Pallas kernels for 0% -> 0%
where the time goes in v1:
time: 151 us
  blocking collectives  142 us (94%)
  Pallas kernels  8.37 us (6%)
    all_to_all x8, blocking collectives, exchange(): lax.all_to_all(values.reshape(rows // 2, 2, 128), axis, split_axis=0, con...  142 us
    pallas_call x9, Pallas kernels, call(): pl.pallas_call(kernel, in_specs=specs, out_specs=[vmem] * len(outs), out_...  8.37 us

profile of v1, /device:TPU:2, one launch (start us, length us, event | category | flops | bytes accessed | tf_op | source)
XLA Modules:
  0.0 150.9 jit_solution(2796785110732195432)
XLA Ops:
  0.6 0.0 copy-start.12
  0.6 0.0 copy-start.19
  0.7 0.0 copy-start.20
  0.7 0.0 copy-start.21
  0.7 1.5 shard_map.257
  2.2 31.1 %all_to_all.40 = bf16[192,2,128]{2,1,0:T(2,128)(2,1)S(1)} all-to-all(bf16[192,2,128]{2,1,0:T(2,128)(2,1)S(1)} %bitcast.31), channel_id=1, replica_groups=mesh['row'=16,'col'=32] {'col'}, dimensions={0} | all-to-all | bytes 196608 | tf_op jit(solution)/shard_map/all_to_all | solution.py:330
  33.3 0.0 copy-done.12
  33.3 0.0 copy-done.19
  33.3 0.0 copy-done.20
  33.3 0.0 copy-done.21
  33.3 0.0 copy-start.5
  33.3 0.0 copy-start.7
  33.3 0.0 copy-start.8
  33.3 0.0 copy-start.18
  33.3 0.4 shard_map.258
  33.7 13.9 %all_to_all.41 = bf16[192,2,128]{2,1,0:T(2,128)(2,1)S(1)} all-to-all(bf16[192,2,128]{2,1,0:T(2,128)(2,1)S(1)} %bitcast.30), channel_id=1, replica_groups=mesh['row'=16,'col'=32] {'row'}, dimensions={0} | all-to-all | bytes 196608 | tf_op jit(solution)/shard_map/all_to_all | solution.py:330
  47.6 0.0 copy-done.5
  47.6 0.0 copy-done.7
  47.6 0.0 copy-done.8
  47.6 0.0 copy-done.18
  47.6 0.0 copy-start.3
  47.6 0.0 copy-start.13
  47.6 0.0 copy-start.14
  47.7 0.0 copy-start.17
  47.7 1.4 shard_map.259
  49.1 11.4 %all_to_all.42 = bf16[384,2,128]{2,1,0:T(2,128)(2,1)S(1)} all-to-all(bf16[384,2,128]{2,1,0:T(2,128)(2,1)S(1)} %bitcast.16), channel_id=1, replica_groups=mesh['row'=16,'col'=32] {'row'}, dimensions={0} | all-to-all | bytes 393216 | tf_op jit(solution)/shard_map/all_to_all | solution.py:330
  60.5 0.0 copy-done.3
  60.5 0.0 copy-done.13
  60.5 0.0 copy-done.14
  60.5 0.0 copy-done.17
  60.5 0.0 copy-start
  60.5 0.0 copy-start.1
  60.5 0.0 copy-start.9
  60.6 0.0 copy-start.10
  60.6 0.7 shard_map.260
  61.3 22.9 %all_to_all.43 = bf16[384,2,128]{2,1,0:T(2,128)(2,1)S(1)} all-to-all(bf16[384,2,128]{2,1,0:T(2,128)(2,1)S(1)} %bitcast.21), channel_id=1, replica_groups=mesh['row'=16,'col'=32] {'col'}, dimensions={0} | all-to-all | bytes 393216 | tf_op jit(solution)/shard_map/all_to_all | solution.py:330
  84.2 0.0 copy-done
  84.2 0.0 copy-done.1
  84.2 0.0 copy-done.9
  84.2 0.0 copy-done.10
  84.2 0.0 copy-start.2
  84.2 0.0 copy-start.16
  84.3 0.7 shard_map.261
  85.0 21.6 %all_to_all.44 = bf16[384,2,128]{2,1,0:T(2,128)(2,1)S(1)} all-to-all(bf16[384,2,128]{2,1,0:T(2,128)(2,1)S(1)} %bitcast.23), channel_id=1, replica_groups=mesh['row'=16,'col'=32] {'col'}, dimensions={0} | all-to-all | bytes 393216 | tf_op jit(solution)/shard_map/all_to_all | solution.py:330
  106.6 0.0 copy-done.2
  106.6 0.0 copy-done.16
  106.6 0.0 copy-start.4
  106.6 0.0 copy-start.6
  106.6 0.7 shard_map.262
  107.3 12.0 %all_to_all.45 = bf16[384,2,128]{2,1,0:T(2,128)(2,1)S(1)} all-to-all(bf16[384,2,128]{2,1,0:T(2,128)(2,1)S(1)} %bitcast.19), channel_id=1, replica_groups=mesh['row'=16,'col'=32] {'row'}, dimensions={0} | all-to-all | bytes 393216 | tf_op jit(solution)/shard_map/all_to_all | solution.py:330
  119.3 0.0 copy-done.4
  119.3 0.0 copy-done.6
  119.3 0.0 copy-start.11
  119.3 0.0 copy-start.15
  119.3 1.6 %shard_map.263 = bf16[384,128]{1,0:T(8,128)(2,1)S(1)} custom-call(bf16[768,128]{1,0:T(8,128)(2,1)S(1)} %bitcast.17, f32[576,128]{1,0:T(8,128)S(1)} %get-tuple-element.5.spectra_ref, bf16[576,768]{1,0:T(8,128)(2,1)S(1)} %copy-done.6, f32[864,128]{1,0:T(8,128)S(1)} %copy-done.8, bf16[768,576]{1,0:T(8,128)(2,1)S(1)} %copy-done.4), custom_call_target="tpu_custom_call" | custom-call | flops 10000000000 | bytes 25000000 | tf_op jit(solution)/shard_map/pallas_call | solution.py:311
  120.9 10.4 %all_to_all.46 = bf16[192,2,128]{2,1,0:T(2,128)(2,1)S(1)} all-to-all(bf16[192,2,128]{2,1,0:T(2,128)(2,1)S(1)} %bitcast.25), channel_id=1, replica_groups=mesh['row'=16,'col'=32] {'row'}, dimensions={0} | all-to-all | bytes 196608 | tf_op jit(solution)/shard_map/all_to_all | solution.py:330
  131.3 0.0 copy-done.11
  131.3 0.0 copy-done.15
  131.3 0.4 shard_map.264
  131.7 18.2 %all_to_all.47 = bf16[192,2,128]{2,1,0:T(2,128)(2,1)S(1)} all-to-all(bf16[192,2,128]{2,1,0:T(2,128)(2,1)S(1)} %bitcast.27), channel_id=1, replica_groups=mesh['row'=16,'col'=32] {'col'}, dimensions={0} | all-to-all | bytes 196608 | tf_op jit(solution)/shard_map/all_to_all | solution.py:330
  150.0 1.0 shard_map.265
Async XLA Ops:
  0.6 32.6 %copy-start.12 = (bf16[384,384]{1,0:T(8,128)(2,1)S(1)}, bf16[384,384]{1,0:T(8,128)(2,1)}, u32[]{:S(2)}) copy-start(bf16[384,384]{1,0:T(8,128)(2,1)} %constant.63.left_ref) | copy-start | bytes 884740
  0.6 32.6 %copy-start.19 = (bf16[256,256]{1,0:T(8,128)(2,1)S(1)}, bf16[256,256]{1,0:T(8,128)(2,1)}, u32[]{:S(2)}) copy-start(bf16[256,256]{1,0:T(8,128)(2,1)} %constant.64.right_ref) | copy-start | bytes 393220
  0.7 32.6 %copy-start.20 = (f32[192,128]{1,0:T(8,128)S(1)}, f32[192,128]{1,0:T(8,128)}, u32[]{:S(2)}) copy-start(f32[192,128]{1,0:T(8,128)} %constant.45.clone.sin_ref) | copy-start | bytes 294916
  0.7 32.6 %copy-start.21 = (f32[192,128]{1,0:T(8,128)S(1)}, f32[192,128]{1,0:T(8,128)}, u32[]{:S(2)}) copy-start(f32[192,128]{1,0:T(8,128)} %constant.44.clone.cos_ref) | copy-start | bytes 294916
  33.3 14.3 %copy-start.5 = (bf16[768,576]{1,0:T(8,128)(2,1)S(1)}, bf16[768,576]{1,0:T(8,128)(2,1)}, u32[]{:S(2)}) copy-start(bf16[768,576]{1,0:T(8,128)(2,1)} %constant.67.back_ref) | copy-start | bytes 2654212
  33.3 14.3 %copy-start.7 = (bf16[576,768]{1,0:T(8,128)(2,1)S(1)}, bf16[576,768]{1,0:T(8,128)(2,1)}, u32[]{:S(2)}) copy-start(bf16[576,768]{1,0:T(8,128)(2,1)} %constant.66.left_ref) | copy-start | bytes 2654212
  33.3 14.3 %copy-start.8 = (f32[864,128]{1,0:T(8,128)S(1)}, f32[864,128]{1,0:T(8,128)}, u32[]{:S(2)}) copy-start(f32[864,128]{1,0:T(8,128)} %constant.42.clone.wave_ref) | copy-start | bytes 1327108
  33.3 14.3 %copy-start.18 = (bf16[128,512]{1,0:T(8,128)(2,1)S(1)}, bf16[128,512]{1,0:T(8,128)(2,1)}, u32[]{:S(2)}) copy-start(bf16[128,512]{1,0:T(8,128)(2,1)} %constant.65.spread_ref) | copy-start | bytes 393220
  47.6 12.9 %copy-start.3 = (bf16[768,768]{1,0:T(8,128)(2,1)S(1)}, bf16[768,768]{1,0:T(8,128)(2,1)}, u32[]{:S(2)}) copy-start(bf16[768,768]{1,0:T(8,128)(2,1)} %constant.68.left_ref) | copy-start | bytes 3538948
  47.6 12.9 %copy-start.13 = (f32[384,128]{1,0:T(8,128)S(1)}, f32[384,128]{1,0:T(8,128)}, u32[]{:S(2)}) copy-start(f32[384,128]{1,0:T(8,128)} %constant.52.clone.sin_ref) | copy-start | bytes 589828
  47.6 12.9 %copy-start.14 = (f32[384,128]{1,0:T(8,128)S(1)}, f32[384,128]{1,0:T(8,128)}, u32[]{:S(2)}) copy-start(f32[384,128]{1,0:T(8,128)} %constant.51.clone.cos_ref) | copy-start | bytes 589828
  47.7 12.9 %copy-start.17 = (bf16[256,256]{1,0:T(8,128)(2,1)S(1)}, bf16[256,256]{1,0:T(8,128)(2,1)}, u32[]{:S(2)}) copy-start(bf16[256,256]{1,0:T(8,128)(2,1)} %constant.69.right_ref) | copy-start | bytes 393220
  60.5 23.7 %copy-start = (f32[3,16,2,512]{3,2,1,0:T(2,128)S(1)}, f32[3,16,2,512]{3,2,1,0:T(2,128)}, u32[]{:S(2)}) copy-start(f32[3,16,2,512]{3,2,1,0:T(2,128)} %vel_ref.1) | copy-start | bytes 589828
  60.5 23.7 %copy-start.1 = (f32[16,2,512]{2,1,0:T(2,128)S(1)}, f32[16,2,512]{2,1,0:T(2,128)}, u32[]{:S(2)}) copy-start(f32[16,2,512]{2,1,0:T(2,128)} %phase_ref.1) | copy-start | bytes 196612
  60.5 23.7 %copy-start.9 = (bf16[384,512]{1,0:T(8,128)(2,1)S(1)}, bf16[384,512]{1,0:T(8,128)(2,1)}, u32[]{:S(2)}) copy-start(bf16[384,512]{1,0:T(8,128)(2,1)} %constant.70.back_ref) | copy-start | bytes 1179652
  60.6 23.7 %copy-start.10 = (bf16[384,512]{1,0:T(8,128)(2,1)S(1)}, bf16[384,512]{1,0:T(8,128)(2,1)}, u32[]{:S(2)}) copy-start(bf16[384,512]{1,0:T(8,128)(2,1)} %constant.62.table_hbm.table_ref) | copy-start | bytes 1179652
  84.2 22.4 %copy-start.2 = (bf16[768,768]{1,0:T(8,128)(2,1)S(1)}, bf16[768,768]{1,0:T(8,128)(2,1)}, u32[]{:S(2)}) copy-start(bf16[768,768]{1,0:T(8,128)(2,1)} %constant.71.left_ref) | copy-start | bytes 3538948
  84.2 22.4 %copy-start.16 = (bf16[256,256]{1,0:T(8,128)(2,1)S(1)}, bf16[256,256]{1,0:T(8,128)(2,1)}, u32[]{:S(2)}) copy-start(bf16[256,256]{1,0:T(8,128)(2,1)} %constant.72.right_ref) | copy-start | bytes 393220
  106.6 12.7 %copy-start.4 = (bf16[768,576]{1,0:T(8,128)(2,1)S(1)}, bf16[768,576]{1,0:T(8,128)(2,1)}, u32[]{:S(2)}) copy-start(bf16[768,576]{1,0:T(8,128)(2,1)} %constant.74.back_ref) | copy-start | bytes 2654212
  106.6 12.7 %copy-start.6 = (bf16[576,768]{1,0:T(8,128)(2,1)S(1)}, bf16[576,768]{1,0:T(8,128)(2,1)}, u32[]{:S(2)}) copy-start(bf16[576,768]{1,0:T(8,128)(2,1)} %constant.73.left_ref) | copy-start | bytes 2654212
  119.3 12.0 %copy-start.11 = (bf16[384,384]{1,0:T(8,128)(2,1)S(1)}, bf16[384,384]{1,0:T(8,128)(2,1)}, u32[]{:S(2)}) copy-start(bf16[384,384]{1,0:T(8,128)(2,1)} %constant.75.left_ref) | copy-start | bytes 884740
  119.3 12.0 %copy-start.15 = (bf16[256,256]{1,0:T(8,128)(2,1)S(1)}, bf16[256,256]{1,0:T(8,128)(2,1)}, u32[]{:S(2)}) copy-start(bf16[256,256]{1,0:T(8,128)(2,1)} %constant.76.right_ref) | copy-start | bytes 393220

commit v2 on v1

--- a/solution.py
+++ b/solution.py
@@ -5,6 +5,7 @@
 from jax import lax
 from jax.experimental import pallas as pl
 from jax.experimental.pallas import tpu as pltpu
+from jax.sharding import Mesh
 from jax.sharding import PartitionSpec as P
 
 NX = 512
@@ -13,16 +14,19 @@
 KC = 192
 KZ = 24
 COLS = 32
-ROWS = 16
-AS = KC // COLS
-LO = 32 // ROWS
+FAR = 2
+NEAR = 8
+AS = KC // (FAR * COLS)
+LO = 32 // NEAR
 YL = NY // COLS
 QS = 12
 QP = 16
 BATCH = AS * LO
 MODES = KZ * BATCH
-LINES = COLS * AS * 2
+LINES = 2 * KC
 COST = 10_000_000_000
+
+BIG = ("far", "col")
 
 time_step = 0.001
 epsilon = 0.01
@@ -58,55 +62,69 @@
 def left_y_table(zr, direction):
     k32 = np.arange(32)
     c, s = roots(k32[:, None] * np.arange(COLS)[None, :], 32)
-    same = np.einsum("ab,zy->abzy", np.eye(AS), np.eye(zr))
-    rot = complex_rotation(c, direction * s).reshape(2, 2, ROWS, LO, COLS)
-    n = 2 * 32 * AS * zr
+    same = np.einsum("ab,xw,zy->abxwzy", np.eye(AS), np.eye(FAR), np.eye(zr))
+    rot = complex_rotation(c, direction * s).reshape(2, 2, NEAR, LO, COLS)
+    n = LINES * zr
     if direction < 0:
-        return np.einsum("pqrlc,abzy->pralzcbqy", rot, same).reshape(n, n)
-    return np.einsum("pqrlc,abzy->capzqrbly", rot, same).reshape(n, n)
-
-
-def twiddles(zr):
-    k32 = np.arange(32).reshape(ROWS, 1, LO, 1, 1)
-    yl = lane_yl(zr).reshape(1, 1, 1, 1, 128)
-    c, s = roots(np.broadcast_to(k32 * yl, (ROWS, AS, LO, zr, 128)), 512)
+        return np.einsum("pqrlc,abxwzy->pralxzwcbqy", rot, same).reshape(n, n)
+    return np.einsum("pqrlc,abxwzy->xcapzqrblwy", rot, same).reshape(n, n)
+
+
+def twiddles(zr, lanes):
+    k32 = np.arange(32).reshape(NEAR, 1, LO, 1, 1)
+    full = (NEAR, AS, LO, FAR * zr, 128)
+    c, s = roots(np.broadcast_to(k32 * lanes.reshape(1, 1, 1, 1, 128), full), 512)
     return c.reshape(-1, 128), s.reshape(-1, 128)
 
 
-def lane_yl(zr):
-    if zr == 1:
-        return np.broadcast_to(np.arange(YL)[None, :, None], (4, YL, 2)).reshape(-1)
+def lanes_yz():
+    return np.broadcast_to(np.arange(YL)[None, :, None], (4, YL, 2)).reshape(-1)
+
+
+def lanes_y():
     return np.broadcast_to(np.arange(YL)[None, :], (8, YL)).reshape(-1)
 
 
-def right_y_table(zr, direction):
+def short_rotation(direction):
     q = np.arange(QS) - QS // 2
     c, s = np.zeros((2, QP, YL))
     c[:QS], s[:QS] = roots(q[:, None] * np.arange(YL)[None, :], 16)
-    rot = complex_rotation(c, direction * s)
+    return complex_rotation(c, direction * s)
+
+
+def right_y_table(zr, direction):
+    rot = short_rotation(direction)
     eye = np.eye
     if zr == 1:
         if direction < 0:
             out = np.einsum("pkqy,fg,zw->kfyzpwgq", rot, eye(4), eye(2))
         else:
             out = np.einsum("pkqy,fg,zw->kzfqpgyw", rot, eye(4), eye(2))
-    elif direction < 0:
-        out = np.einsum("pkqy,fg->kfypgq", rot, eye(8))
     else:
         out = np.einsum("pkqy,fg->kfqpgy", rot, eye(8))
     return out.reshape(256, 256)
 
 
+def right_merge_table():
+    rot = short_rotation(-1)
+    out = np.zeros((2, 16, YL, 2, 2, 8, QP))
+    for z in range(2):
+        for f in range(4):
+            out[:, 4 * z + f, :, z, :, f, :] = np.einsum("pkqy->kypq", rot)
+        out[:, 15 - z, :, z, :, 4, :] = np.einsum("pkqy->kypq", rot)
+    return out.reshape(512, 512)
+
+
 def left_z_table(direction, z_major):
     q = np.arange(KZ) - KZ // 2
     c, s = roots(q[:, None] * np.arange(NZ)[None, :], NZ)
-    rot = complex_rotation(c, direction * s).reshape(2, 2, KZ, ROWS, 2)
+    rot = complex_rotation(c, direction * s).reshape(2, 2, KZ, FAR, NEAR, 2)
     same = np.eye(BATCH)
     if direction < 0:
-        form = "pkmsz,ab->pmazsbk" if z_major else "pkmsz,ab->pmasbzk"
+        form = "pkmxsz,ab->pmazsbxk" if z_major else "pkmxsz,ab->pmasbxzk"
         out = np.einsum(form, rot, same).reshape(2 * MODES, -1)
         return out / (NX * NY * NZ)
-    form = "pkmsz,ab->zsapkmb" if z_major else "pkmsz,ab->sazpkmb"
+    form = "pkmxsz,ab->zsaxpkmb" if z_major else "pkmxsz,ab->saxzpkmb"
     return np.einsum(form, rot, same).reshape(-1, 2 * MODES)
 
 
@@ -159,7 +177,8 @@
 
 
 def x_forward_kernel(
-    phase_hbm, vel_hbm, table_hbm, out_ref, phase_ref, vel_ref, table_ref, sems
+    phase_hbm, vel_hbm, table_hbm, out_ref, bulk_ref, phase_ref, vel_ref, table_ref,
+    sems, wide,
 ):
     copies = [
         pltpu.make_async_copy(src, dst, sems.at[i])
@@ -174,7 +193,14 @@
     x = jnp.concatenate(
         [flat_rows(phase_ref)] + [flat_rows(vel_ref, j) for j in range(3)], axis=0
     )
-    out_ref[...] = to_bf16(dot_nt(table_ref[...], to_bf16(x)))
+    table = table_ref[...]
+    out_ref[...] = to_bf16(dot_nt(table, to_bf16(x)))
+    for z in range(2):
+        phase = phase_ref[:, z, :]
+        bulk = to_bf16(phase * phase * phase - phase)
+        padded = jnp.concatenate([jnp.zeros((7 * YL, NX), jnp.bfloat16), bulk], axis=0)
+        wide[pl.ds(z, LINES, stride=2), :] = dot_nt(table, padded)
+    bulk_ref[...] = to_bf16(wide[...])
 
 
 def y_forward_kernel(in_ref, left_ref, cos_ref, sin_ref, right_ref, out_ref, wide):
@@ -189,7 +215,22 @@
     out_ref[...] = to_bf16(wide[...])
 
 
-def y_inverse_kernel(in_ref, left_ref, cos_ref, sin_ref, right_ref, out_ref, wide):
+def y_merge_kernel(in_ref, bulk_ref, left_ref, cos_ref, sin_ref, right_ref, out_ref, wide):
+    half = in_ref.shape[0] // 2
+    sums = dot(left_ref[...], jnp.concatenate([in_ref[...], bulk_ref[...]], axis=1))
+    c, s = cos_ref[...], sin_ref[...]
+    res, ims = [], []
+    for t in range(2):
+        re, im = (sums[p * half : (p + 1) * half, 128 * t : 128 * (t + 1)] for p in range(2))
+        res.append(to_bf16(re * c + im * s))
+        ims.append(to_bf16(im * c - re * s))
+    modes = dot(jnp.concatenate(res + ims, axis=1), right_ref[...])
+    for t in range(4):
+        wide[pl.ds(t, half, stride=4), :] = modes[:, 128 * t : 128 * (t + 1)]
+    out_ref[...] = to_bf16(wide[...])
+
+
+def y_inverse(in_ref, left_ref, cos_ref, sin_ref, right_ref, wide):
     half = in_ref.shape[0] // 2
     wide[...] = in_ref[...].astype(jnp.float32)
     modes = jnp.concatenate(
@@ -199,12 +240,28 @@
     re, im = lines[:, :128], lines[:, 128:]
     c, s = cos_ref[...], sin_ref[...]
     spun = jnp.concatenate([to_bf16(re * c - im * s), to_bf16(re * s + im * c)], axis=0)
-    out_ref[...] = to_bf16(dot(left_ref[...], spun))
+    return dot(left_ref[...], spun)
+
+
+def y_inverse_kernel(in_ref, left_ref, cos_ref, sin_ref, right_ref, out_ref, wide):
+    out_ref[...] = to_bf16(y_inverse(in_ref, left_ref, cos_ref, sin_ref, right_ref, wide))
+
+
+def y_inverse_rider_kernel(
+    in_ref, rider_ref, left_ref, cos_ref, sin_ref, right_ref, out_ref, wide
+):
+    lines = y_inverse(in_ref, left_ref, cos_ref, sin_ref, right_ref, wide)
+    lane = lax.broadcasted_iota(jnp.int32, lines.shape, 1)
+    out_ref[...] = to_bf16(
+        jnp.where(lane < 7 * YL, lines, rider_ref[...].astype(jnp.float32))
+    )
 
 
 def wave_numbers(wave_ref):
-    kx = wave_ref[0:MODES] + (lax.axis_index("col") * AS).astype(jnp.float32)
-    ky = wave_ref[MODES : 2 * MODES] + (lax.axis_index("row") * LO).astype(jnp.float32)
+    kx = wave_ref[0:MODES] + (
+        (lax.axis_index("far") * COLS + lax.axis_index("col")) * AS
+    ).astype(jnp.float32)
+    ky = wave_ref[MODES : 2 * MODES] + (lax.axis_index("near") * LO).astype(jnp.float32)
     kz = wave_ref[2 * MODES : 3 * MODES]
     slot = lax.broadcasted_iota(jnp.int32, (MODES, 128), 1) // QP
     return kx, ky, kz, kx * kx + ky * ky + kz * kz, slot
@@ -272,29 +329,31 @@
     out_ref[...] = to_bf16(both[:half] + pltpu.roll(both[half:], 64, 1))
 
 
-def nonlinear_kernel(in_ref, phase_ref, vel_ref, back_ref, table_ref, out_ref, wide):
+def nonlinear_kernel(
+    in_ref, phase_ref, vel_ref, back_ref, table_ref, out_ref, bulk_ref, wide
+):
     wide[...] = in_ref[...].astype(jnp.float32)
+    sides = [wide[pl.ds(z, LINES, stride=2), :] for z in range(2)]
+    lane = lax.broadcasted_iota(jnp.int32, (LINES, 128), 1)
+    bulk_ref[...] = to_bf16(
+        jnp.where(lane < 7 * YL, pltpu.roll(sides[1], 7 * YL, 1), sides[0])
+    )
+    terms = []
     for z in range(2):
-        lines = to_bf16(wide[pl.ds(z, LINES, stride=2), :].T)
-        values = dot(lines, back_ref[...])
+        values = dot(to_bf16(sides[z].T), back_ref[...])
         d = [values[YL * f : YL * (f + 1)] for f in range(7)]
         phase = phase_ref[:, z, :]
         v = [vel_ref[j, :, z, :] for j in range(3)]
         g, lap, w = d[0:3], d[3], d[4:7]
-        advect = v[0] * g[0] + v[1] * g[1] + v[2] * g[2]
-        bulk = phase * phase * phase - phase
-        potential = bulk - epsilon * epsilon * lap
-        terms = [
-            advect,
+        potential = phase * phase * phase - phase - epsilon * epsilon * lap
+        terms += [
+            v[0] * g[0] + v[1] * g[1] + v[2] * g[2],
             v[1] * w[2] - v[2] * w[1] + potential * g[0],
             v[2] * w[0] - v[0] * w[2] + potential * g[1],
             v[0] * w[1] - v[1] * w[0] + potential * g[2],
-            bulk,
-            jnp.zeros((3 * YL, NX), jnp.float32),
         ]
-        x = jnp.concatenate([to_bf16(t) for t in terms], axis=0)
-        wide[pl.ds(z, LINES, stride=2), :] = dot_nt(table_ref[...], x)
-    out_ref[...] = to_bf16(wide[...])
+    x = jnp.concatenate([to_bf16(t) for t in terms], axis=0)
+    out_ref[...] = to_bf16(dot_nt(table_ref[...], x))
 
 
 def x_inverse_kernel(in_ref, back_ref, phase_ref, vel_ref):
@@ -305,7 +364,7 @@
         vel_ref[j] = values[32 * (j + 1) : 32 * (j + 2)].reshape(YL, 2, NX)
 
 
-def call(kernel, outs, scratch, *args, space=pltpu.VMEM, traffic=COST // 400):
+def call(kernel, outs, scratch, *args, space=pltpu.VMEM):
     vmem = pl.BlockSpec(memory_space=pltpu.VMEM)
     specs = [pl.BlockSpec(memory_space=space)] * len(args)
     return pl.pallas_call(
@@ -316,7 +375,7 @@
         scratch_shapes=scratch,
         compiler_params=pltpu.CompilerParams(vmem_limit_bytes=16 * 1024 * 1024),
         cost_estimate=pl.CostEstimate(
-            flops=COST, bytes_accessed=traffic, transcendentals=0
+            flops=COST, bytes_accessed=COST // 400, transcendentals=0
         ),
     )(*args)
 
@@ -339,54 +398,61 @@
     x_back = as_bf16(x_inverse_table())
     waves = jnp.asarray(wave_table(), f32)
 
-    def y_tables(zr, direction):
-        cos_t, sin_t = twiddles(zr)
-        return (
-            as_bf16(left_y_table(zr, direction)),
-            jnp.asarray(cos_t, f32),
-            jnp.asarray(sin_t, f32),
-            as_bf16(right_y_table(zr, direction)),
-        )
-
-    def y_step(kernel, lines, zr, direction):
-        rows = LINES * zr
-        return call(
-            kernel, [buffer(rows)], [pltpu.VMEM((rows, 128), f32)],
-            lines, *y_tables(zr, direction),
-        )[0]
-
-    lines = call(
-        x_forward_kernel, [buffer(LINES)],
+    def spin(zr, lanes):
+        return tuple(jnp.asarray(t, f32) for t in twiddles(zr, lanes))
+
+    def scratch(rows):
+        return pltpu.VMEM((rows, 128), f32)
+
+    lines, rider = call(
+        x_forward_kernel, [buffer(LINES), buffer(2 * LINES)],
         [
             pltpu.VMEM(phase.shape, f32),
             pltpu.VMEM(velocity.shape, f32),
             pltpu.VMEM(x_table.shape, x_table.dtype),
             pltpu.SemaphoreType.DMA((3,)),
+            scratch(2 * LINES),
         ],
         *(
             pltpu.with_memory_space_constraint(v, pltpu.HBM)
             for v in (phase, velocity, x_table)
         ),
         space=pltpu.HBM,
+    )
+    planes = call(
+        y_forward_kernel, [buffer(LINES)], [scratch(LINES)],
+        exchange(lines, BIG), as_bf16(left_y_table(1, -1)), *spin(1, lanes_yz()),
+        as_bf16(right_y_table(1, -1)),
     )[0]
-    planes = y_step(y_forward_kernel, exchange(lines, "col"), 1, -1)
     planes, spectra = call(
         derive_kernel, [buffer(2 * LINES), buffer(2 * MODES, f32)], [],
-        exchange(planes, "row"), as_bf16(spread_table()),
+        exchange(planes, "near"), as_bf16(spread_table()),
         as_bf16(left_z_table(-1, True)), waves, as_bf16(left_z_table(1, False)),
     )
-    lines = y_step(y_inverse_kernel, exchange(planes, "row"), 2, 1)
     lines = call(
-        nonlinear_kernel, [buffer(2 * LINES)], [pltpu.VMEM((2 * LINES, 128), f32)],
-        exchange(lines, "col"), phase, velocity, x_back, x_table,
+        y_inverse_rider_kernel, [buffer(2 * LINES)], [scratch(2 * LINES)],
+        exchange(planes, "near"), rider, as_bf16(left_y_table(2, 1)), *spin(2, lanes_y()),
+        as_bf16(right_y_table(2, 1)),
     )[0]
-    planes = y_step(y_forward_kernel, exchange(lines, "col"), 2, -1)
+    lines, bulk = call(
+        nonlinear_kernel, [buffer(LINES), buffer(LINES)], [scratch(2 * LINES)],
+        exchange(lines, BIG), phase, velocity, x_back, x_table,
+    )
+    planes = call(
+        y_merge_kernel, [buffer(2 * LINES)], [scratch(2 * LINES)],
+        exchange(lines, BIG), bulk, as_bf16(left_y_table(1, -1)), *spin(1, lanes_y()),
+        as_bf16(right_merge_table()),
+    )[0]
     planes = call(
         solve_kernel, [buffer(LINES)], [],
-        exchange(planes, "row"), spectra, as_bf16(left_z_table(-1, False)), waves,
+        exchange(planes, "near"), spectra, as_bf16(left_z_table(-1, False)), waves,
         as_bf16(left_z_table(1, True)),
     )[0]
-    lines = y_step(y_inverse_kernel, exchange(planes, "row"), 1, 1)
+    lines = call(
+        y_inverse_kernel, [buffer(LINES)], [scratch(LINES)],
+        exchange(planes, "near"), as_bf16(left_y_table(1, 1)), *spin(1, lanes_yz()),
+        as_bf16(right_y_table(1, 1)),
+    )[0]
     return tuple(
         call(
             x_inverse_kernel,
@@ -394,14 +460,18 @@
                 jax.ShapeDtypeStruct(phase.shape, f32),
                 jax.ShapeDtypeStruct(velocity.shape, f32),
             ],
-            [], exchange(lines, "col"), x_back,
+            [], exchange(lines, BIG), x_back,
         )
     )
 
 
 def solution(mesh):
-    in_specs = (P("col", "row", None), P(None, "col", "row", None))
-    out_specs = (P("col", "row", None), P(None, "col", "row", None))
+    finer = Mesh(
+        mesh.devices.reshape(FAR, NEAR, mesh.shape["col"]), ("far", "near", "col")
+    )
+    row = ("far", "near")
+    in_specs = (P("col", row, None), P(None, "col", row, None))
+    out_specs = (P("col", row, None), P(None, "col", row, None))
     return jax.shard_map(
-        on_device, mesh=mesh, in_specs=in_specs, out_specs=out_specs, check_vma=False
-    )
+        on_device, mesh=finer, in_specs=in_specs, out_specs=out_specs, check_vma=False
+    )

time: 151 us -> 145 us (0.960)
  blocking collectives: 142 us -> 135 us
    all_to_all x8, blocking collectives: 142 us -> 135 us  [exchange(): lax.all_to_all(values.reshape(rows // 2, 2, 128), axis, split_axis=0, con...]
where the time goes in v2:
time: 145 us
  blocking collectives  135 us (93%)
  Pallas kernels  8.48 us (6%)
    all_to_all x8, blocking collectives, exchange(): lax.all_to_all(values.reshape(rows // 2, 2, 128), axis, split_axis=0, con...  135 us
    pallas_call x9, Pallas kernels, call(): pl.pallas_call(kernel, in_specs=specs, out_specs=[vmem] * len(outs), out_...  8.48 us

profile of v2, /device:TPU:2, one launch (start us, length us, event | category | flops | bytes accessed | tf_op | source)
XLA Modules:
  0.0 144.7 jit_solution(15548639568313479176)
XLA Ops:
  0.6 0.0 copy-start.12
  0.6 0.0 copy-start.18
  0.7 0.0 copy-start.19
  0.7 0.0 copy-start.20
  0.7 1.7 %shard_map.257 = (bf16[384,128]{1,0:T(8,128)(2,1)S(1)}, bf16[768,128]{1,0:T(8,128)(2,1)S(1)}) custom-call(f32[16,2,512]{2,1,0:T(2,128)} %phase_ref.1, f32[3,16,2,512]{3,2,1,0:T(2,128)} %vel_ref.1, bf16[384,512]{1,0:T(8,128)(2,1)} %constant.65.table_hbm.table_ref), custom_call_target="tpu_custom_call" | custom-call | flops 10000000000 | bytes 25000000 | tf_op jit(solution)/shard_map/pallas_call | solution.py:370
  2.4 34.0 %all_to_all.40 = bf16[192,2,128]{2,1,0:T(2,128)(2,1)S(1)} all-to-all(bf16[192,2,128]{2,1,0:T(2,128)(2,1)S(1)} %bitcast.29), channel_id=1, replica_groups=mesh['far'=2,'near'=8,'col'=32] {'far','col'}, dimensions={0} | all-to-all | bytes 196608 | tf_op jit(solution)/shard_map/all_to_all | solution.py:389
  36.4 0.0 copy-done.12
  36.4 0.0 copy-done.18
  36.4 0.0 copy-done.19
  36.4 0.0 copy-done.20
  36.4 0.0 copy-start.4
  36.4 0.0 copy-start.6
  36.4 0.0 copy-start.8
  36.5 0.0 copy-start.17
  36.5 0.4 shard_map.258
  36.9 10.2 %all_to_all.41 = bf16[192,2,128]{2,1,0:T(2,128)(2,1)S(1)} all-to-all(bf16[192,2,128]{2,1,0:T(2,128)(2,1)S(1)} %bitcast.31), channel_id=1, replica_groups=mesh['far'=2,'near'=8,'col'=32] {'near'}, dimensions={0} | all-to-all | bytes 196608 | tf_op jit(solution)/shard_map/all_to_all | solution.py:389
  47.1 0.0 copy-done.4
  47.1 0.0 copy-done.6
  47.1 0.0 copy-done.8
  47.1 0.0 copy-done.17
  47.1 0.0 copy-start.2
  47.1 0.0 copy-start.13
  47.1 0.0 copy-start.14
  47.1 0.0 copy-start.16
  47.1 1.4 shard_map.259
  48.5 9.2 %all_to_all.42 = bf16[384,2,128]{2,1,0:T(2,128)(2,1)S(1)} all-to-all(bf16[384,2,128]{2,1,0:T(2,128)(2,1)S(1)} %bitcast.17), channel_id=1, replica_groups=mesh['far'=2,'near'=8,'col'=32] {'near'}, dimensions={0} | all-to-all | bytes 393216 | tf_op jit(solution)/shard_map/all_to_all | solution.py:389
  57.7 0.0 copy-done.2
  57.7 0.0 copy-done.13
  57.7 0.0 copy-done.14
  57.7 0.0 copy-done.16
  57.8 0.0 copy-start
  57.8 0.0 copy-start.1
  57.8 0.0 copy-start.9
  57.8 0.0 copy-start.10
  57.8 0.7 shard_map.260
  58.6 23.9 %all_to_all.43 = bf16[384,2,128]{2,1,0:T(2,128)(2,1)S(1)} all-to-all(bf16[384,2,128]{2,1,0:T(2,128)(2,1)S(1)} %bitcast.18), channel_id=1, replica_groups=mesh['far'=2,'near'=8,'col'=32] {'far','col'}, dimensions={0} | all-to-all | bytes 393216 | tf_op jit(solution)/shard_map/all_to_all | solution.py:389
  82.5 0.0 copy-done
  82.5 0.0 copy-done.1
  82.5 0.0 copy-done.9
  82.5 0.0 copy-done.10
  82.5 0.0 copy-start.7
  82.5 0.0 copy-start.21
  82.5 0.0 copy-start.22
  82.6 0.6 shard_map.261
  83.2 20.2 %all_to_all.44 = bf16[192,2,128]{2,1,0:T(2,128)(2,1)S(1)} all-to-all(bf16[192,2,128]{2,1,0:T(2,128)(2,1)S(1)} %bitcast.27), channel_id=1, replica_groups=mesh['far'=2,'near'=8,'col'=32] {'far','col'}, dimensions={0} | all-to-all | bytes 196608 | tf_op jit(solution)/shard_map/all_to_all | solution.py:389
  103.3 0.0 copy-done.7
  103.3 0.0 copy-done.21
  103.3 0.0 copy-done.22
  103.3 0.0 copy-start.3
  103.4 0.0 copy-start.5
  103.4 0.6 shard_map.262
  104.0 9.2 %all_to_all.45 = bf16[384,2,128]{2,1,0:T(2,128)(2,1)S(1)} all-to-all(bf16[384,2,128]{2,1,0:T(2,128)(2,1)S(1)} %bitcast.19), channel_id=1, replica_groups=mesh['far'=2,'near'=8,'col'=32] {'near'}, dimensions={0} | all-to-all | bytes 393216 | tf_op jit(solution)/shard_map/all_to_all | solution.py:389
  113.2 0.0 copy-done.3
  113.2 0.0 copy-done.5
  113.2 0.0 copy-start.11
  113.2 0.0 copy-start.15
  113.2 1.6 %shard_map.263 = bf16[384,128]{1,0:T(8,128)(2,1)S(1)} custom-call(bf16[768,128]{1,0:T(8,128)(2,1)S(1)} %bitcast.20, f32[576,128]{1,0:T(8,128)S(1)} %get-tuple-element.13.spectra_ref, bf16[576,768]{1,0:T(8,128)(2,1)S(1)} %copy-done.5, f32[864,128]{1,0:T(8,128)S(1)} %copy-done.8, bf16[768,576]{1,0:T(8,128)(2,1)S(1)} %copy-done.3), custom_call_target="tpu_custom_call" | custom-call | flops 10000000000 | bytes 25000000 | tf_op jit(solution)/shard_map/pallas_call | solution.py:370
  114.8 8.2 %all_to_all.46 = bf16[192,2,128]{2,1,0:T(2,128)(2,1)S(1)} all-to-all(bf16[192,2,128]{2,1,0:T(2,128)(2,1)S(1)} %bitcast.24), channel_id=1, replica_groups=mesh['far'=2,'near'=8,'col'=32] {'near'}, dimensions={0} | all-to-all | bytes 196608 | tf_op jit(solution)/shard_map/all_to_all | solution.py:389
  123.0 0.0 copy-done.11
  123.0 0.0 copy-done.15
  123.0 0.4 shard_map.264
  123.4 20.3 %all_to_all.47 = bf16[192,2,128]{2,1,0:T(2,128)(2,1)S(1)} all-to-all(bf16[192,2,128]{2,1,0:T(2,128)(2,1)S(1)} %bitcast.26), channel_id=1, replica_groups=mesh['far'=2,'near'=8,'col'=32] {'far','col'}, dimensions={0} | all-to-all | bytes 196608 | tf_op jit(solution)/shard_map/all_to_all | solution.py:389
  143.8 1.0 shard_map.265
Async XLA Ops:
  0.6 35.8 %copy-start.12 = (bf16[384,384]{1,0:T(8,128)(2,1)S(1)}, bf16[384,384]{1,0:T(8,128)(2,1)}, u32[]{:S(2)}) copy-start(bf16[384,384]{1,0:T(8,128)(2,1)} %constant.66.left_ref) | copy-start | bytes 884740
  0.6 35.8 %copy-start.18 = (bf16[256,256]{1,0:T(8,128)(2,1)S(1)}, bf16[256,256]{1,0:T(8,128)(2,1)}, u32[]{:S(2)}) copy-start(bf16[256,256]{1,0:T(8,128)(2,1)} %constant.67.right_ref) | copy-start | bytes 393220
  0.7 35.7 %copy-start.19 = (f32[192,128]{1,0:T(8,128)S(1)}, f32[192,128]{1,0:T(8,128)}, u32[]{:S(2)}) copy-start(f32[192,128]{1,0:T(8,128)} %constant.47.clone.sin_ref) | copy-start | bytes 294916
  0.7 35.7 %copy-start.20 = (f32[192,128]{1,0:T(8,128)S(1)}, f32[192,128]{1,0:T(8,128)}, u32[]{:S(2)}) copy-start(f32[192,128]{1,0:T(8,128)} %constant.46.clone.cos_ref) | copy-start | bytes 294916
  36.4 10.7 %copy-start.4 = (bf16[768,576]{1,0:T(8,128)(2,1)S(1)}, bf16[768,576]{1,0:T(8,128)(2,1)}, u32[]{:S(2)}) copy-start(bf16[768,576]{1,0:T(8,128)(2,1)} %constant.70.back_ref) | copy-start | bytes 2654212
  36.4 10.6 %copy-start.6 = (bf16[576,768]{1,0:T(8,128)(2,1)S(1)}, bf16[576,768]{1,0:T(8,128)(2,1)}, u32[]{:S(2)}) copy-start(bf16[576,768]{1,0:T(8,128)(2,1)} %constant.69.left_ref) | copy-start | bytes 2654212
  36.4 10.6 %copy-start.8 = (f32[864,128]{1,0:T(8,128)S(1)}, f32[864,128]{1,0:T(8,128)}, u32[]{:S(2)}) copy-start(f32[864,128]{1,0:T(8,128)} %constant.44.clone.wave_ref) | copy-start | bytes 1327108
  36.5 10.6 %copy-start.17 = (bf16[128,512]{1,0:T(8,128)(2,1)S(1)}, bf16[128,512]{1,0:T(8,128)(2,1)}, u32[]{:S(2)}) copy-start(bf16[128,512]{1,0:T(8,128)(2,1)} %constant.68.spread_ref) | copy-start | bytes 393220
  47.1 10.7 %copy-start.2 = (bf16[768,768]{1,0:T(8,128)(2,1)S(1)}, bf16[768,768]{1,0:T(8,128)(2,1)}, u32[]{:S(2)}) copy-start(bf16[768,768]{1,0:T(8,128)(2,1)} %constant.71.left_ref) | copy-start | bytes 3538948
  47.1 10.6 %copy-start.13 = (f32[384,128]{1,0:T(8,128)S(1)}, f32[384,128]{1,0:T(8,128)}, u32[]{:S(2)}) copy-start(f32[384,128]{1,0:T(8,128)} %constant.54.clone.sin_ref) | copy-start | bytes 589828
  47.1 10.6 %copy-start.14 = (f32[384,128]{1,0:T(8,128)S(1)}, f32[384,128]{1,0:T(8,128)}, u32[]{:S(2)}) copy-start(f32[384,128]{1,0:T(8,128)} %constant.53.clone.cos_ref) | copy-start | bytes 589828
  47.1 10.6 %copy-start.16 = (bf16[256,256]{1,0:T(8,128)(2,1)S(1)}, bf16[256,256]{1,0:T(8,128)(2,1)}, u32[]{:S(2)}) copy-start(bf16[256,256]{1,0:T(8,128)(2,1)} %constant.72.right_ref) | copy-start | bytes 393220
  57.8 24.7 %copy-start = (f32[3,16,2,512]{3,2,1,0:T(2,128)S(1)}, f32[3,16,2,512]{3,2,1,0:T(2,128)}, u32[]{:S(2)}) copy-start(f32[3,16,2,512]{3,2,1,0:T(2,128)} %vel_ref.1) | copy-start | bytes 589828
  57.8 24.7 %copy-start.1 = (f32[16,2,512]{2,1,0:T(2,128)S(1)}, f32[16,2,512]{2,1,0:T(2,128)}, u32[]{:S(2)}) copy-start(f32[16,2,512]{2,1,0:T(2,128)} %phase_ref.1) | copy-start | bytes 196612
  57.8 24.7 %copy-start.9 = (bf16[384,512]{1,0:T(8,128)(2,1)S(1)}, bf16[384,512]{1,0:T(8,128)(2,1)}, u32[]{:S(2)}) copy-start(bf16[384,512]{1,0:T(8,128)(2,1)} %constant.73.back_ref) | copy-start | bytes 1179652
  57.8 24.7 %copy-start.10 = (bf16[384,512]{1,0:T(8,128)(2,1)S(1)}, bf16[384,512]{1,0:T(8,128)(2,1)}, u32[]{:S(2)}) copy-start(bf16[384,512]{1,0:T(8,128)(2,1)} %constant.65.table_hbm.table_ref) | copy-start | bytes 1179652
  82.5 20.8 %copy-start.7 = (bf16[512,512]{1,0:T(8,128)(2,1)S(1)}, bf16[512,512]{1,0:T(8,128)(2,1)}, u32[]{:S(2)}) copy-start(bf16[512,512]{1,0:T(8,128)(2,1)} %constant.74.right_ref) | copy-start | bytes 1572868
  82.5 20.8 %copy-start.21 = (f32[192,128]{1,0:T(8,128)S(1)}, f32[192,128]{1,0:T(8,128)}, u32[]{:S(2)}) copy-start(f32[192,128]{1,0:T(8,128)} %constant.57.clone.sin_ref) | copy-start | bytes 294916
  82.5 20.8 %copy-start.22 = (f32[192,128]{1,0:T(8,128)S(1)}, f32[192,128]{1,0:T(8,128)}, u32[]{:S(2)}) copy-start(f32[192,128]{1,0:T(8,128)} %constant.56.clone.cos_ref) | copy-start | bytes 294916
  103.3 9.9 %copy-start.3 = (bf16[768,576]{1,0:T(8,128)(2,1)S(1)}, bf16[768,576]{1,0:T(8,128)(2,1)}, u32[]{:S(2)}) copy-start(bf16[768,576]{1,0:T(8,128)(2,1)} %constant.76.back_ref) | copy-start | bytes 2654212
  103.4 9.9 %copy-start.5 = (bf16[576,768]{1,0:T(8,128)(2,1)S(1)}, bf16[576,768]{1,0:T(8,128)(2,1)}, u32[]{:S(2)}) copy-start(bf16[576,768]{1,0:T(8,128)(2,1)} %constant.75.left_ref) | copy-start | bytes 2654212
  113.2 9.8 %copy-start.11 = (bf16[384,384]{1,0:T(8,128)(2,1)S(1)}, bf16[384,384]{1,0:T(8,128)(2,1)}, u32[]{:S(2)}) copy-start(bf16[384,384]{1,0:T(8,128)(2,1)} %constant.77.left_ref) | copy-start | bytes 884740
  113.2 9.8 %copy-start.15 = (bf16[256,256]{1,0:T(8,128)(2,1)S(1)}, bf16[256,256]{1,0:T(8,128)(2,1)}, u32[]{:S(2)}) copy-start(bf16[256,256]{1,0:T(8,128)(2,1)} %constant.78.right_ref) | copy-start | bytes 393220

commit v3 on v2

--- a/solution.py
+++ b/solution.py
@@ -21,12 +21,11 @@
 YL = NY // COLS
 QS = 12
 QP = 16
-BATCH = AS * LO
-MODES = KZ * BATCH
+MODES = KZ * LO
 LINES = 2 * KC
 COST = 10_000_000_000
 
-BIG = ("far", "col")
+BIG = ("xl", "far", "z")
 
 time_step = 0.001
 epsilon = 0.01
@@ -63,11 +62,11 @@
     k32 = np.arange(32)
     c, s = roots(k32[:, None] * np.arange(COLS)[None, :], 32)
     same = np.einsum("ab,xw,zy->abxwzy", np.eye(AS), np.eye(FAR), np.eye(zr))
-    rot = complex_rotation(c, direction * s).reshape(2, 2, NEAR, LO, COLS)
+    rot = complex_rotation(c, direction * s).reshape(2, 2, NEAR, LO, COLS // 2, 2)
     n = LINES * zr
     if direction < 0:
-        return np.einsum("pqrlc,abxwzy->pralxzwcbqy", rot, same).reshape(n, n)
-    return np.einsum("pqrlc,abxwzy->xcapzqrblwy", rot, same).reshape(n, n)
+        return np.einsum("pqrlcd,abxwzy->pralxzdwcbqy", rot, same).reshape(n, n)
+    return np.einsum("pqrlcd,abxwzy->dxcapzqrblwy", rot, same).reshape(n, n)
 
 
 def twiddles(zr, lanes):
@@ -119,7 +118,7 @@
     q = np.arange(KZ) - KZ // 2
     c, s = roots(q[:, None] * np.arange(NZ)[None, :], NZ)
     rot = complex_rotation(c, direction * s).reshape(2, 2, KZ, FAR, NEAR, 2)
-    same = np.eye(BATCH)
+    same = np.eye(LO)
     if direction < 0:
         form = "pkmxsz,ab->pmazsbxk" if z_major else "pkmxsz,ab->pmasbxzk"
         out = np.einsum(form, rot, same).reshape(2 * MODES, -1)
@@ -142,18 +141,16 @@
 
 
 def wave_table():
-    a = np.arange(AS).reshape(1, AS, 1, 1, 1)
-    lo = np.arange(LO).reshape(1, 1, LO, 1, 1)
-    m = np.arange(KZ).reshape(KZ, 1, 1, 1, 1)
-    q = np.arange(QP).reshape(1, 1, 1, 1, QP)
-    full = (KZ, AS, LO, 8, QP)
+    lo = np.arange(LO).reshape(1, LO, 1, 1)
+    m = np.arange(KZ).reshape(KZ, 1, 1, 1)
+    q = np.arange(QP).reshape(1, 1, 1, QP)
+    full = (KZ, LO, 8, QP)
     return np.stack(
         [
-            np.broadcast_to(a, full),
             np.broadcast_to(32 * (q - QS // 2) + lo, full),
             np.broadcast_to((m - KZ // 2) * (NX // NZ), full),
         ]
-    ).reshape(3 * MODES, 128)
+    ).reshape(2 * MODES, 128)
 
 
 def dot(lhs, rhs):
@@ -193,13 +190,15 @@
     x = jnp.concatenate(
         [flat_rows(phase_ref)] + [flat_rows(vel_ref, j) for j in range(3)], axis=0
     )
-    table = table_ref[...]
-    out_ref[...] = to_bf16(dot_nt(table, to_bf16(x)))
-    for z in range(2):
-        phase = phase_ref[:, z, :]
-        bulk = to_bf16(phase * phase * phase - phase)
-        padded = jnp.concatenate([jnp.zeros((7 * YL, NX), jnp.bfloat16), bulk], axis=0)
-        wide[pl.ds(z, LINES, stride=2), :] = dot_nt(table, padded)
+    phases = [phase_ref[:, z, :] for z in range(2)]
+    bulk = [to_bf16(p * p * p - p) for p in phases]
+    x = jnp.concatenate(
+        [to_bf16(x), jnp.zeros((6 * YL, NX), jnp.bfloat16), bulk[1], bulk[0]], axis=0
+    )
+    lines = dot_nt(table_ref[...], x)
+    out_ref[...] = to_bf16(lines[:, :128])
+    wide[pl.ds(0, LINES, stride=2), :] = lines[:, 128:]
+    wide[pl.ds(1, LINES, stride=2), :] = pltpu.roll(lines[:, 128:], YL, 1)
     bulk_ref[...] = to_bf16(wide[...])
 
 
@@ -257,76 +256,107 @@
     )
 
 
-def wave_numbers(wave_ref):
-    kx = wave_ref[0:MODES] + (
-        (lax.axis_index("far") * COLS + lax.axis_index("col")) * AS
-    ).astype(jnp.float32)
-    ky = wave_ref[MODES : 2 * MODES] + (lax.axis_index("near") * LO).astype(jnp.float32)
-    kz = wave_ref[2 * MODES : 3 * MODES]
+def first_wave():
+    owner = (lax.axis_index("xl") * FAR + lax.axis_index("far")) * (COLS // 2)
+    return ((owner + lax.axis_index("z")) * AS).astype(jnp.float32)
+
+
+def cross_waves(wave_ref):
+    ky = wave_ref[0:MODES] + (lax.axis_index("near") * LO).astype(jnp.float32)
+    kz = wave_ref[MODES : 2 * MODES]
     slot = lax.broadcasted_iota(jnp.int32, (MODES, 128), 1) // QP
-    return kx, ky, kz, kx * kx + ky * ky + kz * kz, slot
+    return ky, kz, slot
+
+
+def rows_of(ref, a):
+    block = ref.shape[0] // NEAR
+    part = block // AS
+    return jnp.concatenate(
+        [ref[pl.ds(r * block + a * part, part), :] for r in range(NEAR)], axis=0
+    )
+
+
+def put_rows(ref, a, values):
+    block = ref.shape[0] // NEAR
+    part = block // AS
+    for r in range(NEAR):
+        ref[pl.ds(r * block + a * part, part), :] = values[r * part : (r + 1) * part]
 
 
 def derive_kernel(
     in_ref, spread_ref, left_ref, wave_ref, back_ref, out_ref, spectra_ref
 ):
-    spread = to_bf16(dot(in_ref[...], spread_ref[...]))
-    modes = dot(left_ref[...], jnp.concatenate([spread[:, :256], spread[:, 256:]], axis=0))
-    spectra_ref[...] = modes[:, 128:]
-    kx, ky, kz, k2, slot = wave_numbers(wave_ref)
-    one = jnp.where(
-        (slot == 0) | (slot == 6),
-        kx,
-        jnp.where(
-            (slot == 1) | (slot == 4),
-            ky,
-            jnp.where((slot == 2) | (slot == 5), kz, jnp.where(slot == 3, -k2, 0.0)),
-        ),
-    )
-    two = jnp.where(
-        slot == 4, kz, jnp.where(slot == 5, kx, jnp.where(slot == 6, ky, 0.0))
-    )
-    re = modes[:MODES, :128] * one - modes[:MODES, 128:] * two
-    im = modes[MODES:, :128] * one - modes[MODES:, 128:] * two
+    ky, kz, slot = cross_waves(wave_ref)
+    across = ky * ky + kz * kz
     plain = slot == 3
-    coeff = jnp.concatenate(
-        [to_bf16(jnp.where(plain, re, -im)), to_bf16(jnp.where(plain, im, re))], axis=0
-    )
-    out_ref[...] = to_bf16(dot(back_ref[...], coeff))
+    for a in range(AS):
+        spread = to_bf16(dot(rows_of(in_ref, a), spread_ref[...]))
+        modes = dot(
+            left_ref[...], jnp.concatenate([spread[:, :256], spread[:, 256:]], axis=0)
+        )
+        spectra_ref[pl.ds(2 * MODES * a, 2 * MODES), :] = modes[:, 128:]
+        kx = first_wave() + float(a)
+        one = jnp.where(
+            (slot == 0) | (slot == 6),
+            kx,
+            jnp.where(
+                (slot == 1) | (slot == 4),
+                ky,
+                jnp.where(
+                    (slot == 2) | (slot == 5),
+                    kz,
+                    jnp.where(plain, -(across + kx * kx), 0.0),
+                ),
+            ),
+        )
+        two = jnp.where(
+            slot == 4, kz, jnp.where(slot == 5, kx, jnp.where(slot == 6, ky, 0.0))
+        )
+        re = modes[:MODES, :128] * one - modes[:MODES, 128:] * two
+        im = modes[MODES:, :128] * one - modes[MODES:, 128:] * two
+        coeff = jnp.concatenate(
+            [to_bf16(jnp.where(plain, re, -im)), to_bf16(jnp.where(plain, im, re))],
+            axis=0,
+        )
+        put_rows(out_ref, a, to_bf16(dot(back_ref[...], coeff)))
 
 
 def solve_kernel(in_ref, spectra_ref, left_ref, wave_ref, back_ref, out_ref):
-    modes = dot(left_ref[...], in_ref[...])
-    kx, ky, kz, k2, slot = wave_numbers(wave_ref)
+    ky, kz, slot = cross_waves(wave_ref)
+    across = ky * ky + kz * kz
     scalar = slot == 0
-    stable = 1.0 / time_step + mobility * stabilizer * k2
-    below = jnp.where(
-        scalar,
-        stable + mobility * epsilon * epsilon * k2 * k2,
-        1.0 / time_step + k2 / reynolds,
-    )
     used = slot < 4
-    inv = jnp.where(used, 1.0 / below, 0.0)
-    keep = jnp.where(scalar, stable, 1.0 / time_step)
-    mean = scalar & (k2 == 0.0)
-    sign = jnp.where(mean, 0.0, jnp.where(scalar, -1.0, 1.0))
-    bulk = jnp.where(scalar, mobility * k2, 0.0)
-    wave = jnp.where(
-        slot == 1, kx, jnp.where(slot == 2, ky, jnp.where(slot == 3, kz, 0.0))
-    )
-    shared = wave / jnp.maximum(k2, 1.0)
-    parts = []
-    for p in range(2):
-        now = modes[p * MODES : (p + 1) * MODES]
-        old = spectra_ref[p * MODES : (p + 1) * MODES]
-        fresh = (keep * old + sign * now - bulk * pltpu.roll(now, 64, 1)) * inv
-        normal = wave * fresh
-        for step in (16, 32, 64):
-            normal = normal + pltpu.roll(normal, step, 1)
-        parts.append(to_bf16(fresh - shared * normal))
-    both = dot(back_ref[...], jnp.concatenate(parts, axis=0))
-    half = both.shape[0] // 2
-    out_ref[...] = to_bf16(both[:half] + pltpu.roll(both[half:], 64, 1))
+    for a in range(AS):
+        modes = dot(left_ref[...], rows_of(in_ref, a))
+        kx = first_wave() + float(a)
+        k2 = across + kx * kx
+        stable = 1.0 / time_step + mobility * stabilizer * k2
+        below = jnp.where(
+            scalar,
+            stable + mobility * epsilon * epsilon * k2 * k2,
+            1.0 / time_step + k2 / reynolds,
+        )
+        inv = jnp.where(used, 1.0 / below, 0.0)
+        keep = jnp.where(scalar, stable, 1.0 / time_step)
+        mean = scalar & (k2 == 0.0)
+        sign = jnp.where(mean, 0.0, jnp.where(scalar, -1.0, 1.0))
+        bulk = jnp.where(scalar, mobility * k2, 0.0)
+        wave = jnp.where(
+            slot == 1, kx, jnp.where(slot == 2, ky, jnp.where(slot == 3, kz, 0.0))
+        )
+        shared = wave / jnp.maximum(k2, 1.0)
+        parts = []
+        for p in range(2):
+            now = modes[p * MODES : (p + 1) * MODES]
+            old = spectra_ref[pl.ds((2 * a + p) * MODES, MODES), :]
+            fresh = (keep * old + sign * now - bulk * pltpu.roll(now, 64, 1)) * inv
+            normal = wave * fresh
+            for step in (16, 32, 64):
+                normal = normal + pltpu.roll(normal, step, 1)
+            parts.append(to_bf16(fresh - shared * normal))
+        both = dot(back_ref[...], jnp.concatenate(parts, axis=0))
+        half = both.shape[0] // 2
+        put_rows(out_ref, a, to_bf16(both[:half] + pltpu.roll(both[half:], 64, 1)))
 
 
 def nonlinear_kernel(
@@ -425,7 +455,7 @@
         as_bf16(right_y_table(1, -1)),
     )[0]
     planes, spectra = call(
-        derive_kernel, [buffer(2 * LINES), buffer(2 * MODES, f32)], [],
+        derive_kernel, [buffer(2 * LINES), buffer(2 * MODES * AS, f32)], [],
         exchange(planes, "near"), as_bf16(spread_table()),
         as_bf16(left_z_table(-1, True)), waves, as_bf16(left_z_table(1, False)),
     )
@@ -467,11 +497,11 @@
 
 def solution(mesh):
     finer = Mesh(
-        mesh.devices.reshape(FAR, NEAR, mesh.shape["col"]), ("far", "near", "col")
-    )
-    row = ("far", "near")
-    in_specs = (P("col", row, None), P(None, "col", row, None))
-    out_specs = (P("col", row, None), P(None, "col", row, None))
+        mesh.devices.reshape(FAR, NEAR, COLS // 2, 2), ("far", "near", "z", "xl")
+    )
+    row, col = ("far", "near"), ("z", "xl")
+    in_specs = (P(col, row, None), P(None, col, row, None))
+    out_specs = (P(col, row, None), P(None, col, row, None))
     return jax.shard_map(
         on_device, mesh=finer, in_specs=in_specs, out_specs=out_specs, check_vma=False
     )

time: 145 us -> 143 us (0.986)
  no operation moved by 1% of the time
where the time goes in v3:
time: 143 us
  blocking collectives  134 us (94%)
  Pallas kernels  7.94 us (6%)
    all_to_all x8, blocking collectives, exchange(): lax.all_to_all(values.reshape(rows // 2, 2, 128), axis, split_axis=0, con...  134 us
    pallas_call x9, Pallas kernels, call(): pl.pallas_call(kernel, in_specs=specs, out_specs=[vmem] * len(outs), out_...  7.94 us

profile of v3, /device:TPU:2, one launch (start us, length us, event | category | flops | bytes accessed | tf_op | source)
XLA Modules:
  0.0 143.1 jit_solution(10528866758505950192)
XLA Ops:
  0.6 0.0 copy-start.7
  0.6 0.0 copy-start.15
  0.7 0.0 copy-start.16
  0.7 0.0 copy-start.17
  0.7 1.7 %shard_map.257 = (bf16[384,128]{1,0:T(8,128)(2,1)S(1)}, bf16[768,128]{1,0:T(8,128)(2,1)S(1)}) custom-call(f32[16,2,512]{2,1,0:T(2,128)} %phase_ref.1, f32[3,16,2,512]{3,2,1,0:T(2,128)} %vel_ref.1, bf16[384,512]{1,0:T(8,128)(2,1)} %constant.65.table_hbm.table_ref), custom_call_target="tpu_custom_call" | custom-call | flops 10000000000 | bytes 25000000 | tf_op jit(solution)/shard_map/pallas_call | solution.py:400
  2.4 33.6 %all_to_all.40 = bf16[192,2,128]{2,1,0:T(2,128)(2,1)S(1)} all-to-all(bf16[192,2,128]{2,1,0:T(2,128)(2,1)S(1)} %bitcast.29), channel_id=1, replica_groups=mesh['far'=2,'near'=8,'z'=16,'xl'=2] {'xl','far','z'}, dimensions={0} | all-to-all | bytes 196608 | tf_op jit(solution)/shard_map/all_to_all | solution.py:419
  35.9 0.0 copy-done.7
  35.9 0.0 copy-done.15
  35.9 0.0 copy-done.16
  35.9 0.0 copy-done.17
  35.9 0.0 copy-start.13
  36.0 0.0 copy-start.14
  36.0 0.0 copy-start.18
  36.0 0.0 copy-start.22
  36.0 0.4 shard_map.258
  36.4 10.1 %all_to_all.41 = bf16[192,2,128]{2,1,0:T(2,128)(2,1)S(1)} all-to-all(bf16[192,2,128]{2,1,0:T(2,128)(2,1)S(1)} %bitcast.31), channel_id=1, replica_groups=mesh['far'=2,'near'=8,'z'=16,'xl'=2] {'near'}, dimensions={0} | all-to-all | bytes 196608 | tf_op jit(solution)/shard_map/all_to_all | solution.py:419
  46.5 0.0 copy-done.13
  46.5 0.0 copy-done.14
  46.5 0.0 copy-done.18
  46.5 0.0 copy-done.22
  46.5 0.0 copy-start.2
  46.5 0.0 copy-start.8
  46.5 0.0 copy-start.9
  46.5 0.0 copy-start.12
  46.5 1.2 shard_map.259
  47.7 9.2 %all_to_all.42 = bf16[384,2,128]{2,1,0:T(2,128)(2,1)S(1)} all-to-all(bf16[384,2,128]{2,1,0:T(2,128)(2,1)S(1)} %bitcast.17), channel_id=1, replica_groups=mesh['far'=2,'near'=8,'z'=16,'xl'=2] {'near'}, dimensions={0} | all-to-all | bytes 393216 | tf_op jit(solution)/shard_map/all_to_all | solution.py:419
  56.9 0.0 copy-done.2
  56.9 0.0 copy-done.8
  56.9 0.0 copy-done.9
  56.9 0.0 copy-done.12
  56.9 0.0 copy-start
  57.0 0.0 copy-start.1
  57.0 0.0 copy-start.4
  57.0 0.0 copy-start.5
  57.0 0.7 shard_map.260
  57.7 23.4 %all_to_all.43 = bf16[384,2,128]{2,1,0:T(2,128)(2,1)S(1)} all-to-all(bf16[384,2,128]{2,1,0:T(2,128)(2,1)S(1)} %bitcast.18), channel_id=1, replica_groups=mesh['far'=2,'near'=8,'z'=16,'xl'=2] {'xl','far','z'}, dimensions={0} | all-to-all | bytes 393216 | tf_op jit(solution)/shard_map/all_to_all | solution.py:419
  81.1 0.0 copy-done
  81.1 0.0 copy-done.1
  81.1 0.0 copy-done.4
  81.1 0.0 copy-done.5
  81.1 0.0 copy-start.3
  81.1 0.0 copy-start.20
  81.1 0.0 copy-start.21
  81.2 0.6 shard_map.261
  81.8 20.6 %all_to_all.44 = bf16[192,2,128]{2,1,0:T(2,128)(2,1)S(1)} all-to-all(bf16[192,2,128]{2,1,0:T(2,128)(2,1)S(1)} %bitcast.27), channel_id=1, replica_groups=mesh['far'=2,'near'=8,'z'=16,'xl'=2] {'xl','far','z'}, dimensions={0} | all-to-all | bytes 196608 | tf_op jit(solution)/shard_map/all_to_all | solution.py:419
  102.4 0.0 copy-done.3
  102.4 0.0 copy-done.20
  102.4 0.0 copy-done.21
  102.4 0.0 copy-start.11
  102.4 0.0 copy-start.19
  102.4 0.6 shard_map.262
  103.1 9.2 %all_to_all.45 = bf16[384,2,128]{2,1,0:T(2,128)(2,1)S(1)} all-to-all(bf16[384,2,128]{2,1,0:T(2,128)(2,1)S(1)} %bitcast.19), channel_id=1, replica_groups=mesh['far'=2,'near'=8,'z'=16,'xl'=2] {'near'}, dimensions={0} | all-to-all | bytes 393216 | tf_op jit(solution)/shard_map/all_to_all | solution.py:419
  112.3 0.0 copy-done.11
  112.3 0.0 copy-done.19
  112.3 0.0 copy-start.6
  112.3 0.0 copy-start.10
  112.3 1.3 shard_map.263
  113.6 8.2 %all_to_all.46 = bf16[192,2,128]{2,1,0:T(2,128)(2,1)S(1)} all-to-all(bf16[192,2,128]{2,1,0:T(2,128)(2,1)S(1)} %bitcast.24), channel_id=1, replica_groups=mesh['far'=2,'near'=8,'z'=16,'xl'=2] {'near'}, dimensions={0} | all-to-all | bytes 196608 | tf_op jit(solution)/shard_map/all_to_all | solution.py:419
  121.7 0.0 copy-done.6
  121.7 0.0 copy-done.10
  121.8 0.4 shard_map.264
  122.2 19.9 %all_to_all.47 = bf16[192,2,128]{2,1,0:T(2,128)(2,1)S(1)} all-to-all(bf16[192,2,128]{2,1,0:T(2,128)(2,1)S(1)} %bitcast.26), channel_id=1, replica_groups=mesh['far'=2,'near'=8,'z'=16,'xl'=2] {'xl','far','z'}, dimensions={0} | all-to-all | bytes 196608 | tf_op jit(solution)/shard_map/all_to_all | solution.py:419
  142.1 1.0 shard_map.265
Async XLA Ops:
  0.6 35.3 %copy-start.7 = (bf16[384,384]{1,0:T(8,128)(2,1)S(1)}, bf16[384,384]{1,0:T(8,128)(2,1)}, u32[]{:S(2)}) copy-start(bf16[384,384]{1,0:T(8,128)(2,1)} %constant.66.left_ref) | copy-start | bytes 884740
  0.6 35.3 %copy-start.15 = (bf16[256,256]{1,0:T(8,128)(2,1)S(1)}, bf16[256,256]{1,0:T(8,128)(2,1)}, u32[]{:S(2)}) copy-start(bf16[256,256]{1,0:T(8,128)(2,1)} %constant.67.right_ref) | copy-start | bytes 393220
  0.7 35.3 %copy-start.16 = (f32[192,128]{1,0:T(8,128)S(1)}, f32[192,128]{1,0:T(8,128)}, u32[]{:S(2)}) copy-start(f32[192,128]{1,0:T(8,128)} %constant.47.clone.sin_ref) | copy-start | bytes 294916
  0.7 35.3 %copy-start.17 = (f32[192,128]{1,0:T(8,128)S(1)}, f32[192,128]{1,0:T(8,128)}, u32[]{:S(2)}) copy-start(f32[192,128]{1,0:T(8,128)} %constant.46.clone.cos_ref) | copy-start | bytes 294916
  35.9 10.5 %copy-start.13 = (bf16[256,192]{1,0:T(8,128)(2,1)S(1)}, bf16[256,192]{1,0:T(8,128)(2,1)}, u32[]{:S(2)}) copy-start(bf16[256,192]{1,0:T(8,128)(2,1)} %constant.70.back_ref) | copy-start | bytes 294916
  36.0 10.5 %copy-start.14 = (bf16[128,512]{1,0:T(8,128)(2,1)S(1)}, bf16[128,512]{1,0:T(8,128)(2,1)}, u32[]{:S(2)}) copy-start(bf16[128,512]{1,0:T(8,128)(2,1)} %constant.68.spread_ref) | copy-start | bytes 393220
  36.0 10.5 %copy-start.18 = (f32[192,128]{1,0:T(8,128)S(1)}, f32[192,128]{1,0:T(8,128)}, u32[]{:S(2)}) copy-start(f32[192,128]{1,0:T(8,128)} %constant.44.clone.wave_ref) | copy-start | bytes 294916
  36.0 10.5 %copy-start.22 = (bf16[192,256]{1,0:T(8,128)(2,1)S(1)}, bf16[192,256]{1,0:T(8,128)(2,1)}, u32[]{:S(2)}) copy-start(bf16[192,256]{1,0:T(8,128)(2,1)} %constant.69.left_ref) | copy-start | bytes 294916
  46.5 10.4 %copy-start.2 = (bf16[768,768]{1,0:T(8,128)(2,1)S(1)}, bf16[768,768]{1,0:T(8,128)(2,1)}, u32[]{:S(2)}) copy-start(bf16[768,768]{1,0:T(8,128)(2,1)} %constant.71.left_ref) | copy-start | bytes 3538948
  46.5 10.4 %copy-start.8 = (f32[384,128]{1,0:T(8,128)S(1)}, f32[384,128]{1,0:T(8,128)}, u32[]{:S(2)}) copy-start(f32[384,128]{1,0:T(8,128)} %constant.54.clone.sin_ref) | copy-start | bytes 589828
  46.5 10.4 %copy-start.9 = (f32[384,128]{1,0:T(8,128)S(1)}, f32[384,128]{1,0:T(8,128)}, u32[]{:S(2)}) copy-start(f32[384,128]{1,0:T(8,128)} %constant.53.clone.cos_ref) | copy-start | bytes 589828
  46.5 10.4 %copy-start.12 = (bf16[256,256]{1,0:T(8,128)(2,1)S(1)}, bf16[256,256]{1,0:T(8,128)(2,1)}, u32[]{:S(2)}) copy-start(bf16[256,256]{1,0:T(8,128)(2,1)} %constant.72.right_ref) | copy-start | bytes 393220
  56.9 24.2 %copy-start = (f32[3,16,2,512]{3,2,1,0:T(2,128)S(1)}, f32[3,16,2,512]{3,2,1,0:T(2,128)}, u32[]{:S(2)}) copy-start(f32[3,16,2,512]{3,2,1,0:T(2,128)} %vel_ref.1) | copy-start | bytes 589828
  57.0 24.2 %copy-start.1 = (f32[16,2,512]{2,1,0:T(2,128)S(1)}, f32[16,2,512]{2,1,0:T(2,128)}, u32[]{:S(2)}) copy-start(f32[16,2,512]{2,1,0:T(2,128)} %phase_ref.1) | copy-start | bytes 196612
  57.0 24.1 %copy-start.4 = (bf16[384,512]{1,0:T(8,128)(2,1)S(1)}, bf16[384,512]{1,0:T(8,128)(2,1)}, u32[]{:S(2)}) copy-start(bf16[384,512]{1,0:T(8,128)(2,1)} %constant.73.back_ref) | copy-start | bytes 1179652
  57.0 24.1 %copy-start.5 = (bf16[384,512]{1,0:T(8,128)(2,1)S(1)}, bf16[384,512]{1,0:T(8,128)(2,1)}, u32[]{:S(2)}) copy-start(bf16[384,512]{1,0:T(8,128)(2,1)} %constant.65.table_hbm.table_ref) | copy-start | bytes 1179652
  81.1 21.2 %copy-start.3 = (bf16[512,512]{1,0:T(8,128)(2,1)S(1)}, bf16[512,512]{1,0:T(8,128)(2,1)}, u32[]{:S(2)}) copy-start(bf16[512,512]{1,0:T(8,128)(2,1)} %constant.74.right_ref) | copy-start | bytes 1572868
  81.1 21.2 %copy-start.20 = (f32[192,128]{1,0:T(8,128)S(1)}, f32[192,128]{1,0:T(8,128)}, u32[]{:S(2)}) copy-start(f32[192,128]{1,0:T(8,128)} %constant.57.clone.sin_ref) | copy-start | bytes 294916
  81.1 21.2 %copy-start.21 = (f32[192,128]{1,0:T(8,128)S(1)}, f32[192,128]{1,0:T(8,128)}, u32[]{:S(2)}) copy-start(f32[192,128]{1,0:T(8,128)} %constant.56.clone.cos_ref) | copy-start | bytes 294916
  102.4 9.9 %copy-start.11 = (bf16[256,192]{1,0:T(8,128)(2,1)S(1)}, bf16[256,192]{1,0:T(8,128)(2,1)}, u32[]{:S(2)}) copy-start(bf16[256,192]{1,0:T(8,128)(2,1)} %constant.76.back_ref) | copy-start | bytes 294916
  102.4 9.9 %copy-start.19 = (bf16[192,256]{1,0:T(8,128)(2,1)S(1)}, bf16[192,256]{1,0:T(8,128)(2,1)}, u32[]{:S(2)}) copy-start(bf16[192,256]{1,0:T(8,128)(2,1)} %constant.75.left_ref) | copy-start | bytes 294916
  112.3 9.5 %copy-start.6 = (bf16[384,384]{1,0:T(8,128)(2,1)S(1)}, bf16[384,384]{1,0:T(8,128)(2,1)}, u32[]{:S(2)}) copy-start(bf16[384,384]{1,0:T(8,128)(2,1)} %constant.77.left_ref) | copy-start | bytes 884740
  112.3 9.5 %copy-start.10 = (bf16[256,256]{1,0:T(8,128)(2,1)S(1)}, bf16[256,256]{1,0:T(8,128)(2,1)}, u32[]{:S(2)}) copy-start(bf16[256,256]{1,0:T(8,128)(2,1)} %constant.78.right_ref) | copy-start | bytes 393220

commit v4 on v3

--- a/solution.py
+++ b/solution.py
@@ -69,15 +69,19 @@
     return np.einsum("pqrlcd,abxwzy->dxcapzqrblwy", rot, same).reshape(n, n)
 
 
-def twiddles(zr, lanes):
+def left_y_single_table():
+    k32 = np.arange(32)
+    c, s = roots(k32[:, None] * np.arange(COLS)[None, :], 32)
+    same = np.einsum("xw,zy->xwzy", np.eye(FAR), np.eye(2))
+    rot = complex_rotation(c, s).reshape(2, 2, NEAR, LO, COLS // 2, 2)
+    return np.einsum("pqrlcd,xwzy->pzdxcqrlwy", rot, same).reshape(256, 256)
+
+
+def twiddles(count, inner, lanes):
     k32 = np.arange(32).reshape(NEAR, 1, LO, 1, 1)
-    full = (NEAR, AS, LO, FAR * zr, 128)
+    full = (NEAR, count, LO, inner, 128)
     c, s = roots(np.broadcast_to(k32 * lanes.reshape(1, 1, 1, 1, 128), full), 512)
     return c.reshape(-1, 128), s.reshape(-1, 128)
-
-
-def lanes_yz():
-    return np.broadcast_to(np.arange(YL)[None, :, None], (4, YL, 2)).reshape(-1)
 
 
 def lanes_y():
@@ -91,17 +95,9 @@
     return complex_rotation(c, direction * s)
 
 
-def right_y_table(zr, direction):
-    rot = short_rotation(direction)
-    eye = np.eye
-    if zr == 1:
-        if direction < 0:
-            out = np.einsum("pkqy,fg,zw->kfyzpwgq", rot, eye(4), eye(2))
-        else:
-            out = np.einsum("pkqy,fg,zw->kzfqpgyw", rot, eye(4), eye(2))
-    else:
-        out = np.einsum("pkqy,fg->kfqpgy", rot, eye(8))
-    return out.reshape(256, 256)
+def right_y_table(direction):
+    form = "pkqy,fg->kfypgq" if direction < 0 else "pkqy,fg->kfqpgy"
+    return np.einsum(form, short_rotation(direction), np.eye(8)).reshape(256, 256)
 
 
 def right_merge_table():
@@ -169,8 +165,32 @@
     return values.astype(jnp.bfloat16)
 
 
-def flat_rows(ref, *lead):
-    return ref[lead].reshape(2 * YL, NX) if lead else ref[...].reshape(2 * YL, NX)
+TILES = NX // 128
+
+
+def tiled(values):
+    lead = values.shape[:-3]
+    split = values.reshape(*lead, YL, 2, TILES, 128)
+    return jnp.swapaxes(split, -3, -2).reshape(*lead, YL * TILES * 2, 128)
+
+
+def untiled(values):
+    lead = values.shape[:-2]
+    split = values.reshape(*lead, YL, TILES, 2, 128)
+    return jnp.swapaxes(split, -3, -2).reshape(*lead, YL, 2, NX)
+
+
+def plane(ref, z, *lead):
+    return jnp.concatenate(
+        [ref[(*lead, pl.ds(2 * t + z, YL, stride=2 * TILES))] for t in range(TILES)], axis=1
+    )
+
+
+def put_plane(ref, z, values, *lead):
+    for t in range(TILES):
+        ref[(*lead, pl.ds(2 * t + z, YL, stride=2 * TILES))] = values[
+            :, 128 * t : 128 * (t + 1)
+        ]
 
 
 def x_forward_kernel(
@@ -185,16 +205,16 @@
     ]
     for c in copies:
         c.start()
-    for c in copies:
+    for c in copies[:2]:
         c.wait()
-    x = jnp.concatenate(
-        [flat_rows(phase_ref)] + [flat_rows(vel_ref, j) for j in range(3)], axis=0
-    )
-    phases = [phase_ref[:, z, :] for z in range(2)]
-    bulk = [to_bf16(p * p * p - p) for p in phases]
-    x = jnp.concatenate(
-        [to_bf16(x), jnp.zeros((6 * YL, NX), jnp.bfloat16), bulk[1], bulk[0]], axis=0
-    )
+    phases = [plane(phase_ref, z) for z in range(2)]
+    rows = []
+    for z in range(2):
+        rows += [phases[z]] + [plane(vel_ref, z, j) for j in range(3)]
+    bulk = [p * p * p - p for p in phases]
+    rows += [jnp.zeros((6 * YL, NX), jnp.float32), bulk[1], bulk[0]]
+    x = jnp.concatenate([to_bf16(r) for r in rows], axis=0)
+    copies[2].wait()
     lines = dot_nt(table_ref[...], x)
     out_ref[...] = to_bf16(lines[:, :128])
     wide[pl.ds(0, LINES, stride=2), :] = lines[:, 128:]
@@ -229,30 +249,43 @@
     out_ref[...] = to_bf16(wide[...])
 
 
-def y_inverse(in_ref, left_ref, cos_ref, sin_ref, right_ref, wide):
+def y_inverse_kernel(in_ref, left_ref, cos_ref, sin_ref, right_ref, out_ref, wide):
     half = in_ref.shape[0] // 2
     wide[...] = in_ref[...].astype(jnp.float32)
     modes = jnp.concatenate(
         [to_bf16(wide[pl.ds(p, half, stride=2), :]) for p in range(2)], axis=1
     )
-    lines = dot(modes, right_ref[...])
+    spun = unspun(dot(modes, right_ref[...]), cos_ref[...], sin_ref[...])
+    out_ref[...] = to_bf16(dot(left_ref[...], spun))
+
+
+def unspun(lines, c, s):
     re, im = lines[:, :128], lines[:, 128:]
+    return jnp.concatenate([to_bf16(re * c - im * s), to_bf16(re * s + im * c)], axis=0)
+
+
+def y_inverse_rider_kernel(
+    in_ref, rider_ref, left_ref, cos_ref, sin_ref, right_ref, out_ref, wide, lines
+):
+    block = 2 * LINES // AS
+    half = block // 2
+    for a in range(AS):
+        wide[pl.ds(a * block, block), :] = rows_of(in_ref, a).astype(jnp.float32)
+    modes = jnp.concatenate(
+        [to_bf16(wide[pl.ds(p, AS * half, stride=2), :]) for p in range(2)], axis=1
+    )
+    turned = dot(modes, right_ref[...])
     c, s = cos_ref[...], sin_ref[...]
-    spun = jnp.concatenate([to_bf16(re * c - im * s), to_bf16(re * s + im * c)], axis=0)
-    return dot(left_ref[...], spun)
-
-
-def y_inverse_kernel(in_ref, left_ref, cos_ref, sin_ref, right_ref, out_ref, wide):
-    out_ref[...] = to_bf16(y_inverse(in_ref, left_ref, cos_ref, sin_ref, right_ref, wide))
-
-
-def y_inverse_rider_kernel(
-    in_ref, rider_ref, left_ref, cos_ref, sin_ref, right_ref, out_ref, wide
-):
-    lines = y_inverse(in_ref, left_ref, cos_ref, sin_ref, right_ref, wide)
-    lane = lax.broadcasted_iota(jnp.int32, lines.shape, 1)
+    spun = [unspun(turned[a * half : (a + 1) * half], c, s) for a in range(AS)]
+    every = dot(left_ref[...], jnp.concatenate(spun, axis=1))
+    for a in range(AS):
+        for j in range(4):
+            lines[pl.ds(4 * a + j, 64, stride=4 * AS), :] = every[
+                64 * j : 64 * (j + 1), 128 * a : 128 * (a + 1)
+            ]
+    lane = lax.broadcasted_iota(jnp.int32, (2 * LINES, 128), 1)
     out_ref[...] = to_bf16(
-        jnp.where(lane < 7 * YL, lines, rider_ref[...].astype(jnp.float32))
+        jnp.where(lane < 7 * YL, lines[...], rider_ref[...].astype(jnp.float32))
     )
 
 
@@ -289,11 +322,17 @@
     ky, kz, slot = cross_waves(wave_ref)
     across = ky * ky + kz * kz
     plain = slot == 3
-    for a in range(AS):
-        spread = to_bf16(dot(rows_of(in_ref, a), spread_ref[...]))
-        modes = dot(
-            left_ref[...], jnp.concatenate([spread[:, :256], spread[:, 256:]], axis=0)
-        )
+    rows = jnp.concatenate([rows_of(in_ref, a) for a in range(AS)], axis=0)
+    spreads = to_bf16(dot(rows, spread_ref[...]))
+    part = rows.shape[0] // AS
+    stacks = [
+        jnp.concatenate([w[:, :256], w[:, 256:]], axis=0)
+        for w in (spreads[part * a : part * (a + 1)] for a in range(AS))
+    ]
+    left = left_ref[...]
+    many = [dot(left, stack) for stack in stacks]
+    coeffs = []
+    for a, modes in enumerate(many):
         spectra_ref[pl.ds(2 * MODES * a, 2 * MODES), :] = modes[:, 128:]
         kx = first_wave() + float(a)
         one = jnp.where(
@@ -314,11 +353,15 @@
         )
         re = modes[:MODES, :128] * one - modes[:MODES, 128:] * two
         im = modes[MODES:, :128] * one - modes[MODES:, 128:] * two
-        coeff = jnp.concatenate(
-            [to_bf16(jnp.where(plain, re, -im)), to_bf16(jnp.where(plain, im, re))],
-            axis=0,
-        )
-        put_rows(out_ref, a, to_bf16(dot(back_ref[...], coeff)))
+        coeffs.append(
+            jnp.concatenate(
+                [to_bf16(jnp.where(plain, re, -im)), to_bf16(jnp.where(plain, im, re))],
+                axis=0,
+            )
+        )
+    back = dot(back_ref[...], jnp.concatenate(coeffs, axis=1))
+    for a in range(AS):
+        put_rows(out_ref, a, to_bf16(back[:, 128 * a : 128 * (a + 1)]))
 
 
 def solve_kernel(in_ref, spectra_ref, left_ref, wave_ref, back_ref, out_ref):
@@ -326,8 +369,12 @@
     across = ky * ky + kz * kz
     scalar = slot == 0
     used = slot < 4
+    many = dot(
+        left_ref[...], jnp.concatenate([rows_of(in_ref, a) for a in range(AS)], axis=1)
+    )
+    coeffs = []
     for a in range(AS):
-        modes = dot(left_ref[...], rows_of(in_ref, a))
+        modes = many[:, 128 * a : 128 * (a + 1)]
         kx = first_wave() + float(a)
         k2 = across + kx * kx
         stable = 1.0 / time_step + mobility * stabilizer * k2
@@ -354,8 +401,11 @@
             for step in (16, 32, 64):
                 normal = normal + pltpu.roll(normal, step, 1)
             parts.append(to_bf16(fresh - shared * normal))
-        both = dot(back_ref[...], jnp.concatenate(parts, axis=0))
-        half = both.shape[0] // 2
+        coeffs.append(jnp.concatenate(parts, axis=0))
+    back = dot(back_ref[...], jnp.concatenate(coeffs, axis=1))
+    half = back.shape[0] // 2
+    for a in range(AS):
+        both = back[:, 128 * a : 128 * (a + 1)]
         put_rows(out_ref, a, to_bf16(both[:half] + pltpu.roll(both[half:], 64, 1)))
 
 
@@ -372,8 +422,8 @@
     for z in range(2):
         values = dot(to_bf16(sides[z].T), back_ref[...])
         d = [values[YL * f : YL * (f + 1)] for f in range(7)]
-        phase = phase_ref[:, z, :]
-        v = [vel_ref[j, :, z, :] for j in range(3)]
+        phase = plane(phase_ref, z)
+        v = [plane(vel_ref, z, j) for j in range(3)]
         g, lap, w = d[0:3], d[3], d[4:7]
         potential = phase * phase * phase - phase - epsilon * epsilon * lap
         terms += [
@@ -386,21 +436,27 @@
     out_ref[...] = to_bf16(dot_nt(table_ref[...], x))
 
 
-def x_inverse_kernel(in_ref, back_ref, phase_ref, vel_ref):
+def x_inverse_kernel(in_ref, back_ref, phase_hbm, vel_hbm, fields, sems):
     lines = to_bf16(in_ref[...].astype(jnp.float32).T)
     values = dot(lines, back_ref[...])
-    phase_ref[...] = values[0:32].reshape(YL, 2, NX)
-    for j in range(3):
-        vel_ref[j] = values[32 * (j + 1) : 32 * (j + 2)].reshape(YL, 2, NX)
-
-
-def call(kernel, outs, scratch, *args, space=pltpu.VMEM):
-    vmem = pl.BlockSpec(memory_space=pltpu.VMEM)
+    copies = []
+    for f in range(4):
+        for z in range(2):
+            row = YL * (4 * z + f)
+            put_plane(fields, z, values[row : row + YL], f)
+        target = phase_hbm if f == 0 else vel_hbm.at[f - 1]
+        copies.append(pltpu.make_async_copy(fields.at[f], target, sems.at[f]))
+        copies[-1].start()
+    for c in copies:
+        c.wait()
+
+
+def call(kernel, outs, scratch, *args, space=pltpu.VMEM, out_space=pltpu.VMEM):
     specs = [pl.BlockSpec(memory_space=space)] * len(args)
     return pl.pallas_call(
         kernel,
         in_specs=specs,
-        out_specs=[vmem] * len(outs),
+        out_specs=[pl.BlockSpec(memory_space=out_space)] * len(outs),
         out_shape=outs,
         scratch_shapes=scratch,
         compiler_params=pltpu.CompilerParams(vmem_limit_bytes=16 * 1024 * 1024),
@@ -423,13 +479,14 @@
 
 
 def on_device(phase, velocity):
+    phase, velocity = tiled(phase), tiled(velocity)
     f32 = jnp.float32
     x_table = as_bf16(x_forward_table())
     x_back = as_bf16(x_inverse_table())
     waves = jnp.asarray(wave_table(), f32)
 
-    def spin(zr, lanes):
-        return tuple(jnp.asarray(t, f32) for t in twiddles(zr, lanes))
+    def spin(count, inner):
+        return tuple(jnp.asarray(t, f32) for t in twiddles(count, inner, lanes_y()))
 
     def scratch(rows):
         return pltpu.VMEM((rows, 128), f32)
@@ -451,8 +508,8 @@
     )
     planes = call(
         y_forward_kernel, [buffer(LINES)], [scratch(LINES)],
-        exchange(lines, BIG), as_bf16(left_y_table(1, -1)), *spin(1, lanes_yz()),
-        as_bf16(right_y_table(1, -1)),
+        exchange(lines, BIG), as_bf16(left_y_table(1, -1)), *spin(AS, FAR),
+        as_bf16(right_y_table(-1)),
     )[0]
     planes, spectra = call(
         derive_kernel, [buffer(2 * LINES), buffer(2 * MODES * AS, f32)], [],
@@ -460,9 +517,9 @@
         as_bf16(left_z_table(-1, True)), waves, as_bf16(left_z_table(1, False)),
     )
     lines = call(
-        y_inverse_rider_kernel, [buffer(2 * LINES)], [scratch(2 * LINES)],
-        exchange(planes, "near"), rider, as_bf16(left_y_table(2, 1)), *spin(2, lanes_y()),
-        as_bf16(right_y_table(2, 1)),
+        y_inverse_rider_kernel, [buffer(2 * LINES)], [scratch(2 * LINES), scratch(2 * LINES)],
+        exchange(planes, "near"), rider, as_bf16(left_y_single_table()), *spin(1, 2 * FAR),
+        as_bf16(right_y_table(1)),
     )[0]
     lines, bulk = call(
         nonlinear_kernel, [buffer(LINES), buffer(LINES)], [scratch(2 * LINES)],
@@ -470,7 +527,7 @@
     )
     planes = call(
         y_merge_kernel, [buffer(2 * LINES)], [scratch(2 * LINES)],
-        exchange(lines, BIG), bulk, as_bf16(left_y_table(1, -1)), *spin(1, lanes_y()),
+        exchange(lines, BIG), bulk, as_bf16(left_y_table(1, -1)), *spin(AS, FAR),
         as_bf16(right_merge_table()),
     )[0]
     planes = call(
@@ -480,19 +537,21 @@
     )[0]
     lines = call(
         y_inverse_kernel, [buffer(LINES)], [scratch(LINES)],
-        exchange(planes, "near"), as_bf16(left_y_table(1, 1)), *spin(1, lanes_yz()),
-        as_bf16(right_y_table(1, 1)),
+        exchange(planes, "near"), as_bf16(left_y_table(1, 1)), *spin(AS, FAR),
+        as_bf16(right_y_table(1)),
     )[0]
-    return tuple(
+    done = tuple(
         call(
             x_inverse_kernel,
             [
                 jax.ShapeDtypeStruct(phase.shape, f32),
                 jax.ShapeDtypeStruct(velocity.shape, f32),
             ],
-            [], exchange(lines, BIG), x_back,
-        )
-    )
+            [pltpu.VMEM((4, *phase.shape), f32), pltpu.SemaphoreType.DMA((4,))],
+            exchange(lines, BIG), x_back, out_space=pltpu.HBM,
+        )
+    )
+    return tuple(untiled(v) for v in done)
 
 
 def solution(mesh):

time: 143 us -> 143 us (level)
  no operation moved by 1% of the time
where the time goes in v4:
time: 143 us; the launch traced here: 142 us
  blocking collectives  135 us (94%)
  Pallas kernels  6.67 us (5%)
    all_to_all x8, blocking collectives, exchange(): lax.all_to_all(values.reshape(rows // 2, 2, 128), axis, split_axis=0, con...  135 us
    pallas_call x9, Pallas kernels, call(): pl.pallas_call(kernel, in_specs=specs, out_specs=[pl.BlockSpec(memory_spa...  6.67 us

profile of v4, /device:TPU:2, one launch (start us, length us, event | category | flops | bytes accessed | tf_op | source)
XLA Modules:
  0.0 142.4 jit_solution(16578414718146284767)
XLA Ops:
  0.6 0.0 copy-start.6
  0.6 0.0 copy-start.13
  0.7 0.0 copy-start.14
  0.7 1.6 %shard_map.257 = (bf16[384,128]{1,0:T(8,128)(2,1)S(1)}, bf16[768,128]{1,0:T(8,128)(2,1)S(1)}) custom-call(f32[128,128]{1,0:T(8,128)} %bitcast.54, f32[3,128,128]{2,1,0:T(8,128)} %bitcast.52, bf16[384,512]{1,0:T(8,128)(2,1)} %constant.56.table_hbm.table_ref), custom_call_target="tpu_custom_call" | custom-call | flops 10000000000 | bytes 25000000 | tf_op jit(solution)/shard_map/pallas_call | solution.py:456
  2.3 0.0 copy-start.12
  2.3 33.7 %all_to_all.40 = bf16[192,2,128]{2,1,0:T(2,128)(2,1)S(1)} all-to-all(bf16[192,2,128]{2,1,0:T(2,128)(2,1)S(1)} %bitcast.49), channel_id=1, replica_groups=mesh['far'=2,'near'=8,'z'=16,'xl'=2] {'xl','far','z'}, dimensions={0} | all-to-all | bytes 196608 | tf_op jit(solution)/shard_map/all_to_all | solution.py:475
  36.0 0.0 copy-done.6
  36.0 0.0 copy-done.13
  36.0 0.0 copy-done.14
  36.0 0.0 copy-done.12
  36.0 0.0 copy-start.11
  36.0 0.0 copy-start.15
  36.0 0.0 copy-start.17
  36.0 0.4 shard_map.258
  36.4 0.0 copy-start.10
  36.5 10.2 %all_to_all.41 = bf16[192,2,128]{2,1,0:T(2,128)(2,1)S(1)} all-to-all(bf16[192,2,128]{2,1,0:T(2,128)(2,1)S(1)} %bitcast.51), channel_id=1, replica_groups=mesh['far'=2,'near'=8,'z'=16,'xl'=2] {'near'}, dimensions={0} | all-to-all | bytes 196608 | tf_op jit(solution)/shard_map/all_to_all | solution.py:475
  46.7 0.0 copy-done.11
  46.7 0.0 copy-done.15
  46.7 0.0 copy-done.17
  46.7 0.0 copy-done.10
  46.7 0.7 shard_map.259
  47.3 0.0 copy-start.7
  47.4 0.0 copy-start.9
  47.4 0.0 copy-start.18
  47.4 0.0 copy-start.19
  47.4 9.3 %all_to_all.42 = bf16[384,2,128]{2,1,0:T(2,128)(2,1)S(1)} all-to-all(bf16[384,2,128]{2,1,0:T(2,128)(2,1)S(1)} %bitcast.36), channel_id=1, replica_groups=mesh['far'=2,'near'=8,'z'=16,'xl'=2] {'near'}, dimensions={0} | all-to-all | bytes 393216 | tf_op jit(solution)/shard_map/all_to_all | solution.py:475
  56.7 0.0 copy-done.7
  56.7 0.0 copy-done.9
  56.7 0.0 copy-done.18
  56.7 0.0 copy-done.19
  56.8 0.0 copy-start.3
  56.8 0.0 copy-start.4
  56.8 0.5 shard_map.260
  57.3 0.0 copy-start
  57.3 0.0 copy-start.1
  57.3 23.5 %all_to_all.43 = bf16[384,2,128]{2,1,0:T(2,128)(2,1)S(1)} all-to-all(bf16[384,2,128]{2,1,0:T(2,128)(2,1)S(1)} %bitcast.39), channel_id=1, replica_groups=mesh['far'=2,'near'=8,'z'=16,'xl'=2] {'xl','far','z'}, dimensions={0} | all-to-all | bytes 393216 | tf_op jit(solution)/shard_map/all_to_all | solution.py:475
  80.8 0.0 copy-done.3
  80.8 0.0 copy-done.4
  80.8 0.0 copy-done
  80.8 0.0 copy-done.1
  80.8 0.0 copy-start.2
  80.8 0.6 shard_map.261
  81.5 20.6 %all_to_all.44 = bf16[192,2,128]{2,1,0:T(2,128)(2,1)S(1)} all-to-all(bf16[192,2,128]{2,1,0:T(2,128)(2,1)S(1)} %bitcast.47), channel_id=1, replica_groups=mesh['far'=2,'near'=8,'z'=16,'xl'=2] {'xl','far','z'}, dimensions={0} | all-to-all | bytes 196608 | tf_op jit(solution)/shard_map/all_to_all | solution.py:475
  102.0 0.0 copy-done.2
  102.0 0.6 shard_map.262
  102.7 0.0 copy-start.8
  102.7 0.0 copy-start.16
  102.7 9.3 %all_to_all.45 = bf16[384,2,128]{2,1,0:T(2,128)(2,1)S(1)} all-to-all(bf16[384,2,128]{2,1,0:T(2,128)(2,1)S(1)} %bitcast.41), channel_id=1, replica_groups=mesh['far'=2,'near'=8,'z'=16,'xl'=2] {'near'}, dimensions={0} | all-to-all | bytes 393216 | tf_op jit(solution)/shard_map/all_to_all | solution.py:475
  112.0 0.0 copy-done.8
  112.0 0.0 copy-done.16
  112.1 0.0 copy-start.5
  112.1 0.8 shard_map.263
  112.9 8.2 %all_to_all.46 = bf16[192,2,128]{2,1,0:T(2,128)(2,1)S(1)} all-to-all(bf16[192,2,128]{2,1,0:T(2,128)(2,1)S(1)} %bitcast.44), channel_id=1, replica_groups=mesh['far'=2,'near'=8,'z'=16,'xl'=2] {'near'}, dimensions={0} | all-to-all | bytes 196608 | tf_op jit(solution)/shard_map/all_to_all | solution.py:475
  121.1 0.0 copy-done.5
  121.1 0.4 shard_map.264
  121.5 19.9 %all_to_all.47 = bf16[192,2,128]{2,1,0:T(2,128)(2,1)S(1)} all-to-all(bf16[192,2,128]{2,1,0:T(2,128)(2,1)S(1)} %bitcast.46), channel_id=1, replica_groups=mesh['far'=2,'near'=8,'z'=16,'xl'=2] {'xl','far','z'}, dimensions={0} | all-to-all | bytes 196608 | tf_op jit(solution)/shard_map/all_to_all | solution.py:475
  141.4 1.0 shard_map.265
Async XLA Ops:
  0.6 35.4 %copy-start.6 = (bf16[384,384]{1,0:T(8,128)(2,1)S(1)}, bf16[384,384]{1,0:T(8,128)(2,1)}, u32[]{:S(2)}) copy-start(bf16[384,384]{1,0:T(8,128)(2,1)} %constant.57.left_ref) | copy-start | bytes 884740
  0.6 35.4 %copy-start.13 = (f32[192,128]{1,0:T(8,128)S(1)}, f32[192,128]{1,0:T(8,128)}, u32[]{:S(2)}) copy-start(f32[192,128]{1,0:T(8,128)} %constant.41.clone.sin_ref) | copy-start | bytes 294916
  0.7 35.3 %copy-start.14 = (f32[192,128]{1,0:T(8,128)S(1)}, f32[192,128]{1,0:T(8,128)}, u32[]{:S(2)}) copy-start(f32[192,128]{1,0:T(8,128)} %constant.40.clone.cos_ref) | copy-start | bytes 294916
  2.3 33.7 %copy-start.12 = (bf16[256,256]{1,0:T(8,128)(2,1)S(1)}, bf16[256,256]{1,0:T(8,128)(2,1)}, u32[]{:S(2)}) copy-start(bf16[256,256]{1,0:T(8,128)(2,1)} %constant.58.right_ref) | copy-start | bytes 393220
  36.0 10.7 %copy-start.11 = (bf16[128,512]{1,0:T(8,128)(2,1)S(1)}, bf16[128,512]{1,0:T(8,128)(2,1)}, u32[]{:S(2)}) copy-start(bf16[128,512]{1,0:T(8,128)(2,1)} %constant.59.spread_ref) | copy-start | bytes 393220
  36.0 10.7 %copy-start.15 = (f32[192,128]{1,0:T(8,128)S(1)}, f32[192,128]{1,0:T(8,128)}, u32[]{:S(2)}) copy-start(f32[192,128]{1,0:T(8,128)} %constant.38.clone.wave_ref) | copy-start | bytes 294916
  36.0 10.6 %copy-start.17 = (bf16[192,256]{1,0:T(8,128)(2,1)S(1)}, bf16[192,256]{1,0:T(8,128)(2,1)}, u32[]{:S(2)}) copy-start(bf16[192,256]{1,0:T(8,128)(2,1)} %constant.60.left_ref) | copy-start | bytes 294916
  36.4 10.2 %copy-start.10 = (bf16[256,192]{1,0:T(8,128)(2,1)S(1)}, bf16[256,192]{1,0:T(8,128)(2,1)}, u32[]{:S(2)}) copy-start(bf16[256,192]{1,0:T(8,128)(2,1)} %constant.61.back_ref) | copy-start | bytes 294916
  47.3 9.4 %copy-start.7 = (bf16[256,256]{1,0:T(8,128)(2,1)S(1)}, bf16[256,256]{1,0:T(8,128)(2,1)}, u32[]{:S(2)}) copy-start(bf16[256,256]{1,0:T(8,128)(2,1)} %constant.63.right_ref) | copy-start | bytes 393220
  47.4 9.4 %copy-start.9 = (bf16[256,256]{1,0:T(8,128)(2,1)S(1)}, bf16[256,256]{1,0:T(8,128)(2,1)}, u32[]{:S(2)}) copy-start(bf16[256,256]{1,0:T(8,128)(2,1)} %constant.62.left_ref) | copy-start | bytes 393220
  47.4 9.4 %copy-start.18 = (f32[128,128]{1,0:T(8,128)S(1)}, f32[128,128]{1,0:T(8,128)}, u32[]{:S(2)}) copy-start(f32[128,128]{1,0:T(8,128)} %constant.48.clone.sin_ref) | copy-start | bytes 196612
  47.4 9.4 %copy-start.19 = (f32[128,128]{1,0:T(8,128)S(1)}, f32[128,128]{1,0:T(8,128)}, u32[]{:S(2)}) copy-start(f32[128,128]{1,0:T(8,128)} %constant.47.clone.cos_ref) | copy-start | bytes 196612
  56.8 24.1 %copy-start.3 = (bf16[384,512]{1,0:T(8,128)(2,1)S(1)}, bf16[384,512]{1,0:T(8,128)(2,1)}, u32[]{:S(2)}) copy-start(bf16[384,512]{1,0:T(8,128)(2,1)} %constant.64.back_ref) | copy-start | bytes 1179652
  56.8 24.0 %copy-start.4 = (bf16[384,512]{1,0:T(8,128)(2,1)S(1)}, bf16[384,512]{1,0:T(8,128)(2,1)}, u32[]{:S(2)}) copy-start(bf16[384,512]{1,0:T(8,128)(2,1)} %constant.56.table_hbm.table_ref) | copy-start | bytes 1179652
  57.3 23.5 %copy-start = (f32[3,16,2,512]{3,2,1,0:T(2,128)S(1)}, f32[3,16,2,512]{3,2,1,0:T(2,128)}, u32[]{:S(2)}) copy-start(f32[3,16,2,512]{3,2,1,0:T(2,128)} %param.27) | copy-start | bytes 589828
  57.3 23.5 %copy-start.1 = (f32[16,2,512]{2,1,0:T(2,128)S(1)}, f32[16,2,512]{2,1,0:T(2,128)}, u32[]{:S(2)}) copy-start(f32[16,2,512]{2,1,0:T(2,128)} %param.26) | copy-start | bytes 196612
  80.8 21.2 %copy-start.2 = (bf16[512,512]{1,0:T(8,128)(2,1)S(1)}, bf16[512,512]{1,0:T(8,128)(2,1)}, u32[]{:S(2)}) copy-start(bf16[512,512]{1,0:T(8,128)(2,1)} %constant.65.right_ref) | copy-start | bytes 1572868
  102.7 9.4 %copy-start.8 = (bf16[256,192]{1,0:T(8,128)(2,1)S(1)}, bf16[256,192]{1,0:T(8,128)(2,1)}, u32[]{:S(2)}) copy-start(bf16[256,192]{1,0:T(8,128)(2,1)} %constant.67.back_ref) | copy-start | bytes 294916
  102.7 9.4 %copy-start.16 = (bf16[192,256]{1,0:T(8,128)(2,1)S(1)}, bf16[192,256]{1,0:T(8,128)(2,1)}, u32[]{:S(2)}) copy-start(bf16[192,256]{1,0:T(8,128)(2,1)} %constant.66.left_ref) | copy-start | bytes 294916
  112.1 9.0 %copy-start.5 = (bf16[384,384]{1,0:T(8,128)(2,1)S(1)}, bf16[384,384]{1,0:T(8,128)(2,1)}, u32[]{:S(2)}) copy-start(bf16[384,384]{1,0:T(8,128)(2,1)} %constant.68.left_ref) | copy-start | bytes 884740

commit v5 on v4

--- a/solution.py
+++ b/solution.py
@@ -163,6 +163,11 @@
 
 def to_bf16(values):
     return values.astype(jnp.bfloat16)
+
+
+def two_parts(values):
+    high = to_bf16(values)
+    return high, to_bf16(values - high.astype(jnp.float32))
 
 
 TILES = NX // 128
@@ -227,8 +232,8 @@
     sums = dot(left_ref[...], in_ref[...])
     re, im = sums[:half], sums[half:]
     c, s = cos_ref[...], sin_ref[...]
-    lines = jnp.concatenate([to_bf16(re * c + im * s), to_bf16(im * c - re * s)], axis=1)
-    modes = dot(lines, right_ref[...])
+    lines = two_parts(jnp.concatenate([re * c + im * s, im * c - re * s], axis=1))
+    modes = dot(lines[0], right_ref[...]) + dot(lines[1], right_ref[...])
     for p in range(2):
         wide[pl.ds(p, half, stride=2), :] = modes[:, 128 * p : 128 * (p + 1)]
     out_ref[...] = to_bf16(wide[...])
@@ -241,9 +246,10 @@
     res, ims = [], []
     for t in range(2):
         re, im = (sums[p * half : (p + 1) * half, 128 * t : 128 * (t + 1)] for p in range(2))
-        res.append(to_bf16(re * c + im * s))
-        ims.append(to_bf16(im * c - re * s))
-    modes = dot(jnp.concatenate(res + ims, axis=1), right_ref[...])
+        res.append(re * c + im * s)
+        ims.append(im * c - re * s)
+    lines = two_parts(jnp.concatenate(res + ims, axis=1))
+    modes = dot(lines[0], right_ref[...]) + dot(lines[1], right_ref[...])
     for t in range(4):
         wide[pl.ds(t, half, stride=4), :] = modes[:, 128 * t : 128 * (t + 1)]
     out_ref[...] = to_bf16(wide[...])
@@ -255,13 +261,13 @@
     modes = jnp.concatenate(
         [to_bf16(wide[pl.ds(p, half, stride=2), :]) for p in range(2)], axis=1
     )
-    spun = unspun(dot(modes, right_ref[...]), cos_ref[...], sin_ref[...])
-    out_ref[...] = to_bf16(dot(left_ref[...], spun))
+    spun = two_parts(unspun(dot(modes, right_ref[...]), cos_ref[...], sin_ref[...]))
+    out_ref[...] = to_bf16(dot(left_ref[...], spun[0]) + dot(left_ref[...], spun[1]))
 
 
 def unspun(lines, c, s):
     re, im = lines[:, :128], lines[:, 128:]
-    return jnp.concatenate([to_bf16(re * c - im * s), to_bf16(re * s + im * c)], axis=0)
+    return jnp.concatenate([re * c - im * s, re * s + im * c], axis=0)
 
 
 def y_inverse_rider_kernel(
@@ -277,7 +283,8 @@
     turned = dot(modes, right_ref[...])
     c, s = cos_ref[...], sin_ref[...]
     spun = [unspun(turned[a * half : (a + 1) * half], c, s) for a in range(AS)]
-    every = dot(left_ref[...], jnp.concatenate(spun, axis=1))
+    spun = two_parts(jnp.concatenate(spun, axis=1))
+    every = dot(left_ref[...], spun[0]) + dot(left_ref[...], spun[1])
     for a in range(AS):
         for j in range(4):
             lines[pl.ds(4 * a + j, 64, stride=4 * AS), :] = every[

time: 143 us -> 143 us (level)
  no operation moved by 1% of the time
where the time goes in v5:
time: 143 us
  blocking collectives  135 us (94%)
  Pallas kernels  7.08 us (5%)
    all_to_all x8, blocking collectives, exchange(): lax.all_to_all(values.reshape(rows // 2, 2, 128), axis, split_axis=0, con...  135 us
    pallas_call x9, Pallas kernels, call(): pl.pallas_call(kernel, in_specs=specs, out_specs=[pl.BlockSpec(memory_spa...  7.08 us

profile of v5, /device:TPU:2, one launch (start us, length us, event | category | flops | bytes accessed | tf_op | source)
XLA Modules:
  0.0 142.8 jit_solution(10009783921215908013)
XLA Ops:
  0.6 0.0 copy-start.6
  0.6 0.0 copy-start.13
  0.7 0.0 copy-start.14
  0.7 1.6 %shard_map.257 = (bf16[384,128]{1,0:T(8,128)(2,1)S(1)}, bf16[768,128]{1,0:T(8,128)(2,1)S(1)}) custom-call(f32[128,128]{1,0:T(8,128)} %bitcast.54, f32[3,128,128]{2,1,0:T(8,128)} %bitcast.52, bf16[384,512]{1,0:T(8,128)(2,1)} %constant.56.table_hbm.table_ref), custom_call_target="tpu_custom_call" | custom-call | flops 10000000000 | bytes 25000000 | tf_op jit(solution)/shard_map/pallas_call | solution.py:463
  2.3 0.0 copy-start.12
  2.3 33.7 %all_to_all.40 = bf16[192,2,128]{2,1,0:T(2,128)(2,1)S(1)} all-to-all(bf16[192,2,128]{2,1,0:T(2,128)(2,1)S(1)} %bitcast.49), channel_id=1, replica_groups=mesh['far'=2,'near'=8,'z'=16,'xl'=2] {'xl','far','z'}, dimensions={0} | all-to-all | bytes 196608 | tf_op jit(solution)/shard_map/all_to_all | solution.py:482
  36.0 0.0 copy-done.6
  36.0 0.0 copy-done.13
  36.0 0.0 copy-done.14
  36.0 0.0 copy-done.12
  36.0 0.0 copy-start.11
  36.0 0.0 copy-start.15
  36.0 0.0 copy-start.17
  36.0 0.5 shard_map.258
  36.6 0.0 copy-start.10
  36.6 10.2 %all_to_all.41 = bf16[192,2,128]{2,1,0:T(2,128)(2,1)S(1)} all-to-all(bf16[192,2,128]{2,1,0:T(2,128)(2,1)S(1)} %bitcast.51), channel_id=1, replica_groups=mesh['far'=2,'near'=8,'z'=16,'xl'=2] {'near'}, dimensions={0} | all-to-all | bytes 196608 | tf_op jit(solution)/shard_map/all_to_all | solution.py:482
  46.8 0.0 copy-done.11
  46.8 0.0 copy-done.15
  46.8 0.0 copy-done.17
  46.8 0.0 copy-done.10
  46.8 0.7 shard_map.259
  47.5 0.0 copy-start.7
  47.5 0.0 copy-start.9
  47.5 0.0 copy-start.18
  47.5 0.0 copy-start.19
  47.5 9.3 %all_to_all.42 = bf16[384,2,128]{2,1,0:T(2,128)(2,1)S(1)} all-to-all(bf16[384,2,128]{2,1,0:T(2,128)(2,1)S(1)} %bitcast.36), channel_id=1, replica_groups=mesh['far'=2,'near'=8,'z'=16,'xl'=2] {'near'}, dimensions={0} | all-to-all | bytes 393216 | tf_op jit(solution)/shard_map/all_to_all | solution.py:482
  56.8 0.0 copy-done.7
  56.8 0.0 copy-done.9
  56.8 0.0 copy-done.18
  56.9 0.0 copy-done.19
  56.9 0.0 copy-start.3
  56.9 0.0 copy-start.4
  56.9 0.6 shard_map.260
  57.5 0.0 copy-start
  57.5 0.0 copy-start.1
  57.5 23.5 %all_to_all.43 = bf16[384,2,128]{2,1,0:T(2,128)(2,1)S(1)} all-to-all(bf16[384,2,128]{2,1,0:T(2,128)(2,1)S(1)} %bitcast.39), channel_id=1, replica_groups=mesh['far'=2,'near'=8,'z'=16,'xl'=2] {'xl','far','z'}, dimensions={0} | all-to-all | bytes 393216 | tf_op jit(solution)/shard_map/all_to_all | solution.py:482
  81.0 0.0 copy-done.3
  81.0 0.0 copy-done.4
  81.0 0.0 copy-done
  81.0 0.0 copy-done.1
  81.0 0.0 copy-start.2
  81.0 0.6 shard_map.261
  81.7 20.6 %all_to_all.44 = bf16[192,2,128]{2,1,0:T(2,128)(2,1)S(1)} all-to-all(bf16[192,2,128]{2,1,0:T(2,128)(2,1)S(1)} %bitcast.47), channel_id=1, replica_groups=mesh['far'=2,'near'=8,'z'=16,'xl'=2] {'xl','far','z'}, dimensions={0} | all-to-all | bytes 196608 | tf_op jit(solution)/shard_map/all_to_all | solution.py:482
  102.2 0.0 copy-done.2
  102.2 0.8 shard_map.262
  103.0 0.0 copy-start.8
  103.0 0.0 copy-start.16
  103.0 9.3 %all_to_all.45 = bf16[384,2,128]{2,1,0:T(2,128)(2,1)S(1)} all-to-all(bf16[384,2,128]{2,1,0:T(2,128)(2,1)S(1)} %bitcast.41), channel_id=1, replica_groups=mesh['far'=2,'near'=8,'z'=16,'xl'=2] {'near'}, dimensions={0} | all-to-all | bytes 393216 | tf_op jit(solution)/shard_map/all_to_all | solution.py:482
  112.4 0.0 copy-done.8
  112.4 0.0 copy-done.16
  112.4 0.0 copy-start.5
  112.4 0.8 shard_map.263
  113.2 8.2 %all_to_all.46 = bf16[192,2,128]{2,1,0:T(2,128)(2,1)S(1)} all-to-all(bf16[192,2,128]{2,1,0:T(2,128)(2,1)S(1)} %bitcast.44), channel_id=1, replica_groups=mesh['far'=2,'near'=8,'z'=16,'xl'=2] {'near'}, dimensions={0} | all-to-all | bytes 196608 | tf_op jit(solution)/shard_map/all_to_all | solution.py:482
  121.4 0.0 copy-done.5
  121.4 0.5 shard_map.264
  121.9 19.9 %all_to_all.47 = bf16[192,2,128]{2,1,0:T(2,128)(2,1)S(1)} all-to-all(bf16[192,2,128]{2,1,0:T(2,128)(2,1)S(1)} %bitcast.46), channel_id=1, replica_groups=mesh['far'=2,'near'=8,'z'=16,'xl'=2] {'xl','far','z'}, dimensions={0} | all-to-all | bytes 196608 | tf_op jit(solution)/shard_map/all_to_all | solution.py:482
  141.9 1.0 shard_map.265
Async XLA Ops:
  0.6 35.4 %copy-start.6 = (bf16[384,384]{1,0:T(8,128)(2,1)S(1)}, bf16[384,384]{1,0:T(8,128)(2,1)}, u32[]{:S(2)}) copy-start(bf16[384,384]{1,0:T(8,128)(2,1)} %constant.57.left_ref) | copy-start | bytes 884740
  0.6 35.4 %copy-start.13 = (f32[192,128]{1,0:T(8,128)S(1)}, f32[192,128]{1,0:T(8,128)}, u32[]{:S(2)}) copy-start(f32[192,128]{1,0:T(8,128)} %constant.41.clone.sin_ref) | copy-start | bytes 294916
  0.7 35.3 %copy-start.14 = (f32[192,128]{1,0:T(8,128)S(1)}, f32[192,128]{1,0:T(8,128)}, u32[]{:S(2)}) copy-start(f32[192,128]{1,0:T(8,128)} %constant.40.clone.cos_ref) | copy-start | bytes 294916
  2.3 33.7 %copy-start.12 = (bf16[256,256]{1,0:T(8,128)(2,1)S(1)}, bf16[256,256]{1,0:T(8,128)(2,1)}, u32[]{:S(2)}) copy-start(bf16[256,256]{1,0:T(8,128)(2,1)} %constant.58.right_ref) | copy-start | bytes 393220
  36.0 10.8 %copy-start.11 = (bf16[128,512]{1,0:T(8,128)(2,1)S(1)}, bf16[128,512]{1,0:T(8,128)(2,1)}, u32[]{:S(2)}) copy-start(bf16[128,512]{1,0:T(8,128)(2,1)} %constant.59.spread_ref) | copy-start | bytes 393220
  36.0 10.8 %copy-start.15 = (f32[192,128]{1,0:T(8,128)S(1)}, f32[192,128]{1,0:T(8,128)}, u32[]{:S(2)}) copy-start(f32[192,128]{1,0:T(8,128)} %constant.38.clone.wave_ref) | copy-start | bytes 294916
  36.0 10.7 %copy-start.17 = (bf16[192,256]{1,0:T(8,128)(2,1)S(1)}, bf16[192,256]{1,0:T(8,128)(2,1)}, u32[]{:S(2)}) copy-start(bf16[192,256]{1,0:T(8,128)(2,1)} %constant.60.left_ref) | copy-start | bytes 294916
  36.6 10.2 %copy-start.10 = (bf16[256,192]{1,0:T(8,128)(2,1)S(1)}, bf16[256,192]{1,0:T(8,128)(2,1)}, u32[]{:S(2)}) copy-start(bf16[256,192]{1,0:T(8,128)(2,1)} %constant.61.back_ref) | copy-start | bytes 294916
  47.5 9.4 %copy-start.7 = (bf16[256,256]{1,0:T(8,128)(2,1)S(1)}, bf16[256,256]{1,0:T(8,128)(2,1)}, u32[]{:S(2)}) copy-start(bf16[256,256]{1,0:T(8,128)(2,1)} %constant.63.right_ref) | copy-start | bytes 393220
  47.5 9.4 %copy-start.9 = (bf16[256,256]{1,0:T(8,128)(2,1)S(1)}, bf16[256,256]{1,0:T(8,128)(2,1)}, u32[]{:S(2)}) copy-start(bf16[256,256]{1,0:T(8,128)(2,1)} %constant.62.left_ref) | copy-start | bytes 393220
  47.5 9.4 %copy-start.18 = (f32[128,128]{1,0:T(8,128)S(1)}, f32[128,128]{1,0:T(8,128)}, u32[]{:S(2)}) copy-start(f32[128,128]{1,0:T(8,128)} %constant.48.clone.sin_ref) | copy-start | bytes 196612
  47.5 9.4 %copy-start.19 = (f32[128,128]{1,0:T(8,128)S(1)}, f32[128,128]{1,0:T(8,128)}, u32[]{:S(2)}) copy-start(f32[128,128]{1,0:T(8,128)} %constant.47.clone.cos_ref) | copy-start | bytes 196612
  56.9 24.1 %copy-start.3 = (bf16[384,512]{1,0:T(8,128)(2,1)S(1)}, bf16[384,512]{1,0:T(8,128)(2,1)}, u32[]{:S(2)}) copy-start(bf16[384,512]{1,0:T(8,128)(2,1)} %constant.64.back_ref) | copy-start | bytes 1179652
  56.9 24.1 %copy-start.4 = (bf16[384,512]{1,0:T(8,128)(2,1)S(1)}, bf16[384,512]{1,0:T(8,128)(2,1)}, u32[]{:S(2)}) copy-start(bf16[384,512]{1,0:T(8,128)(2,1)} %constant.56.table_hbm.table_ref) | copy-start | bytes 1179652
  57.5 23.5 %copy-start = (f32[3,16,2,512]{3,2,1,0:T(2,128)S(1)}, f32[3,16,2,512]{3,2,1,0:T(2,128)}, u32[]{:S(2)}) copy-start(f32[3,16,2,512]{3,2,1,0:T(2,128)} %param.27) | copy-start | bytes 589828
  57.5 23.5 %copy-start.1 = (f32[16,2,512]{2,1,0:T(2,128)S(1)}, f32[16,2,512]{2,1,0:T(2,128)}, u32[]{:S(2)}) copy-start(f32[16,2,512]{2,1,0:T(2,128)} %param.26) | copy-start | bytes 196612
  81.0 21.2 %copy-start.2 = (bf16[512,512]{1,0:T(8,128)(2,1)S(1)}, bf16[512,512]{1,0:T(8,128)(2,1)}, u32[]{:S(2)}) copy-start(bf16[512,512]{1,0:T(8,128)(2,1)} %constant.65.right_ref) | copy-start | bytes 1572868
  103.0 9.4 %copy-start.8 = (bf16[256,192]{1,0:T(8,128)(2,1)S(1)}, bf16[256,192]{1,0:T(8,128)(2,1)}, u32[]{:S(2)}) copy-start(bf16[256,192]{1,0:T(8,128)(2,1)} %constant.67.back_ref) | copy-start | bytes 294916
  103.0 9.4 %copy-start.16 = (bf16[192,256]{1,0:T(8,128)(2,1)S(1)}, bf16[192,256]{1,0:T(8,128)(2,1)}, u32[]{:S(2)}) copy-start(bf16[192,256]{1,0:T(8,128)(2,1)} %constant.66.left_ref) | copy-start | bytes 294916
  112.4 9.0 %copy-start.5 = (bf16[384,384]{1,0:T(8,128)(2,1)S(1)}, bf16[384,384]{1,0:T(8,128)(2,1)}, u32[]{:S(2)}) copy-start(bf16[384,384]{1,0:T(8,128)(2,1)} %constant.68.left_ref) | copy-start | bytes 884740

commit v6 on v4

--- a/solution.py
+++ b/solution.py
@@ -152,6 +152,12 @@
 def dot(lhs, rhs):
     return lax.dot_general(
         lhs, rhs, (((1,), (0,)), ((), ())), preferred_element_type=jnp.float32
+    )
+
+
+def dot_tn(lhs, rhs):
+    return lax.dot_general(
+        lhs, rhs, (((0,), (0,)), ((), ())), preferred_element_type=jnp.float32
     )
 
 
@@ -420,7 +426,7 @@
     )
     terms = []
     for z in range(2):
-        values = dot(to_bf16(sides[z].T), back_ref[...])
+        values = dot_tn(to_bf16(sides[z]), back_ref[...])
         d = [values[YL * f : YL * (f + 1)] for f in range(7)]
         phase = plane(phase_ref, z)
         v = [plane(vel_ref, z, j) for j in range(3)]
@@ -437,8 +443,7 @@
 
 
 def x_inverse_kernel(in_ref, back_ref, phase_hbm, vel_hbm, fields, sems):
-    lines = to_bf16(in_ref[...].astype(jnp.float32).T)
-    values = dot(lines, back_ref[...])
+    values = dot_tn(in_ref[...], back_ref[...])
     copies = []
     for f in range(4):
         for z in range(2):

time: 143 us -> 143 us (level)
  no operation moved by 1% of the time
where the time goes in v6:
time: 143 us; the launch traced here: 142 us
  blocking collectives  135 us (94%)
  Pallas kernels  6.64 us (5%)
    all_to_all x8, blocking collectives, exchange(): lax.all_to_all(values.reshape(rows // 2, 2, 128), axis, split_axis=0, con...  135 us
    pallas_call x9, Pallas kernels, call(): pl.pallas_call(kernel, in_specs=specs, out_specs=[pl.BlockSpec(memory_spa...  6.64 us

profile of v6, /device:TPU:2, one launch (start us, length us, event | category | flops | bytes accessed | tf_op | source)
XLA Modules:
  0.0 142.4 jit_solution(11862829682146790651)
XLA Ops:
  0.6 0.0 copy-start.6
  0.6 0.0 copy-start.13
  0.7 0.0 copy-start.14
  0.7 1.6 %shard_map.257 = (bf16[384,128]{1,0:T(8,128)(2,1)S(1)}, bf16[768,128]{1,0:T(8,128)(2,1)S(1)}) custom-call(f32[128,128]{1,0:T(8,128)} %bitcast.54, f32[3,128,128]{2,1,0:T(8,128)} %bitcast.52, bf16[384,512]{1,0:T(8,128)(2,1)} %constant.56.table_hbm.table_ref), custom_call_target="tpu_custom_call" | custom-call | flops 10000000000 | bytes 25000000 | tf_op jit(solution)/shard_map/pallas_call | solution.py:461
  2.3 0.0 copy-start.12
  2.3 33.7 %all_to_all.40 = bf16[192,2,128]{2,1,0:T(2,128)(2,1)S(1)} all-to-all(bf16[192,2,128]{2,1,0:T(2,128)(2,1)S(1)} %bitcast.49), channel_id=1, replica_groups=mesh['far'=2,'near'=8,'z'=16,'xl'=2] {'xl','far','z'}, dimensions={0} | all-to-all | bytes 196608 | tf_op jit(solution)/shard_map/all_to_all | solution.py:480
  36.0 0.0 copy-done.6
  36.0 0.0 copy-done.13
  36.0 0.0 copy-done.14
  36.0 0.0 copy-done.12
  36.0 0.0 copy-start.11
  36.0 0.0 copy-start.15
  36.0 0.0 copy-start.17
  36.0 0.4 shard_map.258
  36.4 0.0 copy-start.10
  36.5 10.2 %all_to_all.41 = bf16[192,2,128]{2,1,0:T(2,128)(2,1)S(1)} all-to-all(bf16[192,2,128]{2,1,0:T(2,128)(2,1)S(1)} %bitcast.51), channel_id=1, replica_groups=mesh['far'=2,'near'=8,'z'=16,'xl'=2] {'near'}, dimensions={0} | all-to-all | bytes 196608 | tf_op jit(solution)/shard_map/all_to_all | solution.py:480
  46.7 0.0 copy-done.11
  46.7 0.0 copy-done.15
  46.7 0.0 copy-done.17
  46.7 0.0 copy-done.10
  46.7 0.7 shard_map.259
  47.3 0.0 copy-start.7
  47.4 0.0 copy-start.9
  47.4 0.0 copy-start.18
  47.4 0.0 copy-start.19
  47.4 9.3 %all_to_all.42 = bf16[384,2,128]{2,1,0:T(2,128)(2,1)S(1)} all-to-all(bf16[384,2,128]{2,1,0:T(2,128)(2,1)S(1)} %bitcast.36), channel_id=1, replica_groups=mesh['far'=2,'near'=8,'z'=16,'xl'=2] {'near'}, dimensions={0} | all-to-all | bytes 393216 | tf_op jit(solution)/shard_map/all_to_all | solution.py:480
  56.7 0.0 copy-done.7
  56.7 0.0 copy-done.9
  56.7 0.0 copy-done.18
  56.7 0.0 copy-done.19
  56.8 0.0 copy-start.3
  56.8 0.0 copy-start.4
  56.8 0.5 shard_map.260
  57.3 0.0 copy-start
  57.3 0.0 copy-start.1
  57.3 23.5 %all_to_all.43 = bf16[384,2,128]{2,1,0:T(2,128)(2,1)S(1)} all-to-all(bf16[384,2,128]{2,1,0:T(2,128)(2,1)S(1)} %bitcast.39), channel_id=1, replica_groups=mesh['far'=2,'near'=8,'z'=16,'xl'=2] {'xl','far','z'}, dimensions={0} | all-to-all | bytes 393216 | tf_op jit(solution)/shard_map/all_to_all | solution.py:480
  80.8 0.0 copy-done.3
  80.8 0.0 copy-done.4
  80.8 0.0 copy-done
  80.8 0.0 copy-done.1
  80.8 0.0 copy-start.2
  80.8 0.6 shard_map.261
  81.4 20.6 %all_to_all.44 = bf16[192,2,128]{2,1,0:T(2,128)(2,1)S(1)} all-to-all(bf16[192,2,128]{2,1,0:T(2,128)(2,1)S(1)} %bitcast.47), channel_id=1, replica_groups=mesh['far'=2,'near'=8,'z'=16,'xl'=2] {'xl','far','z'}, dimensions={0} | all-to-all | bytes 196608 | tf_op jit(solution)/shard_map/all_to_all | solution.py:480
  102.0 0.0 copy-done.2
  102.0 0.6 shard_map.262
  102.7 0.0 copy-start.8
  102.7 0.0 copy-start.16
  102.7 9.3 %all_to_all.45 = bf16[384,2,128]{2,1,0:T(2,128)(2,1)S(1)} all-to-all(bf16[384,2,128]{2,1,0:T(2,128)(2,1)S(1)} %bitcast.41), channel_id=1, replica_groups=mesh['far'=2,'near'=8,'z'=16,'xl'=2] {'near'}, dimensions={0} | all-to-all | bytes 393216 | tf_op jit(solution)/shard_map/all_to_all | solution.py:480
  112.0 0.0 copy-done.8
  112.0 0.0 copy-done.16
  112.0 0.0 copy-start.5
  112.0 0.8 shard_map.263
  112.9 8.2 %all_to_all.46 = bf16[192,2,128]{2,1,0:T(2,128)(2,1)S(1)} all-to-all(bf16[192,2,128]{2,1,0:T(2,128)(2,1)S(1)} %bitcast.44), channel_id=1, replica_groups=mesh['far'=2,'near'=8,'z'=16,'xl'=2] {'near'}, dimensions={0} | all-to-all | bytes 196608 | tf_op jit(solution)/shard_map/all_to_all | solution.py:480
  121.0 0.0 copy-done.5
  121.0 0.4 shard_map.264
  121.5 19.9 %all_to_all.47 = bf16[192,2,128]{2,1,0:T(2,128)(2,1)S(1)} all-to-all(bf16[192,2,128]{2,1,0:T(2,128)(2,1)S(1)} %bitcast.46), channel_id=1, replica_groups=mesh['far'=2,'near'=8,'z'=16,'xl'=2] {'xl','far','z'}, dimensions={0} | all-to-all | bytes 196608 | tf_op jit(solution)/shard_map/all_to_all | solution.py:480
  141.4 1.0 shard_map.265
Async XLA Ops:
  0.6 35.4 %copy-start.6 = (bf16[384,384]{1,0:T(8,128)(2,1)S(1)}, bf16[384,384]{1,0:T(8,128)(2,1)}, u32[]{:S(2)}) copy-start(bf16[384,384]{1,0:T(8,128)(2,1)} %constant.57.left_ref) | copy-start | bytes 884740
  0.6 35.4 %copy-start.13 = (f32[192,128]{1,0:T(8,128)S(1)}, f32[192,128]{1,0:T(8,128)}, u32[]{:S(2)}) copy-start(f32[192,128]{1,0:T(8,128)} %constant.41.clone.sin_ref) | copy-start | bytes 294916
  0.7 35.3 %copy-start.14 = (f32[192,128]{1,0:T(8,128)S(1)}, f32[192,128]{1,0:T(8,128)}, u32[]{:S(2)}) copy-start(f32[192,128]{1,0:T(8,128)} %constant.40.clone.cos_ref) | copy-start | bytes 294916
  2.3 33.7 %copy-start.12 = (bf16[256,256]{1,0:T(8,128)(2,1)S(1)}, bf16[256,256]{1,0:T(8,128)(2,1)}, u32[]{:S(2)}) copy-start(bf16[256,256]{1,0:T(8,128)(2,1)} %constant.58.right_ref) | copy-start | bytes 393220
  36.0 10.7 %copy-start.11 = (bf16[128,512]{1,0:T(8,128)(2,1)S(1)}, bf16[128,512]{1,0:T(8,128)(2,1)}, u32[]{:S(2)}) copy-start(bf16[128,512]{1,0:T(8,128)(2,1)} %constant.59.spread_ref) | copy-start | bytes 393220
  36.0 10.7 %copy-start.15 = (f32[192,128]{1,0:T(8,128)S(1)}, f32[192,128]{1,0:T(8,128)}, u32[]{:S(2)}) copy-start(f32[192,128]{1,0:T(8,128)} %constant.38.clone.wave_ref) | copy-start | bytes 294916
  36.0 10.6 %copy-start.17 = (bf16[192,256]{1,0:T(8,128)(2,1)S(1)}, bf16[192,256]{1,0:T(8,128)(2,1)}, u32[]{:S(2)}) copy-start(bf16[192,256]{1,0:T(8,128)(2,1)} %constant.60.left_ref) | copy-start | bytes 294916
  36.4 10.2 %copy-start.10 = (bf16[256,192]{1,0:T(8,128)(2,1)S(1)}, bf16[256,192]{1,0:T(8,128)(2,1)}, u32[]{:S(2)}) copy-start(bf16[256,192]{1,0:T(8,128)(2,1)} %constant.61.back_ref) | copy-start | bytes 294916
  47.3 9.4 %copy-start.7 = (bf16[256,256]{1,0:T(8,128)(2,1)S(1)}, bf16[256,256]{1,0:T(8,128)(2,1)}, u32[]{:S(2)}) copy-start(bf16[256,256]{1,0:T(8,128)(2,1)} %constant.63.right_ref) | copy-start | bytes 393220
  47.4 9.4 %copy-start.9 = (bf16[256,256]{1,0:T(8,128)(2,1)S(1)}, bf16[256,256]{1,0:T(8,128)(2,1)}, u32[]{:S(2)}) copy-start(bf16[256,256]{1,0:T(8,128)(2,1)} %constant.62.left_ref) | copy-start | bytes 393220
  47.4 9.4 %copy-start.18 = (f32[128,128]{1,0:T(8,128)S(1)}, f32[128,128]{1,0:T(8,128)}, u32[]{:S(2)}) copy-start(f32[128,128]{1,0:T(8,128)} %constant.48.clone.sin_ref) | copy-start | bytes 196612
  47.4 9.4 %copy-start.19 = (f32[128,128]{1,0:T(8,128)S(1)}, f32[128,128]{1,0:T(8,128)}, u32[]{:S(2)}) copy-start(f32[128,128]{1,0:T(8,128)} %constant.47.clone.cos_ref) | copy-start | bytes 196612
  56.8 24.1 %copy-start.3 = (bf16[384,512]{1,0:T(8,128)(2,1)S(1)}, bf16[384,512]{1,0:T(8,128)(2,1)}, u32[]{:S(2)}) copy-start(bf16[384,512]{1,0:T(8,128)(2,1)} %constant.64.back_ref) | copy-start | bytes 1179652
  56.8 24.0 %copy-start.4 = (bf16[384,512]{1,0:T(8,128)(2,1)S(1)}, bf16[384,512]{1,0:T(8,128)(2,1)}, u32[]{:S(2)}) copy-start(bf16[384,512]{1,0:T(8,128)(2,1)} %constant.56.table_hbm.table_ref) | copy-start | bytes 1179652
  57.3 23.5 %copy-start = (f32[3,16,2,512]{3,2,1,0:T(2,128)S(1)}, f32[3,16,2,512]{3,2,1,0:T(2,128)}, u32[]{:S(2)}) copy-start(f32[3,16,2,512]{3,2,1,0:T(2,128)} %param.27) | copy-start | bytes 589828
  57.3 23.5 %copy-start.1 = (f32[16,2,512]{2,1,0:T(2,128)S(1)}, f32[16,2,512]{2,1,0:T(2,128)}, u32[]{:S(2)}) copy-start(f32[16,2,512]{2,1,0:T(2,128)} %param.26) | copy-start | bytes 196612
  80.8 21.2 %copy-start.2 = (bf16[512,512]{1,0:T(8,128)(2,1)S(1)}, bf16[512,512]{1,0:T(8,128)(2,1)}, u32[]{:S(2)}) copy-start(bf16[512,512]{1,0:T(8,128)(2,1)} %constant.65.right_ref) | copy-start | bytes 1572868
  102.7 9.4 %copy-start.8 = (bf16[256,192]{1,0:T(8,128)(2,1)S(1)}, bf16[256,192]{1,0:T(8,128)(2,1)}, u32[]{:S(2)}) copy-start(bf16[256,192]{1,0:T(8,128)(2,1)} %constant.67.back_ref) | copy-start | bytes 294916
  102.7 9.4 %copy-start.16 = (bf16[192,256]{1,0:T(8,128)(2,1)S(1)}, bf16[192,256]{1,0:T(8,128)(2,1)}, u32[]{:S(2)}) copy-start(bf16[192,256]{1,0:T(8,128)(2,1)} %constant.66.left_ref) | copy-start | bytes 294916
  112.0 9.0 %copy-start.5 = (bf16[384,384]{1,0:T(8,128)(2,1)S(1)}, bf16[384,384]{1,0:T(8,128)(2,1)}, u32[]{:S(2)}) copy-start(bf16[384,384]{1,0:T(8,128)(2,1)} %constant.68.left_ref) | copy-start | bytes 884740

commit v7 on v6

--- a/solution.py
+++ b/solution.py
@@ -209,15 +209,15 @@
             [(phase_hbm, phase_ref), (vel_hbm, vel_ref), (table_hbm, table_ref)]
         )
     ]
-    for c in copies:
-        c.start()
-    for c in copies[:2]:
-        c.wait()
+    for i in (2, 1, 0):
+        copies[i].start()
+    copies[0].wait()
     phases = [plane(phase_ref, z) for z in range(2)]
+    bulk = [p * p * p - p for p in phases]
+    copies[1].wait()
     rows = []
     for z in range(2):
         rows += [phases[z]] + [plane(vel_ref, z, j) for j in range(3)]
-    bulk = [p * p * p - p for p in phases]
     rows += [jnp.zeros((6 * YL, NX), jnp.float32), bulk[1], bulk[0]]
     x = jnp.concatenate([to_bf16(r) for r in rows], axis=0)
     copies[2].wait()

time: 143 us -> 143 us (level)
  no operation moved by 1% of the time
where the time goes in v7:
time: 143 us; the launch traced here: 142 us
  blocking collectives  135 us (94%)
  Pallas kernels  6.61 us (5%)
    all_to_all x8, blocking collectives, exchange(): lax.all_to_all(values.reshape(rows // 2, 2, 128), axis, split_axis=0, con...  135 us
    pallas_call x9, Pallas kernels, call(): pl.pallas_call(kernel, in_specs=specs, out_specs=[pl.BlockSpec(memory_spa...  6.61 us

profile of v7, /device:TPU:2, one launch (start us, length us, event | category | flops | bytes accessed | tf_op | source)
XLA Modules:
  0.0 142.3 jit_solution(16690383712401445145)
XLA Ops:
  0.6 0.0 copy-start.6
  0.6 0.0 copy-start.13
  0.7 0.0 copy-start.14
  0.7 1.6 %shard_map.257 = (bf16[384,128]{1,0:T(8,128)(2,1)S(1)}, bf16[768,128]{1,0:T(8,128)(2,1)S(1)}) custom-call(f32[128,128]{1,0:T(8,128)} %bitcast.54, f32[3,128,128]{2,1,0:T(8,128)} %bitcast.52, bf16[384,512]{1,0:T(8,128)(2,1)} %constant.56.table_hbm.table_ref), custom_call_target="tpu_custom_call" | custom-call | flops 10000000000 | bytes 25000000 | tf_op jit(solution)/shard_map/pallas_call | solution.py:461
  2.3 0.0 copy-start.12
  2.3 33.7 %all_to_all.40 = bf16[192,2,128]{2,1,0:T(2,128)(2,1)S(1)} all-to-all(bf16[192,2,128]{2,1,0:T(2,128)(2,1)S(1)} %bitcast.49), channel_id=1, replica_groups=mesh['far'=2,'near'=8,'z'=16,'xl'=2] {'xl','far','z'}, dimensions={0} | all-to-all | bytes 196608 | tf_op jit(solution)/shard_map/all_to_all | solution.py:480
  36.0 0.0 copy-done.6
  36.0 0.0 copy-done.13
  36.0 0.0 copy-done.14
  36.0 0.0 copy-done.12
  36.0 0.0 copy-start.11
  36.0 0.0 copy-start.15
  36.0 0.0 copy-start.17
  36.0 0.4 shard_map.258
  36.4 0.0 copy-start.10
  36.4 10.2 %all_to_all.41 = bf16[192,2,128]{2,1,0:T(2,128)(2,1)S(1)} all-to-all(bf16[192,2,128]{2,1,0:T(2,128)(2,1)S(1)} %bitcast.51), channel_id=1, replica_groups=mesh['far'=2,'near'=8,'z'=16,'xl'=2] {'near'}, dimensions={0} | all-to-all | bytes 196608 | tf_op jit(solution)/shard_map/all_to_all | solution.py:480
  46.6 0.0 copy-done.11
  46.6 0.0 copy-done.15
  46.6 0.0 copy-done.17
  46.6 0.0 copy-done.10
  46.7 0.7 shard_map.259
  47.3 0.0 copy-start.7
  47.3 0.0 copy-start.9
  47.3 0.0 copy-start.18
  47.4 0.0 copy-start.19
  47.4 9.3 %all_to_all.42 = bf16[384,2,128]{2,1,0:T(2,128)(2,1)S(1)} all-to-all(bf16[384,2,128]{2,1,0:T(2,128)(2,1)S(1)} %bitcast.36), channel_id=1, replica_groups=mesh['far'=2,'near'=8,'z'=16,'xl'=2] {'near'}, dimensions={0} | all-to-all | bytes 393216 | tf_op jit(solution)/shard_map/all_to_all | solution.py:480
  56.7 0.0 copy-done.7
  56.7 0.0 copy-done.9
  56.7 0.0 copy-done.18
  56.7 0.0 copy-done.19
  56.7 0.0 copy-start.3
  56.7 0.0 copy-start.4
  56.7 0.5 shard_map.260
  57.3 0.0 copy-start
  57.3 0.0 copy-start.1
  57.3 23.5 %all_to_all.43 = bf16[384,2,128]{2,1,0:T(2,128)(2,1)S(1)} all-to-all(bf16[384,2,128]{2,1,0:T(2,128)(2,1)S(1)} %bitcast.39), channel_id=1, replica_groups=mesh['far'=2,'near'=8,'z'=16,'xl'=2] {'xl','far','z'}, dimensions={0} | all-to-all | bytes 393216 | tf_op jit(solution)/shard_map/all_to_all | solution.py:480
  80.8 0.0 copy-done.3
  80.8 0.0 copy-done.4
  80.8 0.0 copy-done
  80.8 0.0 copy-done.1
  80.8 0.0 copy-start.2
  80.8 0.6 shard_map.261
  81.4 20.6 %all_to_all.44 = bf16[192,2,128]{2,1,0:T(2,128)(2,1)S(1)} all-to-all(bf16[192,2,128]{2,1,0:T(2,128)(2,1)S(1)} %bitcast.47), channel_id=1, replica_groups=mesh['far'=2,'near'=8,'z'=16,'xl'=2] {'xl','far','z'}, dimensions={0} | all-to-all | bytes 196608 | tf_op jit(solution)/shard_map/all_to_all | solution.py:480
  102.0 0.0 copy-done.2
  102.0 0.6 shard_map.262
  102.6 0.0 copy-start.8
  102.6 0.0 copy-start.16
  102.7 9.3 %all_to_all.45 = bf16[384,2,128]{2,1,0:T(2,128)(2,1)S(1)} all-to-all(bf16[384,2,128]{2,1,0:T(2,128)(2,1)S(1)} %bitcast.41), channel_id=1, replica_groups=mesh['far'=2,'near'=8,'z'=16,'xl'=2] {'near'}, dimensions={0} | all-to-all | bytes 393216 | tf_op jit(solution)/shard_map/all_to_all | solution.py:480
  112.0 0.0 copy-done.8
  112.0 0.0 copy-done.16
  112.0 0.0 copy-start.5
  112.0 0.8 shard_map.263
  112.8 8.2 %all_to_all.46 = bf16[192,2,128]{2,1,0:T(2,128)(2,1)S(1)} all-to-all(bf16[192,2,128]{2,1,0:T(2,128)(2,1)S(1)} %bitcast.44), channel_id=1, replica_groups=mesh['far'=2,'near'=8,'z'=16,'xl'=2] {'near'}, dimensions={0} | all-to-all | bytes 196608 | tf_op jit(solution)/shard_map/all_to_all | solution.py:480
  121.0 0.0 copy-done.5
  121.0 0.4 shard_map.264
  121.5 19.9 %all_to_all.47 = bf16[192,2,128]{2,1,0:T(2,128)(2,1)S(1)} all-to-all(bf16[192,2,128]{2,1,0:T(2,128)(2,1)S(1)} %bitcast.46), channel_id=1, replica_groups=mesh['far'=2,'near'=8,'z'=16,'xl'=2] {'xl','far','z'}, dimensions={0} | all-to-all | bytes 196608 | tf_op jit(solution)/shard_map/all_to_all | solution.py:480
  141.4 1.0 shard_map.265
Async XLA Ops:
  0.6 35.3 %copy-start.6 = (bf16[384,384]{1,0:T(8,128)(2,1)S(1)}, bf16[384,384]{1,0:T(8,128)(2,1)}, u32[]{:S(2)}) copy-start(bf16[384,384]{1,0:T(8,128)(2,1)} %constant.57.left_ref) | copy-start | bytes 884740
  0.6 35.3 %copy-start.13 = (f32[192,128]{1,0:T(8,128)S(1)}, f32[192,128]{1,0:T(8,128)}, u32[]{:S(2)}) copy-start(f32[192,128]{1,0:T(8,128)} %constant.41.clone.sin_ref) | copy-start | bytes 294916
  0.7 35.3 %copy-start.14 = (f32[192,128]{1,0:T(8,128)S(1)}, f32[192,128]{1,0:T(8,128)}, u32[]{:S(2)}) copy-start(f32[192,128]{1,0:T(8,128)} %constant.40.clone.cos_ref) | copy-start | bytes 294916
  2.3 33.7 %copy-start.12 = (bf16[256,256]{1,0:T(8,128)(2,1)S(1)}, bf16[256,256]{1,0:T(8,128)(2,1)}, u32[]{:S(2)}) copy-start(bf16[256,256]{1,0:T(8,128)(2,1)} %constant.58.right_ref) | copy-start | bytes 393220
  36.0 10.6 %copy-start.11 = (bf16[128,512]{1,0:T(8,128)(2,1)S(1)}, bf16[128,512]{1,0:T(8,128)(2,1)}, u32[]{:S(2)}) copy-start(bf16[128,512]{1,0:T(8,128)(2,1)} %constant.59.spread_ref) | copy-start | bytes 393220
  36.0 10.6 %copy-start.15 = (f32[192,128]{1,0:T(8,128)S(1)}, f32[192,128]{1,0:T(8,128)}, u32[]{:S(2)}) copy-start(f32[192,128]{1,0:T(8,128)} %constant.38.clone.wave_ref) | copy-start | bytes 294916
  36.0 10.6 %copy-start.17 = (bf16[192,256]{1,0:T(8,128)(2,1)S(1)}, bf16[192,256]{1,0:T(8,128)(2,1)}, u32[]{:S(2)}) copy-start(bf16[192,256]{1,0:T(8,128)(2,1)} %constant.60.left_ref) | copy-start | bytes 294916
  36.4 10.2 %copy-start.10 = (bf16[256,192]{1,0:T(8,128)(2,1)S(1)}, bf16[256,192]{1,0:T(8,128)(2,1)}, u32[]{:S(2)}) copy-start(bf16[256,192]{1,0:T(8,128)(2,1)} %constant.61.back_ref) | copy-start | bytes 294916
  47.3 9.4 %copy-start.7 = (bf16[256,256]{1,0:T(8,128)(2,1)S(1)}, bf16[256,256]{1,0:T(8,128)(2,1)}, u32[]{:S(2)}) copy-start(bf16[256,256]{1,0:T(8,128)(2,1)} %constant.63.right_ref) | copy-start | bytes 393220
  47.3 9.4 %copy-start.9 = (bf16[256,256]{1,0:T(8,128)(2,1)S(1)}, bf16[256,256]{1,0:T(8,128)(2,1)}, u32[]{:S(2)}) copy-start(bf16[256,256]{1,0:T(8,128)(2,1)} %constant.62.left_ref) | copy-start | bytes 393220
  47.3 9.4 %copy-start.18 = (f32[128,128]{1,0:T(8,128)S(1)}, f32[128,128]{1,0:T(8,128)}, u32[]{:S(2)}) copy-start(f32[128,128]{1,0:T(8,128)} %constant.48.clone.sin_ref) | copy-start | bytes 196612
  47.4 9.4 %copy-start.19 = (f32[128,128]{1,0:T(8,128)S(1)}, f32[128,128]{1,0:T(8,128)}, u32[]{:S(2)}) copy-start(f32[128,128]{1,0:T(8,128)} %constant.47.clone.cos_ref) | copy-start | bytes 196612
  56.7 24.0 %copy-start.3 = (bf16[384,512]{1,0:T(8,128)(2,1)S(1)}, bf16[384,512]{1,0:T(8,128)(2,1)}, u32[]{:S(2)}) copy-start(bf16[384,512]{1,0:T(8,128)(2,1)} %constant.64.back_ref) | copy-start | bytes 1179652
  56.7 24.0 %copy-start.4 = (bf16[384,512]{1,0:T(8,128)(2,1)S(1)}, bf16[384,512]{1,0:T(8,128)(2,1)}, u32[]{:S(2)}) copy-start(bf16[384,512]{1,0:T(8,128)(2,1)} %constant.56.table_hbm.table_ref) | copy-start | bytes 1179652
  57.3 23.5 %copy-start = (f32[3,16,2,512]{3,2,1,0:T(2,128)S(1)}, f32[3,16,2,512]{3,2,1,0:T(2,128)}, u32[]{:S(2)}) copy-start(f32[3,16,2,512]{3,2,1,0:T(2,128)} %param.27) | copy-start | bytes 589828
  57.3 23.5 %copy-start.1 = (f32[16,2,512]{2,1,0:T(2,128)S(1)}, f32[16,2,512]{2,1,0:T(2,128)}, u32[]{:S(2)}) copy-start(f32[16,2,512]{2,1,0:T(2,128)} %param.26) | copy-start | bytes 196612
  80.8 21.2 %copy-start.2 = (bf16[512,512]{1,0:T(8,128)(2,1)S(1)}, bf16[512,512]{1,0:T(8,128)(2,1)}, u32[]{:S(2)}) copy-start(bf16[512,512]{1,0:T(8,128)(2,1)} %constant.65.right_ref) | copy-start | bytes 1572868
  102.6 9.4 %copy-start.8 = (bf16[256,192]{1,0:T(8,128)(2,1)S(1)}, bf16[256,192]{1,0:T(8,128)(2,1)}, u32[]{:S(2)}) copy-start(bf16[256,192]{1,0:T(8,128)(2,1)} %constant.67.back_ref) | copy-start | bytes 294916
  102.6 9.4 %copy-start.16 = (bf16[192,256]{1,0:T(8,128)(2,1)S(1)}, bf16[192,256]{1,0:T(8,128)(2,1)}, u32[]{:S(2)}) copy-start(bf16[192,256]{1,0:T(8,128)(2,1)} %constant.66.left_ref) | copy-start | bytes 294916
  112.0 9.0 %copy-start.5 = (bf16[384,384]{1,0:T(8,128)(2,1)S(1)}, bf16[384,384]{1,0:T(8,128)(2,1)}, u32[]{:S(2)}) copy-start(bf16[384,384]{1,0:T(8,128)(2,1)} %constant.68.left_ref) | copy-start | bytes 884740

commit v8 on v7

--- a/solution.py
+++ b/solution.py
@@ -206,10 +206,15 @@
     copies = [
         pltpu.make_async_copy(src, dst, sems.at[i])
         for i, (src, dst) in enumerate(
-            [(phase_hbm, phase_ref), (vel_hbm, vel_ref), (table_hbm, table_ref)]
+            [
+                (phase_hbm, phase_ref),
+                (vel_hbm, vel_ref),
+                (table_hbm.at[pl.ds(0, KC)], table_ref.at[pl.ds(0, KC)]),
+                (table_hbm.at[pl.ds(KC, KC)], table_ref.at[pl.ds(KC, KC)]),
+            ]
         )
     ]
-    for i in (2, 1, 0):
+    for i in (2, 3, 1, 0):
         copies[i].start()
     copies[0].wait()
     phases = [plane(phase_ref, z) for z in range(2)]
@@ -221,6 +226,7 @@
     rows += [jnp.zeros((6 * YL, NX), jnp.float32), bulk[1], bulk[0]]
     x = jnp.concatenate([to_bf16(r) for r in rows], axis=0)
     copies[2].wait()
+    copies[3].wait()
     lines = dot_nt(table_ref[...], x)
     out_ref[...] = to_bf16(lines[:, :128])
     wide[pl.ds(0, LINES, stride=2), :] = lines[:, 128:]
@@ -502,7 +508,7 @@
             pltpu.VMEM(phase.shape, f32),
             pltpu.VMEM(velocity.shape, f32),
             pltpu.VMEM(x_table.shape, x_table.dtype),
-            pltpu.SemaphoreType.DMA((3,)),
+            pltpu.SemaphoreType.DMA((4,)),
             scratch(2 * LINES),
         ],
         *(

time: 143 us -> 143 us (level)
  no operation moved by 1% of the time
where the time goes in v8:
time: 143 us; the launch traced here: 142 us
  blocking collectives  135 us (94%)
  Pallas kernels  6.69 us (5%)
    all_to_all x8, blocking collectives, exchange(): lax.all_to_all(values.reshape(rows // 2, 2, 128), axis, split_axis=0, con...  135 us
    pallas_call x9, Pallas kernels, call(): pl.pallas_call(kernel, in_specs=specs, out_specs=[pl.BlockSpec(memory_spa...  6.69 us

profile of v8, /device:TPU:2, one launch (start us, length us, event | category | flops | bytes accessed | tf_op | source)
XLA Modules:
  0.0 142.4 jit_solution(17808653413822937131)
XLA Ops:
  0.6 0.0 copy-start.6
  0.6 0.0 copy-start.13
  0.7 0.0 copy-start.14
  0.7 1.7 %shard_map.257 = (bf16[384,128]{1,0:T(8,128)(2,1)S(1)}, bf16[768,128]{1,0:T(8,128)(2,1)S(1)}) custom-call(f32[128,128]{1,0:T(8,128)} %bitcast.54, f32[3,128,128]{2,1,0:T(8,128)} %bitcast.52, bf16[384,512]{1,0:T(8,128)(2,1)} %constant.56.table_hbm.table_ref), custom_call_target="tpu_custom_call" | custom-call | flops 10000000000 | bytes 25000000 | tf_op jit(solution)/shard_map/pallas_call | solution.py:467
  2.3 0.0 copy-start.12
  2.4 33.7 %all_to_all.40 = bf16[192,2,128]{2,1,0:T(2,128)(2,1)S(1)} all-to-all(bf16[192,2,128]{2,1,0:T(2,128)(2,1)S(1)} %bitcast.49), channel_id=1, replica_groups=mesh['far'=2,'near'=8,'z'=16,'xl'=2] {'xl','far','z'}, dimensions={0} | all-to-all | bytes 196608 | tf_op jit(solution)/shard_map/all_to_all | solution.py:486
  36.0 0.0 copy-done.6
  36.0 0.0 copy-done.13
  36.0 0.0 copy-done.14
  36.1 0.0 copy-done.12
  36.1 0.0 copy-start.11
  36.1 0.0 copy-start.15
  36.1 0.0 copy-start.17
  36.1 0.4 shard_map.258
  36.5 0.0 copy-start.10
  36.5 10.2 %all_to_all.41 = bf16[192,2,128]{2,1,0:T(2,128)(2,1)S(1)} all-to-all(bf16[192,2,128]{2,1,0:T(2,128)(2,1)S(1)} %bitcast.51), channel_id=1, replica_groups=mesh['far'=2,'near'=8,'z'=16,'xl'=2] {'near'}, dimensions={0} | all-to-all | bytes 196608 | tf_op jit(solution)/shard_map/all_to_all | solution.py:486
  46.7 0.0 copy-done.11
  46.7 0.0 copy-done.15
  46.7 0.0 copy-done.17
  46.7 0.0 copy-done.10
  46.7 0.7 shard_map.259
  47.4 0.0 copy-start.7
  47.4 0.0 copy-start.9
  47.4 0.0 copy-start.18
  47.4 0.0 copy-start.19
  47.4 9.3 %all_to_all.42 = bf16[384,2,128]{2,1,0:T(2,128)(2,1)S(1)} all-to-all(bf16[384,2,128]{2,1,0:T(2,128)(2,1)S(1)} %bitcast.36), channel_id=1, replica_groups=mesh['far'=2,'near'=8,'z'=16,'xl'=2] {'near'}, dimensions={0} | all-to-all | bytes 393216 | tf_op jit(solution)/shard_map/all_to_all | solution.py:486
  56.8 0.0 copy-done.7
  56.8 0.0 copy-done.9
  56.8 0.0 copy-done.18
  56.8 0.0 copy-done.19
  56.8 0.0 copy-start.3
  56.8 0.0 copy-start.4
  56.8 0.5 shard_map.260
  57.3 0.0 copy-start
  57.3 0.0 copy-start.1
  57.4 23.5 %all_to_all.43 = bf16[384,2,128]{2,1,0:T(2,128)(2,1)S(1)} all-to-all(bf16[384,2,128]{2,1,0:T(2,128)(2,1)S(1)} %bitcast.39), channel_id=1, replica_groups=mesh['far'=2,'near'=8,'z'=16,'xl'=2] {'xl','far','z'}, dimensions={0} | all-to-all | bytes 393216 | tf_op jit(solution)/shard_map/all_to_all | solution.py:486
  80.8 0.0 copy-done.3
  80.9 0.0 copy-done.4
  80.9 0.0 copy-done
  80.9 0.0 copy-done.1
  80.9 0.0 copy-start.2
  80.9 0.6 shard_map.261
  81.5 20.6 %all_to_all.44 = bf16[192,2,128]{2,1,0:T(2,128)(2,1)S(1)} all-to-all(bf16[192,2,128]{2,1,0:T(2,128)(2,1)S(1)} %bitcast.47), channel_id=1, replica_groups=mesh['far'=2,'near'=8,'z'=16,'xl'=2] {'xl','far','z'}, dimensions={0} | all-to-all | bytes 196608 | tf_op jit(solution)/shard_map/all_to_all | solution.py:486
  102.1 0.0 copy-done.2
  102.1 0.6 shard_map.262
  102.7 0.0 copy-start.8
  102.7 0.0 copy-start.16
  102.7 9.3 %all_to_all.45 = bf16[384,2,128]{2,1,0:T(2,128)(2,1)S(1)} all-to-all(bf16[384,2,128]{2,1,0:T(2,128)(2,1)S(1)} %bitcast.41), channel_id=1, replica_groups=mesh['far'=2,'near'=8,'z'=16,'xl'=2] {'near'}, dimensions={0} | all-to-all | bytes 393216 | tf_op jit(solution)/shard_map/all_to_all | solution.py:486
  112.1 0.0 copy-done.8
  112.1 0.0 copy-done.16
  112.1 0.0 copy-start.5
  112.1 0.8 shard_map.263
  112.9 8.2 %all_to_all.46 = bf16[192,2,128]{2,1,0:T(2,128)(2,1)S(1)} all-to-all(bf16[192,2,128]{2,1,0:T(2,128)(2,1)S(1)} %bitcast.44), channel_id=1, replica_groups=mesh['far'=2,'near'=8,'z'=16,'xl'=2] {'near'}, dimensions={0} | all-to-all | bytes 196608 | tf_op jit(solution)/shard_map/all_to_all | solution.py:486
  121.1 0.0 copy-done.5
  121.1 0.4 shard_map.264
  121.5 19.9 %all_to_all.47 = bf16[192,2,128]{2,1,0:T(2,128)(2,1)S(1)} all-to-all(bf16[192,2,128]{2,1,0:T(2,128)(2,1)S(1)} %bitcast.46), channel_id=1, replica_groups=mesh['far'=2,'near'=8,'z'=16,'xl'=2] {'xl','far','z'}, dimensions={0} | all-to-all | bytes 196608 | tf_op jit(solution)/shard_map/all_to_all | solution.py:486
  141.5 1.0 shard_map.265
Async XLA Ops:
  0.6 35.4 %copy-start.6 = (bf16[384,384]{1,0:T(8,128)(2,1)S(1)}, bf16[384,384]{1,0:T(8,128)(2,1)}, u32[]{:S(2)}) copy-start(bf16[384,384]{1,0:T(8,128)(2,1)} %constant.57.left_ref) | copy-start | bytes 884740
  0.6 35.4 %copy-start.13 = (f32[192,128]{1,0:T(8,128)S(1)}, f32[192,128]{1,0:T(8,128)}, u32[]{:S(2)}) copy-start(f32[192,128]{1,0:T(8,128)} %constant.41.clone.sin_ref) | copy-start | bytes 294916
  0.7 35.4 %copy-start.14 = (f32[192,128]{1,0:T(8,128)S(1)}, f32[192,128]{1,0:T(8,128)}, u32[]{:S(2)}) copy-start(f32[192,128]{1,0:T(8,128)} %constant.40.clone.cos_ref) | copy-start | bytes 294916
  2.3 33.7 %copy-start.12 = (bf16[256,256]{1,0:T(8,128)(2,1)S(1)}, bf16[256,256]{1,0:T(8,128)(2,1)}, u32[]{:S(2)}) copy-start(bf16[256,256]{1,0:T(8,128)(2,1)} %constant.58.right_ref) | copy-start | bytes 393220
  36.1 10.6 %copy-start.11 = (bf16[128,512]{1,0:T(8,128)(2,1)S(1)}, bf16[128,512]{1,0:T(8,128)(2,1)}, u32[]{:S(2)}) copy-start(bf16[128,512]{1,0:T(8,128)(2,1)} %constant.59.spread_ref) | copy-start | bytes 393220
  36.1 10.6 %copy-start.15 = (f32[192,128]{1,0:T(8,128)S(1)}, f32[192,128]{1,0:T(8,128)}, u32[]{:S(2)}) copy-start(f32[192,128]{1,0:T(8,128)} %constant.38.clone.wave_ref) | copy-start | bytes 294916
  36.1 10.6 %copy-start.17 = (bf16[192,256]{1,0:T(8,128)(2,1)S(1)}, bf16[192,256]{1,0:T(8,128)(2,1)}, u32[]{:S(2)}) copy-start(bf16[192,256]{1,0:T(8,128)(2,1)} %constant.60.left_ref) | copy-start | bytes 294916
  36.5 10.2 %copy-start.10 = (bf16[256,192]{1,0:T(8,128)(2,1)S(1)}, bf16[256,192]{1,0:T(8,128)(2,1)}, u32[]{:S(2)}) copy-start(bf16[256,192]{1,0:T(8,128)(2,1)} %constant.61.back_ref) | copy-start | bytes 294916
  47.4 9.4 %copy-start.7 = (bf16[256,256]{1,0:T(8,128)(2,1)S(1)}, bf16[256,256]{1,0:T(8,128)(2,1)}, u32[]{:S(2)}) copy-start(bf16[256,256]{1,0:T(8,128)(2,1)} %constant.63.right_ref) | copy-start | bytes 393220
  47.4 9.4 %copy-start.9 = (bf16[256,256]{1,0:T(8,128)(2,1)S(1)}, bf16[256,256]{1,0:T(8,128)(2,1)}, u32[]{:S(2)}) copy-start(bf16[256,256]{1,0:T(8,128)(2,1)} %constant.62.left_ref) | copy-start | bytes 393220
  47.4 9.4 %copy-start.18 = (f32[128,128]{1,0:T(8,128)S(1)}, f32[128,128]{1,0:T(8,128)}, u32[]{:S(2)}) copy-start(f32[128,128]{1,0:T(8,128)} %constant.48.clone.sin_ref) | copy-start | bytes 196612
  47.4 9.4 %copy-start.19 = (f32[128,128]{1,0:T(8,128)S(1)}, f32[128,128]{1,0:T(8,128)}, u32[]{:S(2)}) copy-start(f32[128,128]{1,0:T(8,128)} %constant.47.clone.cos_ref) | copy-start | bytes 196612
  56.8 24.1 %copy-start.3 = (bf16[384,512]{1,0:T(8,128)(2,1)S(1)}, bf16[384,512]{1,0:T(8,128)(2,1)}, u32[]{:S(2)}) copy-start(bf16[384,512]{1,0:T(8,128)(2,1)} %constant.64.back_ref) | copy-start | bytes 1179652
  56.8 24.0 %copy-start.4 = (bf16[384,512]{1,0:T(8,128)(2,1)S(1)}, bf16[384,512]{1,0:T(8,128)(2,1)}, u32[]{:S(2)}) copy-start(bf16[384,512]{1,0:T(8,128)(2,1)} %constant.56.table_hbm.table_ref) | copy-start | bytes 1179652
  57.3 23.5 %copy-start = (f32[3,16,2,512]{3,2,1,0:T(2,128)S(1)}, f32[3,16,2,512]{3,2,1,0:T(2,128)}, u32[]{:S(2)}) copy-start(f32[3,16,2,512]{3,2,1,0:T(2,128)} %param.27) | copy-start | bytes 589828
  57.3 23.5 %copy-start.1 = (f32[16,2,512]{2,1,0:T(2,128)S(1)}, f32[16,2,512]{2,1,0:T(2,128)}, u32[]{:S(2)}) copy-start(f32[16,2,512]{2,1,0:T(2,128)} %param.26) | copy-start | bytes 196612
  80.9 21.2 %copy-start.2 = (bf16[512,512]{1,0:T(8,128)(2,1)S(1)}, bf16[512,512]{1,0:T(8,128)(2,1)}, u32[]{:S(2)}) copy-start(bf16[512,512]{1,0:T(8,128)(2,1)} %constant.65.right_ref) | copy-start | bytes 1572868
  102.7 9.4 %copy-start.8 = (bf16[256,192]{1,0:T(8,128)(2,1)S(1)}, bf16[256,192]{1,0:T(8,128)(2,1)}, u32[]{:S(2)}) copy-start(bf16[256,192]{1,0:T(8,128)(2,1)} %constant.67.back_ref) | copy-start | bytes 294916
  102.7 9.4 %copy-start.16 = (bf16[192,256]{1,0:T(8,128)(2,1)S(1)}, bf16[192,256]{1,0:T(8,128)(2,1)}, u32[]{:S(2)}) copy-start(bf16[192,256]{1,0:T(8,128)(2,1)} %constant.66.left_ref) | copy-start | bytes 294916
  112.1 9.0 %copy-start.5 = (bf16[384,384]{1,0:T(8,128)(2,1)S(1)}, bf16[384,384]{1,0:T(8,128)(2,1)}, u32[]{:S(2)}) copy-start(bf16[384,384]{1,0:T(8,128)(2,1)} %constant.68.left_ref) | copy-start | bytes 884740
